TPU v7x, 32 devices: a whole 2x2x4 slice. The times are simulated.
32 devices in a mesh: dp: 16 (over z, y, core), mp: 2 (over x).
Axes of the slice: x: 2, y: 2, z: 4, core: 2. Of those that a mesh axis runs over, the one named last changes fastest.
Arguments:
- tokens: bfloat16 [8192, 768], P('dp'), may hold values from -6 to 6
- crop_ids: int32 [32, 256], P('dp'), may hold values from 0 to 7, never falling along the last dimension, each value on 1 to 64 neighbouring positions
- w_query: bfloat16 [768, 768], P(None, 'mp'), may hold values from -0.4375 to 0.4375
- w_key: bfloat16 [768, 768], P(None, 'mp'), may hold values from -0.21875 to 0.21875
- w_value: bfloat16 [768, 768], P(None, 'mp'), may hold values from -0.21875 to 0.21875
- bias_query: float32 [768], P('mp'), may hold values from -3 to 3
- bias_value: float32 [768], P('mp'), may hold values from -2 to 2
- w_out: bfloat16 [768, 768], P('mp'), may hold values from -0.875 to 0.875
- bias_out: float32 [768], replicated, may hold values from -2 to 2
- gain_attn: float32 [768], replicated, may hold values from 0.5 to 1.5
- shift_attn: float32 [768], replicated, may hold values from -2 to 2
- gain_mlp: float32 [768], replicated, may hold values from 0.5 to 1.5
- shift_mlp: float32 [768], replicated, may hold values from -2 to 2
- w_up: bfloat16 [768, 3072], P(None, 'mp'), may hold values from -0.21875 to 0.21875
- bias_up: float32 [3072], P('mp'), may hold values from -3 to 3
- w_down: bfloat16 [3072, 768], P('mp'), may hold values from -0.109375 to 0.109375
- bias_down: float32 [768], replicated, may hold values from -2 to 2
- cotangent: bfloat16 [8192, 768], P('dp'), may hold values from -6 to 6
Outputs:
- block_out: bfloat16 [8192, 768], P('dp')
- grad_tokens: float32 [8192, 768], P('dp')
- grad_w_query: float32 [768, 768], P('dp', 'mp')
- grad_w_key: float32 [768, 768], P('dp', 'mp')
- grad_w_value: float32 [768, 768], P('dp', 'mp')
- grad_bias_query: float32 [768], P('mp')
- grad_bias_value: float32 [768], P('mp')
- grad_w_out: float32 [768, 768], P('mp', 'dp')
- grad_bias_out: float32 [768], P('dp')
- grad_gain_attn: float32 [768], P('dp')
- grad_shift_attn: float32 [768], P('dp')
- grad_gain_mlp: float32 [768], P('dp')
- grad_shift_mlp: float32 [768], P('dp')
- grad_w_up: float32 [768, 3072], P('dp', 'mp')
- grad_bias_up: float32 [3072], P('mp')
- grad_w_down: float32 [3072, 768], P('mp', 'dp')
- grad_bias_down: float32 [768], P('dp')
Inputs may be any that keep to these rules, and one draw needn't show every extreme that they name: `crop_ids`: within each sequence the crop ids never fall, every crop has 1 to 64 patches, and some crop has exactly 64.
All inputs are finite; a program needn't handle non-finite values.
Results may differ from a plain program's by a relative error of at most 0.012.
The roundings to bfloat16 on the way count: a program that leaves them out, or rounds other values in their place, can miss the bound.
Values sent between devices are 32-bit elements; how exact they have to be, the bound alone decides.
No kernel may reach another device: no remote copies, remote signals or barrier semaphores. Data moves between devices by JAX's collectives and lax.ppermute only.
A program may use at most 128 MiB of HBM per device.

v0:
```python
from functools import partial

import jax
import jax.numpy as jnp
from jax import lax
from jax.sharding import PartitionSpec as P

HEAD_DIM = 64
LEN = 256


EPS = 1e-06
NEGATIVE = -1e30


def norm_rows(values, gain, shift):
    mean = jnp.mean(values, axis=-1, keepdims=True)
    centred = values - mean
    var = jnp.mean(centred * centred, axis=-1, keepdims=True)
    scale = lax.rsqrt(var + EPS)
    unit = centred * scale
    return (unit * gain + shift, unit, scale)


def norm_back(grad_out, unit, scale, gain):
    grad_unit = grad_out * gain
    inner = jnp.mean(grad_unit * unit, axis=-1, keepdims=True)
    return scale * (grad_unit - jnp.mean(grad_unit, axis=-1, keepdims=True) - unit * inner)


def plain_dot(left, right):
    return jnp.dot(left, right, preferred_element_type=jnp.float32)


def right_trans(left, right):
    return lax.dot_general(
        left, right, (((1,), (1,)), ((), ())), preferred_element_type=jnp.float32
    )


def left_trans(left, right):
    return lax.dot_general(
        left, right, (((0,), (0,)), ((), ())), preferred_element_type=jnp.float32
    )


def scores_of(query, key_rows, crops):
    raw = jnp.einsum("qhd,khd->hqk", query, key_rows, preferred_element_type=jnp.float32) * 0.125
    same = crops[:, None] == crops[None, :]
    return jnp.where(same[None], raw, NEGATIVE)


def attend_block(item):
    query, key_rows, value_rows, crops = item
    scores = scores_of(query, key_rows, crops)
    top = jnp.max(scores, axis=-1, keepdims=True)
    expo = jnp.exp(scores - top)
    total = jnp.sum(expo, axis=-1, keepdims=True)
    probs = (expo / total).astype(jnp.bfloat16)
    mixed = jnp.einsum("hqk,khd->qhd", probs, value_rows, preferred_element_type=jnp.float32)
    return (mixed.astype(jnp.bfloat16), top + jnp.log(total))


def attend_back(item):
    query, key_rows, value_rows, crops, log_total, grad_mixed = item
    probs = jnp.exp(scores_of(query, key_rows, crops) - log_total)
    grad_value = jnp.einsum(
        "hqk,qhd->khd", probs.astype(jnp.bfloat16), grad_mixed, preferred_element_type=jnp.float32
    )
    grad_probs = jnp.einsum(
        "qhd,khd->hqk", grad_mixed, value_rows, preferred_element_type=jnp.float32
    )
    inner = jnp.sum(grad_probs * probs, axis=-1, keepdims=True)
    grad_scores = (probs * (grad_probs - inner)).astype(jnp.bfloat16)
    grad_query = (
        jnp.einsum("hqk,khd->qhd", grad_scores, key_rows, preferred_element_type=jnp.float32)
        * 0.125
    )
    grad_key = (
        jnp.einsum("hqk,qhd->khd", grad_scores, query, preferred_element_type=jnp.float32) * 0.125
    )
    return (
        grad_query.astype(jnp.bfloat16),
        grad_key.astype(jnp.bfloat16),
        grad_value.astype(jnp.bfloat16),
    )


def body(
    tokens,
    crop_ids,
    w_query,
    w_key,
    w_value,
    bias_query,
    bias_value,
    w_out,
    bias_out,
    gain_attn,
    shift_attn,
    gain_mlp,
    shift_mlp,
    w_up,
    bias_up,
    w_down,
    bias_down,
    cotangent,
):
    rows = tokens.shape[0]
    local = w_query.shape[1]
    heads = local // HEAD_DIM
    seq_count = crop_ids.shape[0]
    pair = 2
    blocks = seq_count // pair
    block_rows = pair * LEN
    inputs = tokens.astype(jnp.float32)
    first, unit_one, scale_one = norm_rows(inputs, gain_attn, shift_attn)
    first = first.astype(jnp.bfloat16)
    query = (plain_dot(first, w_query) + bias_query).astype(jnp.bfloat16)
    key_rows = plain_dot(first, w_key).astype(jnp.bfloat16)
    value_rows = (plain_dot(first, w_value) + bias_value).astype(jnp.bfloat16)
    seq_base = lax.broadcasted_iota(jnp.int32, crop_ids.shape, 0) * LEN
    crop_keys = (crop_ids + seq_base).reshape(blocks, block_rows)

    def split(values):
        return values.reshape(blocks, block_rows, heads, HEAD_DIM)

    q_blocks = split(query)
    k_blocks = split(key_rows)
    v_blocks = split(value_rows)
    mixed, log_total = lax.map(attend_block, (q_blocks, k_blocks, v_blocks, crop_keys))
    heads_out = mixed.reshape(rows, local)
    attn = lax.psum(plain_dot(heads_out, w_out), "mp") + bias_out
    hidden = inputs + attn
    second, unit_two, scale_two = norm_rows(hidden, gain_mlp, shift_mlp)
    second = second.astype(jnp.bfloat16)
    pre = plain_dot(second, w_up) + bias_up
    active, gelu_pull = jax.vjp(partial(jax.nn.gelu, approximate=False), pre)
    active = active.astype(jnp.bfloat16)
    mlp_sum = lax.psum(plain_dot(active, w_down), "mp")
    block_out = (hidden + mlp_sum + bias_down).astype(jnp.bfloat16)
    grad_out = cotangent.astype(jnp.float32)
    grad_bias_down = jnp.sum(grad_out, axis=0)
    grad_w_down = left_trans(active, cotangent)
    grad_active = right_trans(cotangent, w_down)
    grad_pre = gelu_pull(grad_active)[0].astype(jnp.bfloat16)
    grad_bias_up = jnp.sum(grad_pre.astype(jnp.float32), axis=0)
    grad_w_up = left_trans(second, grad_pre)
    grad_second = lax.psum(right_trans(grad_pre, w_up), "mp")
    grad_gain_mlp = jnp.sum(grad_second * unit_two, axis=0)
    grad_shift_mlp = jnp.sum(grad_second, axis=0)
    grad_hidden = grad_out + norm_back(grad_second, unit_two, scale_two, gain_mlp)
    grad_bias_out = jnp.sum(grad_hidden, axis=0)
    hidden_low = grad_hidden.astype(jnp.bfloat16)
    grad_w_out = left_trans(heads_out, hidden_low)
    grad_heads = right_trans(hidden_low, w_out).astype(jnp.bfloat16)
    grad_q, grad_k, grad_v = lax.map(
        attend_back, (q_blocks, k_blocks, v_blocks, crop_keys, log_total, split(grad_heads))
    )
    grad_q = grad_q.reshape(rows, local)
    grad_k = grad_k.reshape(rows, local)
    grad_v = grad_v.reshape(rows, local)
    grad_bias_query = jnp.sum(grad_q.astype(jnp.float32), axis=0)
    grad_bias_value = jnp.sum(grad_v.astype(jnp.float32), axis=0)
    grad_w_query = left_trans(first, grad_q)
    grad_w_key = left_trans(first, grad_k)
    grad_w_value = left_trans(first, grad_v)
    partial_first = (
        right_trans(grad_q, w_query) + right_trans(grad_k, w_key) + right_trans(grad_v, w_value)
    )
    grad_first = lax.psum(partial_first, "mp")
    grad_gain_attn = jnp.sum(grad_first * unit_one, axis=0)
    grad_shift_attn = jnp.sum(grad_first, axis=0)
    grad_tokens = grad_hidden + norm_back(grad_first, unit_one, scale_one, gain_attn)
    (
        done_w_query,
        done_w_key,
        done_w_value,
        done_w_out,
        done_gain_attn,
        done_shift_attn,
        done_bias_out,
        done_w_up,
        done_w_down,
        done_gain_mlp,
        done_shift_mlp,
        done_bias_down,
    ) = (
        lax.psum_scatter(grad_w_query, "dp", scatter_dimension=0, tiled=True),
        lax.psum_scatter(grad_w_key, "dp", scatter_dimension=0, tiled=True),
        lax.psum_scatter(grad_w_value, "dp", scatter_dimension=0, tiled=True),
        lax.psum_scatter(grad_w_out, "dp", scatter_dimension=1, tiled=True),
        lax.psum_scatter(grad_gain_attn, "dp", scatter_dimension=0, tiled=True),
        lax.psum_scatter(grad_shift_attn, "dp", scatter_dimension=0, tiled=True),
        lax.psum_scatter(grad_bias_out, "dp", scatter_dimension=0, tiled=True),
        lax.psum_scatter(grad_w_up, "dp", scatter_dimension=0, tiled=True),
        lax.psum_scatter(grad_w_down, "dp", scatter_dimension=1, tiled=True),
        lax.psum_scatter(grad_gain_mlp, "dp", scatter_dimension=0, tiled=True),
        lax.psum_scatter(grad_shift_mlp, "dp", scatter_dimension=0, tiled=True),
        lax.psum_scatter(grad_bias_down, "dp", scatter_dimension=0, tiled=True),
    )
    done_bias_query, done_bias_value, done_bias_up = lax.psum(
        (grad_bias_query, grad_bias_value, grad_bias_up), "dp"
    )
    return (
        block_out,
        grad_tokens,
        done_w_query,
        done_w_key,
        done_w_value,
        done_bias_query,
        done_bias_value,
        done_w_out,
        done_bias_out,
        done_gain_attn,
        done_shift_attn,
        done_gain_mlp,
        done_shift_mlp,
        done_w_up,
        done_bias_up,
        done_w_down,
        done_bias_down,
    )


def solution(mesh):
    placed = (
        P("dp", None),
        P("dp", None),
        P(None, "mp"),
        P(None, "mp"),
        P(None, "mp"),
        P("mp"),
        P("mp"),
        P("mp", None),
        P(),
        P(),
        P(),
        P(),
        P(),
        P(None, "mp"),
        P("mp"),
        P("mp", None),
        P(),
        P("dp", None),
    )
    return jax.shard_map(
        body,
        mesh=mesh,
        in_specs=placed,
        out_specs=(
            P("dp", None),
            P("dp", None),
            P("dp", "mp"),
            P("dp", "mp"),
            P("dp", "mp"),
            P("mp"),
            P("mp"),
            P("mp", "dp"),
            P("dp"),
            P("dp"),
            P("dp"),
            P("dp"),
            P("dp"),
            P("dp", "mp"),
            P("mp"),
            P("mp", "dp"),
            P("dp"),
        ),
        check_vma=False,
    )
```

profile of v0, /device:TPU:0, one launch (start us, length us, event | category | flops | bytes accessed | tf_op | source)
XLA Modules:
  0.0 667.7 jit_solution(14110133247439254627)
XLA Ops:
  22.5 54.2 %all-reduce.12.cloned.1.call-done = f32[512,768]{1,0:T(8,128)} async-done(((f32[512,768]{1,0:T(8,128)}), f32[512,768]{1,0:T(8,128)}) %all-reduce.12.cloned.1.call-update) | async-done | bytes 1572880 | tf_op jit(solution)/shard_map/psum | solution.py:133
  81.3 10.2 %convert_reduce_fusion = (f32[1536]{0:T(1024)}, bf16[512,1536]{1,0:T(8,128)(2,1)S(1)}, f32[512,1536]{1,0:T(8,128)}) fusion(f32[512,1536]{1,0:T(8,128)S(1)} %convolution_add_fusion, bf16[512,768]{1,0:T(8,128)(2,1)S(1)} %copy-done.15, bf16[1536,768]{1,0:T(8,128)(2,1)S(1)} %copy-done), kind=kOutput, calls=%fused_computation.12 | convolution fusion | flops 1266153984 | bytes 11016192 | tf_op jit(solution)/shard_map/dot_general | solution.py:36
  92.6 2.6 fusion.44
  95.5 3.6 multiply_convert_fusion.1
  100.2 2.5 fusion.43
  102.7 44.1 %all-reduce.14.cloned.1.call-done = f32[512,768]{1,0:T(8,128)} async-done(((f32[512,768]{1,0:T(8,128)}), f32[512,768]{1,0:T(8,128)}) %all-reduce.14.cloned.1.call-update) | async-done | bytes 1572880 | tf_op jit(solution)/shard_map/psum | solution.py:149
  146.9 3.3 multiply_reduce_fusion.1
  150.3 2.6 fusion.39
  154.6 4.7 convert_reduce_fusion.3
  169.0 3.2 fusion.34
  172.3 2.8 fusion.49
  175.1 3.1 fusion.47
  178.6 2.8 fusion.48
  181.5 5.6 fusion.37
  187.2 5.2 fusion.50
  194.5 60.5 %all-reduce.16.cloned.1.call-done = (f32[512,768]{1,0:T(8,128)}, f32[512,768]{1,0:T(8,128)}) async-done(((f32[512,768]{1,0:T(8,128)}, f32[512,768]{1,0:T(8,128)}), (f32[512,768]{1,0:T(8,128)}, f32[512,768]{1,0:T(8,128)})) %all-reduce.16.cloned.1.call-update) | async-done | bytes 3145744 | tf_op jit(solution)/shard_map/psum | solution.py:140
  255.1 2.2 fusion.24
  257.3 61.4 %all-reduce.6 = (f32[384]{0:T(512)}, f32[384]{0:T(512)}, f32[768]{0:T(1024)S(1)}, f32[768]{0:T(1024)S(1)}, f32[768]{0:T(1024)S(1)}, /*index=5*/f32[768]{0:T(1024...) all-reduce(f32[384]{0:T(512)S(1)} %reduce_sum.188, ...), channel_id=1, replica_groups=mesh['dp'=16,'mp'=2] {'dp'}, use_global_device_ids=true, to_apply=%region_19.20 | all-reduce | flops 6912 | bytes 55296 | tf_op jit(solution)/shard_map/psum | solution.py:202
  322.2 3.0 add_convert_fusion.1
  326.9 52.4 %reduce-scatter.11.cloned.1.call-done = f32[48,384]{1,0:T(8,128)} async-done(((f32[768,384]{1,0:T(8,128)}), f32[48,384]{1,0:T(8,128)}) %reduce-scatter.11.cloned.1.call-update) | async-done | bytes 73744 | tf_op jit(solution)/shard_map/reduce_scatter | solution.py:191
  379.3 61.6 %reduce-scatter.7.cloned.1.call-done = f32[48,384]{1,0:T(8,128)} async-done(((f32[768,384]{1,0:T(8,128)}), f32[48,384]{1,0:T(8,128)}) %reduce-scatter.7.cloned.1.call-update) | async-done | bytes 73744 | tf_op jit(solution)/shard_map/reduce_scatter | solution.py:189
  440.9 61.7 %reduce-scatter.9.cloned.1.call-done = f32[48,384]{1,0:T(8,128)} async-done(((f32[768,384]{1,0:T(8,128)}), f32[48,384]{1,0:T(8,128)}) %reduce-scatter.9.cloned.1.call-update) | async-done | bytes 73744 | tf_op jit(solution)/shard_map/reduce_scatter | solution.py:190
  502.6 79.5 %reduce-scatter.15.cloned.1.call-done = f32[48,1536]{1,0:T(8,128)} async-done(((f32[768,1536]{1,0:T(8,128)}), f32[48,1536]{1,0:T(8,128)}) %reduce-scatter.15.cloned.1.call-update) | async-done | bytes 294928 | tf_op jit(solution)/shard_map/reduce_scatter | solution.py:196
  582.2 79.1 %reduce-scatter.17.cloned.1.call-done = f32[1536,48]{0,1:T(8,128)} async-done(((f32[1536,768]{0,1:T(8,128)}), f32[1536,48]{0,1:T(8,128)}) %reduce-scatter.17.cloned.1.call-update) | async-done | bytes 294928 | tf_op jit(solution)/shard_map/reduce_scatter | solution.py:197
  (179 shorter events, 40.4 us)
Async XLA Ops:
  7.2 74.1 %copy-start = (bf16[1536,768]{1,0:T(8,128)(2,1)S(1)}, bf16[1536,768]{1,0:T(8,128)(2,1)}, u32[]{:S(2)}) copy-start(bf16[1536,768]{1,0:T(8,128)(2,1)} %param.33) | copy-start | bytes 7077892
  7.2 69.5 %all-reduce.12.cloned.1.call-start = ((), (), s32[]{:S(2)}) async-start(), calls=%async_computation.6 | async-start | bytes 3145728 | tf_op jit(solution)/shard_map/psum | solution.py:133
  22.4 57.3 %copy-start.39 = (f32[768]{0:T(1024)S(1)}, f32[768]{0:T(1024)}, u32[]{:S(2)}) copy-start(f32[768]{0:T(1024)} %param.29) | copy-start | bytes 9220
  22.4 57.3 %copy-start.50 = (f32[1536]{0:T(1024)S(1)}, f32[1536]{0:T(1024)}, u32[]{:S(2)}) copy-start(f32[1536]{0:T(1024)} %param.32) | copy-start | bytes 18436
  22.4 57.3 %copy-start.51 = (f32[768]{0:T(1024)S(1)}, f32[768]{0:T(1024)}, u32[]{:S(2)}) copy-start(f32[768]{0:T(1024)} %param.30) | copy-start | bytes 9220
  22.4 124.5 %all-reduce.14.cloned.1.call-start = ((), (), s32[]{:S(2)}) async-start(), calls=%async_computation.7 | async-start | bytes 3145728 | tf_op jit(solution)/shard_map/psum | solution.py:149
  78.6 71.7 %copy-start.35 = (f32[512]{0:T(512)}, f32[512]{0:T(512)S(1)}, u32[]{:S(2)}) copy-start(f32[512]{0:T(512)S(1)} %broadcast_multiply_fusion.4) | copy-start | bytes 6148
  79.7 70.5 %copy-start.37 = (f32[512]{0:T(512)}, f32[512]{0:T(512)S(1)}, u32[]{:S(2)}) copy-start(f32[512]{0:T(512)S(1)} %add_rsqrt_fusion) | copy-start | bytes 6148
  95.2 159.8 %all-reduce.16.cloned.1.call-start = ((), (), s32[]{:S(2)}) async-start(), calls=%async_computation.14 | async-start | bytes 6291456 | tf_op jit(solution)/shard_map/psum | solution.py:140
  169.0 158.0 %reduce-scatter.13.cloned.1.call-start = ((), (), s32[]{:S(2)}) async-start(), calls=%async_computation.11 | async-start | bytes 1253376 | tf_op jit(solution)/shard_map/reduce_scatter | solution.py:192
  172.2 207.1 %reduce-scatter.11.cloned.1.call-start = ((), (), s32[]{:S(2)}) async-start(), calls=%async_computation.10 | async-start | bytes 1253376 | tf_op jit(solution)/shard_map/reduce_scatter | solution.py:191
  175.1 265.8 %reduce-scatter.7.cloned.1.call-start = ((), (), s32[]{:S(2)}) async-start(), calls=%async_computation.8 | async-start | bytes 1253376 | tf_op jit(solution)/shard_map/reduce_scatter | solution.py:189
  178.3 324.3 %reduce-scatter.9.cloned.1.call-start = ((), (), s32[]{:S(2)}) async-start(), calls=%async_computation.9 | async-start | bytes 1253376 | tf_op jit(solution)/shard_map/reduce_scatter | solution.py:190
  181.4 400.7 %reduce-scatter.15.cloned.1.call-start = ((), (), s32[]{:S(2)}) async-start(), calls=%async_computation.12 | async-start | bytes 5013504 | tf_op jit(solution)/shard_map/reduce_scatter | solution.py:196
  187.2 474.0 %reduce-scatter.17.cloned.1.call-start = ((), (), s32[]{:S(2)}) async-start(), calls=%async_computation.13 | async-start | bytes 5013504 | tf_op jit(solution)/shard_map/reduce_scatter | solution.py:197
  192.5 62.6 %copy-start.31 = (f32[512]{0:T(512)S(1)}, f32[512]{0:T(512)}, u32[]{:S(2)}) copy-start(f32[512]{0:T(512)} %copy-done.30) | copy-start | bytes 6148
  192.5 62.6 %copy-start.32 = (f32[768]{0:T(1024)S(1)}, f32[768]{0:T(1024)}, u32[]{:S(2)}) copy-start(f32[768]{0:T(1024)} %param.27) | copy-start | bytes 9220
  192.5 62.6 %copy-start.34 = (f32[512]{0:T(512)S(1)}, f32[512]{0:T(512)}, u32[]{:S(2)}) copy-start(f32[512]{0:T(512)} %copy-done.33) | copy-start | bytes 6148
  192.5 64.7 %copy-start.41 = (f32[768]{0:T(1024)S(1)}, f32[768]{0:T(1024)}, u32[]{:S(2)}) copy-start(f32[768]{0:T(1024)} %get-tuple-element.68) | copy-start | bytes 9220
  192.5 64.7 %copy-start.42 = (f32[768]{0:T(1024)S(1)}, f32[768]{0:T(1024)}, u32[]{:S(2)}) copy-start(f32[768]{0:T(1024)} %get-tuple-element.74) | copy-start | bytes 9220
  192.5 64.7 %copy-start.43 = (f32[768]{0:T(1024)S(1)}, f32[768]{0:T(1024)}, u32[]{:S(2)}) copy-start(f32[768]{0:T(1024)} %get-tuple-element.90) | copy-start | bytes 9220
  192.5 64.7 %copy-start.44 = (f32[768]{0:T(1024)S(1)}, f32[768]{0:T(1024)}, u32[]{:S(2)}) copy-start(f32[768]{0:T(1024)} %get-tuple-element.94) | copy-start | bytes 9220
  192.6 64.7 %copy-start.46 = (f32[1536]{0:T(1024)S(1)}, f32[1536]{0:T(1024)}, u32[]{:S(2)}) copy-start(f32[1536]{0:T(1024)} %get-tuple-element.87) | copy-start | bytes 18436
  192.6 129.7 %copy-start.47 = (f32[768]{0:T(1024)S(1)}, f32[768]{0:T(1024)}, u32[]{:S(2)}) copy-start(f32[768]{0:T(1024)} %param.34) | copy-start | bytes 9220
  (43 other events, 180.8 us)
Sparse Core Ops, SparseCore 0:
  22.5 54.1 all-reduce.11
  95.4 51.4 all-reduce.13
  169.1 85.9 all-reduce.15
  259.6 58.1 reduce-scatter.12
  322.2 57.0 reduce-scatter.10
  383.8 57.0 reduce-scatter.6
  445.5 57.0 reduce-scatter.8
  507.6 74.5 reduce-scatter.14
  586.6 74.5 reduce-scatter.16
where the time goes:
time: 668 us
  waiting for transfers between devices  493 us (74%)
  blocking collectives  61.4 us (9%)
  matrix products  57.7 us (9%)
  other arithmetic  26.4 us (4%)
  between operations  15.2 us (2%)
  local copies, waits for them, and re-layouts  12.9 us (2%)
    reduce_scatter x1, waiting for transfers between devices, body(): lax.psum_scatter(grad_w_up, 'dp', scatter_dimension=0, tiled=True)  79.5 us
    reduce_scatter x1, waiting for transfers between devices, body(): lax.psum_scatter(grad_w_down, 'dp', scatter_dimension=1, tiled=True)  79.1 us
    reduce_scatter x1, waiting for transfers between devices, body(): lax.psum_scatter(grad_w_key, 'dp', scatter_dimension=0, tiled=True)  61.7 us
    reduce_scatter x1, waiting for transfers between devices, body(): lax.psum_scatter(grad_w_query, 'dp', scatter_dimension=0, tiled=True)  61.6 us
    psum x1, blocking collectives, body(): lax.psum((grad_bias_query, grad_bias_value, grad_bias_up), 'dp')  61.4 us
    psum x1, waiting for transfers between devices, body(): mlp_sum = lax.psum(plain_dot(active, w_down), 'mp')  60.5 us
    psum x1, waiting for transfers between devices, body(): attn = lax.psum(plain_dot(heads_out, w_out), 'mp') + bias_out  54.2 us
    reduce_scatter x1, waiting for transfers between devices, body(): lax.psum_scatter(grad_w_value, 'dp', scatter_dimension=0, tiled=True)  52.4 us
  transfers between devices with their start and end apart: 9, of which 8 were waited for; matrix products, arithmetic and copies ran while one was open for 6% of the time, Pallas kernels for 0%

commit v1 on v0

v1 whole, which is shorter than its diff:
```python
from functools import partial

import jax
import jax.numpy as jnp
from jax import lax
from jax.experimental import pallas as pl
from jax.experimental.pallas import tpu as pltpu
from jax.sharding import PartitionSpec as P

HEAD_DIM = 64
PAIR = 2 * HEAD_DIM
EPS = 1e-06
NEGATIVE = -1e30
LOW = jnp.bfloat16
HIGH = jnp.float32
VMEM = pl.BlockSpec(memory_space=pltpu.VMEM)


def plain_dot(left, right):
    return jnp.dot(left, right, preferred_element_type=HIGH)


def right_trans(left, right):
    return lax.dot_general(left, right, (((1,), (1,)), ((), ())), preferred_element_type=HIGH)


def left_trans(left, right):
    return lax.dot_general(left, right, (((0,), (0,)), ((), ())), preferred_element_type=HIGH)


def unit_rows(values):
    mean = jnp.mean(values, axis=-1, keepdims=True)
    centred = values - mean
    scale = lax.rsqrt(jnp.mean(centred * centred, axis=-1, keepdims=True) + EPS)
    return centred * scale, scale


def norm_back(grad_unit, unit, scale):
    inner = jnp.mean(grad_unit * unit, axis=-1, keepdims=True)
    return scale * (grad_unit - jnp.mean(grad_unit, axis=-1, keepdims=True) - unit * inner)


def half_masks():
    lane = lax.broadcasted_iota(jnp.int32, (1, PAIR), 1)
    first = lane < HEAD_DIM
    return first, (first.astype(HIGH).astype(LOW), (~first).astype(HIGH).astype(LOW))


def col_sum(values):
    return jnp.sum(values, axis=0, keepdims=True)


def front_kernel(*refs, length, seqs):
    sources, targets = refs[:9], refs[9:13]
    first_out, outs = refs[13], refs[14 : 14 + seqs]
    held, (q, k, v, lse), sems = refs[14 + seqs : -5], refs[-5:-1], refs[-1]
    copies = [pltpu.make_async_copy(a, b, sems.at[i]) for i, (a, b) in enumerate(zip(sources, held))]
    for copy in copies:
        copy.start()
    tokens, gain, shift, w_q, w_k, w_v, b_q, b_v, crops = held
    for copy in copies[:3]:
        copy.wait()
    unit, _ = unit_rows(tokens[...].astype(HIGH))
    first = (unit * row(gain) + row(shift)).astype(LOW)
    first_out[...] = first
    for copy in copies[3:]:
        copy.wait()
    q_all = ((plain_dot(first, w_q[...]) + row(b_q)).astype(LOW) * 0.125).astype(LOW)
    k_all = plain_dot(first, w_k[...]).astype(LOW)
    v_all = (plain_dot(first, w_v[...]) + row(b_v)).astype(LOW)
    q[...] = q_all
    k[...] = k_all
    v[...] = v_all
    stores = [
        pltpu.make_async_copy(a, b, sems.at[len(sources) + i])
        for i, (a, b) in enumerate(zip((q, k, v, lse), targets))
    ]
    for store in stores[:3]:
        store.start()
    low_half, masks = half_masks()
    for s, o in enumerate(outs):
        rows = slice(s * length, (s + 1) * length)
        same = same_crop(crops, s)
        for t in range(q_all.shape[1] // PAIR):
            at = slice(t * PAIR, (t + 1) * PAIR)
            q_pair, k_pair, v_pair = q_all[rows, at], k_all[rows, at], v_all[rows, at]
            got = []
            for half in range(2):
                scores = jnp.where(same, right_trans(q_pair * masks[half], k_pair), NEGATIVE)
                top = jnp.max(scores, axis=-1, keepdims=True)
                expo = jnp.exp(scores - top)
                total = jnp.sum(expo, axis=-1, keepdims=True)
                probs = (expo * (1.0 / total)).astype(LOW)
                got.append(plain_dot(probs, v_pair))
                h = 2 * t + half
                lse[rows, h : h + 1] = top + jnp.log(total)
            o[:, at] = jnp.where(low_half, got[0], got[1])
    stores[3].start()
    for store in stores:
        store.wait()


def turn_kernel(order, first, cotangent, a1_t, cot_t, sums):
    cot = cotangent[...]
    a1_t[...] = right_trans(order[...], first[...]).astype(LOW)
    cot_t[...] = right_trans(order[...], cot).astype(LOW)
    sums[...] = col_sum(cot.astype(HIGH))


def middle_kernel(*refs, blocks, seq, length, chained):
    place, tokens, o_own, o_other, w_out, b_out, gain, shift, w_up, b_up = refs[:10]
    w_down, cotangent, order = refs[10:13]
    pieces = refs[13:17]
    hidden, g_second, a2_t, active, g_pre, g_bias, w_low = refs[17 + 5 * chained :]
    rows = slice(seq * length, (seq + 1) * length)
    for b in range(4):
        size = pieces[b].shape[0]
        start = pl.multiple_of((place[0] ^ b) * size, size)
        w_low[pl.ds(start, size), :] = pieces[b][...].astype(LOW)
    attn = plain_dot(o_own[...].astype(LOW), w_out[...])
    attn = attn + plain_dot(o_other[...].astype(LOW), w_low[...])
    values = tokens[rows, :].astype(HIGH) + (attn + row(b_out))
    hidden[...] = values
    unit, _ = unit_rows(values)
    second = (unit * row(gain) + row(shift)).astype(LOW)
    cot = cotangent[rows, :]
    size = w_up.shape[1] // blocks
    total = None
    for b in range(blocks):
        at = slice(b * size, (b + 1) * size)
        pre = plain_dot(second, w_up[:, at]) + b_up[at].reshape(1, size)
        cdf = 0.5 * (1.0 + lax.erf(pre * 0.7071067811865476))
        active[rows, at] = (pre * cdf).astype(LOW)
        slope = cdf + pre * (0.3989422804014327 * jnp.exp(-0.5 * (pre * pre)))
        grad = (right_trans(cot, w_down[at, :]) * slope).astype(LOW)
        g_pre[rows, at] = grad
        bias = col_sum(grad.astype(HIGH))
        g_bias[:, at] = refs[21][:, at] + bias if chained else bias
        part = right_trans(grad, w_up[:, at])
        total = part if total is None else total + part
    g_second[rows, :] = total
    a2_t[:, rows] = right_trans(order[...], second).astype(LOW)


def back_kernel(*refs, seqs, length):
    tokens, crops, cotangent, own, other, gain, w_out, w_q, w_k, w_v = refs[:10]
    q, k, v, lse, order, g_bias, cot_sum = refs[10:17]
    hidden = refs[17 : 17 + seqs]
    g_hidden, g_first, gh_t, g_qkv, sums = refs[17 + seqs :]
    width, local = tokens.shape[1], q.shape[1]
    low_half, masks = half_masks()

    def put(s, r, at, value):
        sums[r : r + 1, at] = sums[r : r + 1, at] + value if s else value

    full = slice(0, width)
    for s in range(seqs):
        rows = slice(s * length, (s + 1) * length)
        unit, scale = unit_rows(hidden[s][...])
        grad = own[rows, :] + other[rows, :]
        put(s, 0, full, col_sum(grad * unit))
        put(s, 1, full, col_sum(grad))
        values = cotangent[rows, :].astype(HIGH) + norm_back(grad * row(gain), unit, scale)
        g_hidden[rows, :] = values
        put(s, 2, full, col_sum(values))
        low = values.astype(LOW)
        gh_t[:, rows] = right_trans(order[...], low).astype(LOW)
        g_o = right_trans(low, w_out[...]).astype(LOW)
        same = same_crop(crops, s)
        for t in range(local // PAIR):
            at = slice(t * PAIR, (t + 1) * PAIR)
            q_pair, k_pair, v_pair, o_pair = q[rows, at], k[rows, at], v[rows, at], g_o[:, at]
            got = []
            for half in range(2):
                h = 2 * t + half
                scores = right_trans(q_pair * masks[half], k_pair)
                probs = jnp.exp(jnp.where(same, scores, NEGATIVE) - lse[rows, h : h + 1])
                g_probs = right_trans(o_pair * masks[half], v_pair)
                inner = jnp.sum(g_probs * probs, axis=-1, keepdims=True)
                g_scores = (probs * (g_probs - inner)).astype(LOW)
                got.append(
                    (
                        plain_dot(g_scores, k_pair),
                        left_trans(g_scores, q_pair),
                        left_trans(probs.astype(LOW), o_pair),
                    )
                )
            g_q = (jnp.where(low_half, got[0][0], got[1][0]) * 0.125).astype(LOW)
            g_k = jnp.where(low_half, got[0][1], got[1][1]).astype(LOW)
            g_v = jnp.where(low_half, got[0][2], got[1][2]).astype(LOW)
            for i, part in enumerate((g_q, g_k, g_v)):
                g_qkv[rows, i * local + t * PAIR : i * local + (t + 1) * PAIR] = part
            put(s, 5, at, col_sum(g_q.astype(HIGH)))
            put(s, 5, slice(local + t * PAIR, local + (t + 1) * PAIR), col_sum(g_v.astype(HIGH)))
        part = right_trans(g_qkv[rows, :local], w_q[...])
        part = part + right_trans(g_qkv[rows, local : 2 * local], w_k[...])
        part = part + right_trans(g_qkv[rows, 2 * local :], w_v[...])
        g_first[rows, :] = part
        unit_one, _ = unit_rows(tokens[rows, :].astype(HIGH))
        put(s, 3, full, col_sum(part * unit_one))
        put(s, 4, full, col_sum(part))
    sums[6:7, :] = g_bias[:, :width]
    sums[7:8, :] = g_bias[:, width:]
    sums[8:9, :] = cot_sum[...]
    sums[9:, :] = jnp.zeros_like(sums[9:, :])


def last_kernel(tokens, gain, g_hidden, own, other, g_tokens):
    unit, scale = unit_rows(tokens[...].astype(HIGH))
    grad = own[...] + other[...]
    g_tokens[...] = g_hidden[...] + norm_back(grad * row(gain), unit, scale)


def out_kernel(*refs, seqs, length):
    bias, own, other = refs[:3]
    for s in range(seqs):
        rows = slice(s * length, (s + 1) * length)
        total = refs[3 + s][...] + (own[rows, :] + other[rows, :])
        refs[3 + seqs][rows, :] = (total + row(bias)).astype(LOW)


def dot_kernel(left, right, *refs, start, with_add):
    outs = refs[with_add:]
    for o, out in enumerate(outs):
        size = out.shape[0]
        at = slice(start + o * size, start + (o + 1) * size)
        step = min(512, right.shape[1])
        for n in range(0, right.shape[1], step):
            value = plain_dot(left[at, :], right[:, n : n + step])
            if with_add:
                part = refs[0].shape[0]
                if size > part:
                    got = [r[:, n : n + step] for r in refs[o * size // part : (o + 1) * size // part]]
                    value = value + jnp.concatenate(got)
                else:
                    low = o * size % part
                    value = value + refs[o * size // part][low : low + size, n : n + step]
            out[:, n : n + step] = value


def add_kernel(left, right, *outs):
    size = outs[0].shape[0]
    if left.shape[0] != size * len(outs):
        wide = outs[0].shape[1]
        for o, out in enumerate(outs):
            at = slice(o * wide, (o + 1) * wide)
            out[...] = left[:, at] + right[:, at]
        return
    for o, out in enumerate(outs):
        at = slice(o * size, (o + 1) * size)
        out[...] = left[at, :] + right[at, :]


def small_kernel(sums, other, out):
    out[...] = sums[...]
    out[3:5, :] = sums[3:5, :] + other[...]


def row(ref):
    return ref[...].reshape(1, ref.shape[0])


def same_crop(crops, seq):
    ids = crops[seq : seq + 1, :]
    marks = lax.broadcasted_iota(jnp.int32, (16, ids.shape[1]), 0) == ids
    marks = marks.astype(HIGH).astype(LOW)
    return left_trans(marks, marks) > 0.5


class Steps:
    def __init__(self):
        self.last = None

    def __call__(self, kernel, name, outs, args, scratch=(), limit=12, smem=0, tie=0, alias=None, whole=0, whole_out=0):
        args = list(args)
        if self.last is not None:
            args[tie], _ = lax.optimization_barrier((args[tie], self.last))
        result = pl.pallas_call(
            kernel,
            name=name,
            out_shape=[jax.ShapeDtypeStruct(s, d) for s, d in outs],
            in_specs=[pl.BlockSpec(memory_space=pltpu.SMEM)] * smem
            + [pl.BlockSpec(memory_space=pl.ANY)] * whole
            + [VMEM] * (len(args) - smem - whole),
            out_specs=[pl.BlockSpec(memory_space=pl.ANY)] * whole_out
            + [VMEM] * (len(outs) - whole_out),
            scratch_shapes=list(scratch),
            input_output_aliases=alias or {},
            compiler_params=pltpu.CompilerParams(vmem_limit_bytes=limit << 20),
            cost_estimate=pl.CostEstimate(flops=1000, bytes_accessed=1000, transcendentals=0),
        )(*args)
        self.last = result[0]
        return result


def pair_swap(bit, count):
    return [(i, i ^ bit) for i in range(count)]


def relative_rows(width, count, side_first):
    rest = count // 4
    size = width // count
    here = lax.axis_index("dp")
    place = lax.broadcasted_iota(jnp.int32, (width, 1), 0)
    block = place // size
    core = (here & 1) ^ (block // (2 * rest))
    inner = block % (2 * rest)
    side, far = (inner // rest, inner % rest) if side_first else (inner % 2, inner // 2)
    side = ((here >> 1) & 1) ^ side
    own = here >> 2
    if rest == 4:
        half = (own >= 2).astype(jnp.int32)
        mid = 1 + half
        edge = 3 * half
        far = jnp.where(far < 2, own ^ far, jnp.where(far == 2, 3 - mid, 3 - edge))
    else:
        far = own ^ far
    source = (far * 4 + side * 2 + core) * size + place % size
    return (lax.broadcasted_iota(jnp.int32, (width, width), 1) == source).astype(LOW)


def send(values, pairs):
    return lax.ppermute(values, "dp", pairs)


def swap(values):
    return lax.ppermute(values, "mp", [(0, 1), (1, 0)])


class Scatter:
    def __init__(self, steps, count, left, right, side_first, wide=1):
        self.steps, self.count, self.left, self.right = steps, count, left, right
        self.side_first, self.wide = side_first, wide
        self.columns = right.shape[1]
        self.half = left.shape[0] // 2

    def dot(self, start, added, sizes):
        outs = [((n, self.columns), HIGH) for n in sizes]
        kernel = partial(dot_kernel, start=start, with_add=len(added))
        return self.steps(kernel, "grad", outs, [self.left, self.right] + added)

    def add(self, left, right, pieces=1, wide=1):
        shape = (left.shape[0] // pieces, left.shape[1] // wide)
        return self.steps(add_kernel, "sum", [(shape, HIGH)] * (pieces * wide), [left, right])

    def start(self):
        parts = self.dot(self.half, [], [self.half // 2] * 2)
        self.far = [send(p, pair_swap(1, self.count)) for p in parts]

    def near(self):
        if self.side_first:
            self.keep, sent = self.dot(0, self.far, [self.half // 2] * 2)
            self.side = send(sent, pair_swap(2, self.count))
        elif self.count == 16:
            self.slots = self.dot(0, self.far, [self.half // 4] * 4)
            self.edges()
        else:
            self.keep = self.dot(0, self.far, [self.half])[0]

    def sides(self):
        if self.count == 16:
            self.slots = self.add(self.keep, self.side, 4)
            self.edges()
        else:
            self.keep = self.add(self.keep, self.side)[0]

    def edges(self):
        pairs = [(i, i ^ 4) for i in range(16) if i // 4 in (0, 3)]
        self.beyond = [send(self.slots[i], pairs) for i in (3, 2)]

    def mids(self, i):
        if self.count != 16:
            return
        pairs = [(i, i ^ 12) for i in range(16) if i // 4 in (1, 2)]
        total = self.add(self.slots[3 - i], self.beyond[i])[0]
        self.beyond[i] = send(total, pairs)

    def pairs(self):
        if self.count != 16:
            return
        total = self.add(self.slots[1], self.beyond[0])[0]
        self.near_sum = send(total, pair_swap(4, 16))

    def own(self):
        if self.count != 16:
            return
        self.keep = self.add(self.slots[0], self.beyond[1])[0]

    def finish(self):
        if self.count != 16:
            slots, bit = self.keep, self.count // 8
            while bit:
                part = slots.shape[0] // 2
                slots = slots[:part] + send(slots[part:], pair_swap(4 * bit, self.count))
                bit //= 2
            if not self.side_first:
                part = slots.shape[0] // 2
                slots = slots[:part] + send(slots[part:], pair_swap(2, self.count))
            wide = self.columns // self.wide
            return [slots[:, i * wide : (i + 1) * wide] for i in range(self.wide)]
        if self.side_first:
            return self.add(self.keep, self.near_sum, 1, self.wide)
        self.keep, sent = self.add(self.keep, self.near_sum, 2)
        self.side = send(sent, pair_swap(2, 16))
        return None

    def close(self):
        if self.count != 16:
            return self.finish()
        return self.add(self.keep, self.side, 1, self.wide)


def body(
    tokens,
    crop_ids,
    w_query,
    w_key,
    w_value,
    bias_query,
    bias_value,
    w_out,
    bias_out,
    gain_attn,
    shift_attn,
    gain_mlp,
    shift_mlp,
    w_up,
    bias_up,
    w_down,
    bias_down,
    cotangent,
    count,
):
    width = tokens.shape[1]
    local = w_query.shape[1]
    hidden_units = w_up.shape[1]
    seqs, length = crop_ids.shape
    rows = seqs * length
    here = lax.axis_index("dp")
    place = here & 3
    steps = Steps()

    piece = local // 4
    mine = lax.dynamic_slice(w_out, (place * piece, 0), (piece, width)).astype(HIGH)
    got = swap(mine)

    loaded = [
        tokens,
        gain_attn,
        shift_attn,
        w_query,
        w_key,
        w_value,
        bias_query,
        bias_value,
        crop_ids,
    ]
    kept = [((rows, local), LOW)] * 3 + [((rows, 128), HIGH)]
    front = steps(
        partial(front_kernel, length=length, seqs=seqs),
        "front",
        kept + [((rows, width), LOW)] + [((length, local), HIGH)] * seqs,
        loaded,
        scratch=[pltpu.VMEM(a.shape, a.dtype) for a in loaded]
        + [pltpu.VMEM(*k) for k in kept]
        + [pltpu.SemaphoreType.DMA((len(loaded) + len(kept),))],
        whole=len(loaded),
        whole_out=len(kept),
        limit=52,
    )
    query, key_rows, value_rows, log_total, first = front[:5]
    mixed = front[5:]
    mixed_other = [swap(o) for o in mixed]

    o_low = jnp.concatenate([o.astype(LOW) for o in mixed])
    side_order = relative_rows(width, count, True)
    far_order = relative_rows(width, count, False)
    beside = send(got, pair_swap(2, count))
    pieces = [got, send(got, pair_swap(1, count)), beside, send(beside, pair_swap(1, count))]
    a1_t, cot_t, cot_sum = steps(
        turn_kernel,
        "turn",
        [((width, rows), LOW)] * 2 + [((1, width), HIGH)],
        [side_order, first, cotangent],
    )

    shared = [
        ((rows, width), HIGH),
        ((width, rows), LOW),
        ((rows, hidden_units), LOW),
        ((rows, hidden_units), LOW),
        ((1, hidden_units), HIGH),
    ]
    hidden, carried = [], []
    for s in range(seqs):
        result = steps(
            partial(middle_kernel, blocks=3, seq=s, length=length, chained=s > 0),
            "middle",
            [((length, width), HIGH)] + shared,
            [
                place.reshape(1),
                tokens,
                mixed[s],
                mixed_other[s],
                w_out,
                bias_out,
                gain_mlp,
                shift_mlp,
                w_up,
                bias_up,
                w_down,
                cotangent,
                far_order,
            ]
            + pieces
            + carried,
            scratch=[pltpu.VMEM((local, width), LOW)],
            smem=1,
            tie=2,
            alias={17 + i: 1 + i for i in range(5)} if s else None,
        )
        hidden.append(result[0])
        carried = list(result[1:])
    second, a2_t, active, g_pre, bias_sum = carried
    second_other = swap(second)

    down = Scatter(steps, count, cot_t, active, True)
    up = Scatter(steps, count, a2_t, g_pre, False)
    down.start()
    up.start()
    mlp_part = steps(
        partial(dot_kernel, start=0, with_add=0), "mlp", [((rows, width), HIGH)], [active, w_down]
    )[0]
    mlp_other = swap(mlp_part)
    down.near()
    up.near()

    up.mids(0)
    down.sides()
    g_hidden, g_first, gh_t, g_qkv, sums = steps(
        partial(back_kernel, seqs=seqs, length=length),
        "back",
        [((rows, width), HIGH)] * 2
        + [((width, rows), LOW), ((rows, 3 * local), LOW), ((16, width), HIGH)],
        [
            tokens,
            crop_ids,
            cotangent,
            second,
            second_other,
            gain_mlp,
            w_out,
            w_query,
            w_key,
            w_value,
            query,
            key_rows,
            value_rows,
            log_total,
            far_order,
            bias_sum,
            cot_sum,
        ]
        + hidden,
        tie=3,
    )
    heads_grad = Scatter(steps, count, a1_t, g_qkv, True, 3)
    out_grad = Scatter(steps, count, gh_t, o_low, False)
    first_other = swap(g_first)
    finals = {}

    def keep(name, act):
        finals[name] = act()

    def write_out():
        return steps(
            partial(out_kernel, seqs=seqs, length=length),
            "out",
            [((rows, width), LOW)],
            [bias_down, mlp_part, mlp_other] + hidden,
            tie=1,
        )[0]

    turns = [
        [lambda: up.mids(1), up.pairs, lambda: down.mids(0), lambda: down.mids(1)],
        [heads_grad.start, out_grad.start],
        [heads_grad.near, out_grad.near, up.own, down.pairs],
        [up.finish, down.own, lambda: keep("out", write_out)],
        [lambda: out_grad.mids(0), lambda: out_grad.mids(1), out_grad.pairs, out_grad.own],
        [heads_grad.sides, lambda: keep("down", down.finish), out_grad.finish],
        [lambda: heads_grad.mids(0), lambda: heads_grad.mids(1)],
        [lambda: keep("up", up.close), heads_grad.pairs, heads_grad.own],
        [lambda: keep("wo", out_grad.close), lambda: keep("heads", heads_grad.finish)],
    ]
    small, bit = sums, 1
    for acts in turns:
        got = send(small, pair_swap(bit, count)) if bit < count else None
        for act in acts:
            act()
        if bit < count:
            small = steps(add_kernel, "small", [((16, width), HIGH)], [small, got])[0]
        bit *= 2
    while bit < count:
        got = send(small, pair_swap(bit, count))
        small = steps(add_kernel, "small", [((16, width), HIGH)], [small, got])[0]
        bit *= 2
    block_out, grads = finals["out"], finals["heads"]
    done_w_down, done_w_up, done_w_out = finals["down"][0].T, finals["up"][0], finals["wo"][0].T
    small_other = swap(small[3:5])
    grad_tokens = steps(
        last_kernel,
        "last",
        [((rows, width), HIGH)],
        [tokens, gain_attn, g_hidden, g_first, first_other],
        tie=3,
    )[0]
    packed = steps(small_kernel, "packed", [((16, width), HIGH)], [small, small_other])[0]
    size = width // count
    blocks = lax.dynamic_slice(packed, (0, here * size), (9, size))
    return (
        block_out,
        grad_tokens,
        grads[0],
        grads[1],
        grads[2],
        packed[5, :local],
        packed[5, local:],
        done_w_out,
        blocks[2],
        blocks[3],
        blocks[4],
        blocks[0],
        blocks[1],
        done_w_up,
        packed[6:8].reshape(-1),
        done_w_down,
        blocks[8],
    )


def solution(mesh):
    placed = (
        P("dp", None),
        P("dp", None),
        P(None, "mp"),
        P(None, "mp"),
        P(None, "mp"),
        P("mp"),
        P("mp"),
        P("mp", None),
        P(),
        P(),
        P(),
        P(),
        P(),
        P(None, "mp"),
        P("mp"),
        P("mp", None),
        P(),
        P("dp", None),
    )
    return jax.shard_map(
        partial(body, count=mesh.shape["dp"]),
        mesh=mesh,
        in_specs=placed,
        out_specs=(
            P("dp", None),
            P("dp", None),
            P("dp", "mp"),
            P("dp", "mp"),
            P("dp", "mp"),
            P("mp"),
            P("mp"),
            P("mp", "dp"),
            P("dp"),
            P("dp"),
            P("dp"),
            P("dp"),
            P("dp"),
            P("dp", "mp"),
            P("mp"),
            P("mp", "dp"),
            P("dp"),
        ),
        check_vma=False,
    )
```

time: 668 us -> 191 us (0.29)
  waiting for transfers between devices: 493 us -> 56.8 us
  starting transfers between devices: 0.77 us -> 73 us
  blocking collectives: 61.4 us -> 0 us
  matrix products: 57.7 us -> 0 us
  Pallas kernels: 0 us -> 44.9 us
  other arithmetic: 26.4 us -> 1.6 us
  between operations: 15.2 us -> 1.44 us
    reduce_scatter x6 -> x0, waiting for transfers between devices: 334 us -> none  [the longest x1 79.5 us: body(): lax.psum_scatter(grad_w_up, 'dp', scatter_dimension=0, tiled=True)]
    psum x3 -> x0, waiting for transfers between devices: 159 us -> none  [the longest x1 60.5 us: body(): mlp_sum = lax.psum(plain_dot(active, w_down), 'mp')]
    ppermute x0 -> x46, starting transfers between devices: none -> 73 us  [the longest x39 65.3 us: send(): return lax.ppermute(values, 'dp', pairs)]
    psum x1 -> x0, blocking collectives: 61.4 us -> none  [body(): lax.psum((grad_bias_query, grad_bias_value, grad_bias_up), 'dp')]
    dot_general x24 -> x0, matrix products: 57.7 us -> none  [the longest x6 22.8 us: left_trans(): lax.dot_general(left, right, (((0,), (0,)), ((), ())), preferred_element_...]
    ppermute x0 -> x46, waiting for transfers between devices: none -> 56.8 us  [the longest x39 43.4 us: send(): return lax.ppermute(values, 'dp', pairs)]
    pallas_call x0 -> x45, Pallas kernels: none -> 44.9 us  [__call__(): pl.pallas_call(kernel, name=name, out_shape=[jax.ShapeDtypeStruct(s, d) f...]
    reduce_sum x8 -> x0, other arithmetic: 14 us -> none  [the longest x1 3.32 us: body(): grad_gain_mlp = jnp.sum(grad_second * unit_two, axis=0)]
  transfers between devices with their start and end apart: 9 -> 46, of which waited for: 8 -> 17; matrix products, arithmetic and copies ran while one was open for 6% -> 1% of each run, Pallas kernels for 0% -> 21%
where the time goes in v1:
time: 191 us; the launch traced here: 190 us
  starting transfers between devices  73 us (38%)
  waiting for transfers between devices  56.8 us (30%)
  Pallas kernels  44.9 us (24%)
  local copies, waits for them, and re-layouts  12.1 us (6%)
    ppermute x39, starting transfers between devices, send(): return lax.ppermute(values, 'dp', pairs)  65.3 us
    pallas_call x45, Pallas kernels, __call__(): pl.pallas_call(kernel, name=name, out_shape=[jax.ShapeDtypeStruct(s, d) f...  44.9 us
    ppermute x39, waiting for transfers between devices, send(): return lax.ppermute(values, 'dp', pairs)  43.4 us
    ppermute x7, waiting for transfers between devices, swap(): return lax.ppermute(values, 'mp', [(0, 1), (1, 0)])  13.5 us
    unnamed x74, local copies, waits for them, and re-layouts  9.73 us
    ppermute x7, starting transfers between devices, swap(): return lax.ppermute(values, 'mp', [(0, 1), (1, 0)])  7.64 us
  transfers between devices with their start and end apart: 46, of which 17 were waited for; matrix products, arithmetic and copies ran while one was open for 1% of the time, Pallas kernels for 21%

profile of v1, /device:TPU:0, one launch (start us, length us, event | category | flops | bytes accessed | tf_op | source)
XLA Modules:
  0.0 189.9 jit_solution(7969603538914266185)
XLA Ops:
  1.6 3.0 %collective-permute-start.1 = (f32[96,768]{1,0:T(8,128)S(1)}, f32[96,768]{1,0:T(8,128)S(1)}, u32[]{:S(2)}, u32[]{:S(2)}) collective-permute-start(f32[96,768]{1,0:T(8,128)S(1)} %dynamic-slice_convert_fusion), channel_id=1, source_target_pairs={{0,1},{1,0},{2,3},{3,2},{4,5},{5,4},{6,7},{7,6},{8,9},{9,8},{10,11... | collective-permute-start | bytes 884744 | tf_op jit(solution)/shard_map/ppermute | solution.py:327
  8.0 7.1 %front.1 = (bf16[512,384]{1,0:T(8,128)(2,1)S(1)}, bf16[512,384]{1,0:T(8,128)(2,1)S(1)}, bf16[512,384]{1,0:T(8,128)(2,1)S(1)}, f32[512,128]{1,0:T(8,128)S(1)}, bf...) custom-call(bf16[512,768]{1,0:T(8,128)(2,1)} %tokens.1, f32[768]{0:T(1024)S(1)} %copy-done.27, ...), custom_call_target="tpu_custom_call" | custom-call | flops 1000 | bytes 1000 | tf_op jit(solution)/shard_map/front/pallas_call | solution.py:278
  22.1 6.0 %collective-permute-done.3.refs_15_ = f32[96,768]{1,0:T(8,128)S(1)} collective-permute-done((f32[96,768]{1,0:T(8,128)S(1)}, f32[96,768]{1,0:T(8,128)S(1)}, u32[]{:S(2)}, u32[]{:S(2)}) %collective-permute-start.3) | collective-permute-done | bytes 294944 | tf_op jit(solution)/shard_map/ppermute | solution.py:323
  32.0 3.6 %middle.2 = (f32[256,768]{1,0:T(8,128)S(1)}, f32[512,768]{1,0:T(8,128)S(1)}, bf16[768,512]{1,0:T(8,128)(2,1)S(1)}, bf16[512,1536]{1,0:T(8,128)(2,1)S(1)}, bf16[5...) custom-call(s32[1]{0:T(128)} %bitcast.refs_0_, bf16[512,768]{1,0:T(8,128)(2,1)S(1)} %copy-done.1, ...), custom_call_target="tpu_custom_call" | custom-call | flops 1000 | bytes 1000 | tf_op jit(solution)/shard_map/middle/pallas_call | solution.py:278
  37.3 4.6 %middle.3 = (f32[256,768]{1,0:T(8,128)S(1)}, f32[512,768]{1,0:T(8,128)S(1)}, bf16[768,512]{1,0:T(8,128)(2,1)S(1)}, bf16[512,1536]{1,0:T(8,128)(2,1)S(1)}, bf16[5...) custom-call(s32[1]{0:T(128)} %bitcast.refs_0_, ...), custom_call_target="tpu_custom_call", output_to_operand_aliasing={{1}: (17, {}), {2}: (18, {}), {3}: (19, {}), {4}: (20, {}),... | custom-call | flops 1000 | bytes 1000 | tf_op jit(solution)/shard_map/middle/pallas_call | solution.py:278
  52.0 3.5 %collective-permute-start.10 = (f32[96,1536]{1,0:T(8,128)S(1)}, f32[96,1536]{1,0:T(8,128)S(1)}, u32[]{:S(2)}, u32[]{:S(2)}) collective-permute-start(f32[96,1536]{1,0:T(8,128)S(1)} %get-tuple-element.154.left), channel_id=1, source_target_pairs={{0,8},{2,10},{4,12},{6,14},{24,16},{26,18},{28,20},{30,22},{1,9},{... | collective-permute-start | bytes 1769480 | tf_op jit(solution)/shard_map/ppermute | solution.py:323
  57.4 11.7 %collective-permute-done.10.right = f32[96,1536]{1,0:T(8,128)S(1)} collective-permute-done((f32[96,1536]{1,0:T(8,128)S(1)}, f32[96,1536]{1,0:T(8,128)S(1)}, u32[]{:S(2)}, u32[]{:S(2)}) %collective-permute-start.10) | collective-permute-done | bytes 589856 | tf_op jit(solution)/shard_map/ppermute | solution.py:323
  70.1 6.0 %collective-permute-done.11.right = f32[192,1536]{1,0:T(8,128)S(1)} collective-permute-done((f32[192,1536]{1,0:T(8,128)S(1)}, f32[192,1536]{1,0:T(8,128)S(1)}, u32[]{:S(2)}, u32[]{:S(2)}) %collective-permute-start.11) | collective-permute-done | bytes 1179680 | tf_op jit(solution)/shard_map/ppermute | solution.py:323
  76.3 3.5 %collective-permute-start.15 = (f32[48,1536]{1,0:T(8,128)S(1)}, f32[48,1536]{1,0:T(8,128)S(1)}, u32[]{:S(2)}, u32[]{:S(2)}) collective-permute-start(f32[48,1536]{1,0:T(8,128)S(1)} %get-tuple-element.174.left), channel_id=1, source_target_pairs={{0,8},{2,10},{4,12},{6,14},{24,16},{26,18},{28,20},{30,22},{1,9},{... | collective-permute-start | bytes 884744 | tf_op jit(solution)/shard_map/ppermute | solution.py:323
  79.8 2.1 %collective-permute-done.12.refs_4_ = f32[512,768]{1,0:T(8,128)S(1)} collective-permute-done((f32[512,768]{1,0:T(8,128)S(1)}, f32[512,768]{1,0:T(8,128)S(1)}, u32[]{:S(2)}, u32[]{:S(2)}) %collective-permute-start.12) | collective-permute-done | bytes 1572896 | tf_op jit(solution)/shard_map/ppermute | solution.py:327
  81.9 3.5 %collective-permute-start.16 = (f32[48,1536]{1,0:T(8,128)S(1)}, f32[48,1536]{1,0:T(8,128)S(1)}, u32[]{:S(2)}, u32[]{:S(2)}) collective-permute-start(f32[48,1536]{1,0:T(8,128)S(1)} %get-tuple-element.175.left), channel_id=1, source_target_pairs={{0,8},{2,10},{4,12},{6,14},{24,16},{26,18},{28,20},{30,22},{1,9},{... | collective-permute-start | bytes 884744 | tf_op jit(solution)/shard_map/ppermute | solution.py:323
  85.4 10.2 %back.1 = (f32[512,768]{1,0:T(8,128)S(1)}, f32[512,768]{1,0:T(8,128)}, bf16[768,512]{1,0:T(8,128)(2,1)S(1)}, bf16[512,1152]{1,0:T(8,128)(2,1)S(1)}, f32[16,768]{1,0:T(8,128)S(1)}) custom-call(bf16[512,768]{1,0:T(8,128)(2,1)S(1)} %copy-done.1, s32[2,256]{1,0:T(2,128)S(1)} %copy-done.32, bf16[512,768]{1,0:T(8,128)(2,1)S(1)} %copy-done.2, ...), custom_call_target="tpu_custom_call" | custom-call | flops 1000 | bytes 1000 | tf_op jit(solution)/shard_map/back/pallas_call | solution.py:278
  100.9 2.2 %collective-permute-done.18.right = f32[16,768]{1,0:T(8,128)S(1)} collective-permute-done((f32[16,768]{1,0:T(8,128)S(1)}, f32[16,768]{1,0:T(8,128)S(1)}, u32[]{:S(2)}, u32[]{:S(2)}) %collective-permute-start.18) | collective-permute-done | bytes 49184 | tf_op jit(solution)/shard_map/ppermute | solution.py:323
  103.1 2.2 %collective-permute-start.25 = (f32[16,768]{1,0:T(8,128)S(1)}, f32[16,768]{1,0:T(8,128)S(1)}, u32[]{:S(2)}, u32[]{:S(2)}) collective-permute-start(f32[16,768]{1,0:T(8,128)S(1)} %small.5.left), channel_id=1, source_target_pairs={{0,8},{2,10},{4,12},{6,14},{8,0},{10,2},{12,4},{14,6},{16,24},{18,... | collective-permute-start | bytes 147464 | tf_op jit(solution)/shard_map/ppermute | solution.py:323
  105.3 9.4 %collective-permute-done.28.refs_2_ = f32[512,768]{1,0:T(8,128)S(1)} collective-permute-done((f32[512,768]{1,0:T(8,128)S(1)}, f32[512,768]{1,0:T(8,128)S(1)}, u32[]{:S(2)}, u32[]{:S(2)}) %collective-permute-start.28) | collective-permute-done | bytes 1572896 | tf_op jit(solution)/shard_map/ppermute | solution.py:327
  121.8 7.4 %collective-permute-done.26.right = f32[96,1536]{1,0:T(8,128)S(1)} collective-permute-done((f32[96,1536]{1,0:T(8,128)S(1)}, f32[96,1536]{1,0:T(8,128)S(1)}, u32[]{:S(2)}, u32[]{:S(2)}) %collective-permute-start.26) | collective-permute-done | bytes 589856 | tf_op jit(solution)/shard_map/ppermute | solution.py:323
  129.3 3.6 %collective-permute-start.30 = (f32[96,384]{1,0:T(8,128)S(1)}, f32[96,384]{1,0:T(8,128)S(1)}, u32[]{:S(2)}, u32[]{:S(2)}) collective-permute-start(f32[96,384]{1,0:T(8,128)S(1)} %get-tuple-element.202.left), channel_id=1, source_target_pairs={{0,8},{2,10},{4,12},{6,14},{24,16},{26,18},{28,20},{30,22},{1,9},{... | collective-permute-start | bytes 442376 | tf_op jit(solution)/shard_map/ppermute | solution.py:323
  134.6 4.7 %collective-permute-start.29 = (f32[16,768]{1,0:T(8,128)S(1)}, f32[16,768]{1,0:T(8,128)S(1)}, u32[]{:S(2)}, u32[]{:S(2)}) collective-permute-start(f32[16,768]{1,0:T(8,128)S(1)} %small.6.left), channel_id=1, source_target_pairs={{0,16},{2,18},{4,20},{6,22},{8,24},{10,26},{12,28},{14,30},{16,0},... | collective-permute-start | bytes 147464 | tf_op jit(solution)/shard_map/ppermute | solution.py:323
  143.4 5.8 %collective-permute-start.35 = (f32[48,1536]{1,0:T(8,128)S(1)}, f32[48,1536]{1,0:T(8,128)S(1)}, u32[]{:S(2)}, u32[]{:S(2)}) collective-permute-start(f32[48,1536]{1,0:T(8,128)S(1)} %sum.31), channel_id=1, source_target_pairs={{0,8},{2,10},{4,12},{6,14},{8,0},{10,2},{12,4},{14,6},{16,24},{18,... | collective-permute-start | bytes 884744 | tf_op jit(solution)/shard_map/ppermute | solution.py:323
  150.0 6.6 %collective-permute-start.37 = (f32[48,1152]{1,0:T(8,128)S(1)}, f32[48,1152]{1,0:T(8,128)S(1)}, u32[]{:S(2)}, u32[]{:S(2)}) collective-permute-start(f32[48,1152]{1,0:T(8,128)S(1)} %get-tuple-element.215.left), channel_id=1, source_target_pairs={{0,8},{2,10},{4,12},{6,14},{24,16},{26,18},{28,20},{30,22},{1,9},{... | collective-permute-start | bytes 663560 | tf_op jit(solution)/shard_map/ppermute | solution.py:323
  157.3 3.9 %collective-permute-start.38 = (f32[48,1152]{1,0:T(8,128)S(1)}, f32[48,1152]{1,0:T(8,128)S(1)}, u32[]{:S(2)}, u32[]{:S(2)}) collective-permute-start(f32[48,1152]{1,0:T(8,128)S(1)} %get-tuple-element.216.left), channel_id=1, source_target_pairs={{0,8},{2,10},{4,12},{6,14},{24,16},{26,18},{28,20},{30,22},{1,9},{... | collective-permute-start | bytes 663560 | tf_op jit(solution)/shard_map/ppermute | solution.py:323
  161.9 3.2 %collective-permute-done.36.right = f32[96,384]{1,0:T(8,128)S(1)} collective-permute-done((f32[96,384]{1,0:T(8,128)S(1)}, f32[96,384]{1,0:T(8,128)S(1)}, u32[]{:S(2)}, u32[]{:S(2)}) %collective-permute-start.36) | collective-permute-done | bytes 147488 | tf_op jit(solution)/shard_map/ppermute | solution.py:323
  169.7 7.5 %collective-permute-start.43 = (f32[48,1152]{1,0:T(8,128)S(1)}, f32[48,1152]{1,0:T(8,128)S(1)}, u32[]{:S(2)}, u32[]{:S(2)}) collective-permute-start(f32[48,1152]{1,0:T(8,128)S(1)} %sum.44), channel_id=1, source_target_pairs={{0,8},{2,10},{4,12},{6,14},{8,0},{10,2},{12,4},{14,6},{16,24},{18,... | collective-permute-start | bytes 663560 | tf_op jit(solution)/shard_map/ppermute | solution.py:323
  184.0 4.1 %last.1 = f32[512,768]{1,0:T(8,128)} custom-call(bf16[512,768]{1,0:T(8,128)(2,1)S(1)} %copy-done.1, f32[768]{0:T(1024)S(1)} %copy-done.28, f32[512,768]{1,0:T(8,128)S(1)} %get-tuple-element.171.g_hidden, f32[512,768]{1,0:T(8,128)} %get-tuple-element.225.own, f32[512,768]{1,0:T(8,128)} %collective-permute-done.44.other), custom_call_target="tpu_custom_call" | custom-call | flops 1000 | bytes 1000 | tf_op jit(solution)/shard_map/last/pallas_call | solution.py:278
  (200 shorter events, 63.0 us)
Async XLA Ops:
  1.6 18.6 %collective-permute-start.1 = (f32[96,768]{1,0:T(8,128)S(1)}, f32[96,768]{1,0:T(8,128)S(1)}, u32[]{:S(2)}, u32[]{:S(2)}) collective-permute-start(f32[96,768]{1,0:T(8,128)S(1)} %dynamic-slice_convert_fusion), channel_id=1, source_target_pairs={{0,1},{1,0},{2,3},{3,2},{4,5},{5,4},{6,7},{7,6},{8,9},{9,8},{10,11... | collective-permute-start | bytes 884744 | tf_op jit(solution)/shard_map/ppermute | solution.py:327
  18.2 19.0 %collective-permute-start.5 = (f32[256,384]{1,0:T(8,128)}, f32[256,384]{1,0:T(8,128)}, u32[]{:S(2)}, u32[]{:S(2)}) collective-permute-start(f32[256,384]{1,0:T(8,128)} %get-tuple-element.131.refs_2_), channel_id=1, source_target_pairs={{0,1},{1,0},{2,3},{3,2},{4,5},{5,4},{6,7},{7,6},{8,9},{9,8},{10,11... | collective-permute-start | bytes 1179656 | tf_op jit(solution)/shard_map/ppermute | solution.py:327
  44.6 37.2 %collective-permute-start.12 = (f32[512,768]{1,0:T(8,128)S(1)}, f32[512,768]{1,0:T(8,128)S(1)}, u32[]{:S(2)}, u32[]{:S(2)}) collective-permute-start(f32[512,768]{1,0:T(8,128)S(1)} %get-tuple-element.159.refs_3_), channel_id=1, source_target_pairs={{0,1},{1,0},{2,3},{3,2},{4,5},{5,4},{6,7},{7,6},{8,9},{9,8},{10,11... | collective-permute-start | bytes 4718600 | tf_op jit(solution)/shard_map/ppermute | solution.py:327
  48.1 28.1 %collective-permute-start.11 = (f32[192,1536]{1,0:T(8,128)S(1)}, f32[192,1536]{1,0:T(8,128)S(1)}, u32[]{:S(2)}, u32[]{:S(2)}) collective-permute-start(f32[192,1536]{1,0:T(8,128)S(1)} %get-tuple-element.156), channel_id=1, source_target_pairs={{0,4},{2,6},{4,0},{6,2},{8,12},{10,14},{12,8},{14,10},{16,20},{18,... | collective-permute-start | bytes 3538952 | tf_op jit(solution)/shard_map/ppermute | solution.py:323
  52.0 17.2 %collective-permute-start.10 = (f32[96,1536]{1,0:T(8,128)S(1)}, f32[96,1536]{1,0:T(8,128)S(1)}, u32[]{:S(2)}, u32[]{:S(2)}) collective-permute-start(f32[96,1536]{1,0:T(8,128)S(1)} %get-tuple-element.154.left), channel_id=1, source_target_pairs={{0,8},{2,10},{4,12},{6,14},{24,16},{26,18},{28,20},{30,22},{1,9},{... | collective-permute-start | bytes 1769480 | tf_op jit(solution)/shard_map/ppermute | solution.py:323
  55.5 59.2 %collective-permute-start.28 = (f32[512,768]{1,0:T(8,128)S(1)}, f32[512,768]{1,0:T(8,128)S(1)}, u32[]{:S(2)}, u32[]{:S(2)}) collective-permute-start(f32[512,768]{1,0:T(8,128)S(1)} %mlp.1.refs_1_), channel_id=1, source_target_pairs={{0,1},{1,0},{2,3},{3,2},{4,5},{5,4},{6,7},{7,6},{8,9},{9,8},{10,11... | collective-permute-start | bytes 4718600 | tf_op jit(solution)/shard_map/ppermute | solution.py:327
  56.1 39.5 %collective-permute-start.13 = (f32[96,1536]{1,0:T(8,128)S(1)}, f32[96,1536]{1,0:T(8,128)S(1)}, u32[]{:S(2)}, u32[]{:S(2)}) collective-permute-start(f32[96,1536]{1,0:T(8,128)S(1)} %get-tuple-element.172.left), channel_id=1, source_target_pairs={{0,8},{2,10},{4,12},{6,14},{24,16},{26,18},{28,20},{30,22},{1,9},{... | collective-permute-start | bytes 1769480 | tf_op jit(solution)/shard_map/ppermute | solution.py:323
  69.3 26.4 %collective-permute-start.14 = (f32[96,1536]{1,0:T(8,128)S(1)}, f32[96,1536]{1,0:T(8,128)S(1)}, u32[]{:S(2)}, u32[]{:S(2)}) collective-permute-start(f32[96,1536]{1,0:T(8,128)S(1)} %sum.24), channel_id=1, source_target_pairs={{8,16},{10,18},{12,20},{14,22},{16,8},{18,10},{20,12},{22,14},{9,1... | collective-permute-start | bytes 1769480 | tf_op jit(solution)/shard_map/ppermute | solution.py:323
  76.3 19.5 %collective-permute-start.15 = (f32[48,1536]{1,0:T(8,128)S(1)}, f32[48,1536]{1,0:T(8,128)S(1)}, u32[]{:S(2)}, u32[]{:S(2)}) collective-permute-start(f32[48,1536]{1,0:T(8,128)S(1)} %get-tuple-element.174.left), channel_id=1, source_target_pairs={{0,8},{2,10},{4,12},{6,14},{24,16},{26,18},{28,20},{30,22},{1,9},{... | collective-permute-start | bytes 884744 | tf_op jit(solution)/shard_map/ppermute | solution.py:323
  81.9 14.0 %collective-permute-start.16 = (f32[48,1536]{1,0:T(8,128)S(1)}, f32[48,1536]{1,0:T(8,128)S(1)}, u32[]{:S(2)}, u32[]{:S(2)}) collective-permute-start(f32[48,1536]{1,0:T(8,128)S(1)} %get-tuple-element.175.left), channel_id=1, source_target_pairs={{0,8},{2,10},{4,12},{6,14},{24,16},{26,18},{28,20},{30,22},{1,9},{... | collective-permute-start | bytes 884744 | tf_op jit(solution)/shard_map/ppermute | solution.py:323
  97.6 17.5 %collective-permute-start.19 = (f32[192,1152]{1,0:T(8,128)S(1)}, f32[192,1152]{1,0:T(8,128)S(1)}, u32[]{:S(2)}, u32[]{:S(2)}) collective-permute-start(f32[192,1152]{1,0:T(8,128)S(1)} %get-tuple-element.179), channel_id=1, source_target_pairs={{0,2},{2,0},{4,6},{6,4},{8,10},{10,8},{12,14},{14,12},{16,18},{18,... | collective-permute-start | bytes 2654216 | tf_op jit(solution)/shard_map/ppermute | solution.py:323
  97.8 19.0 %collective-permute-start.20 = (f32[192,1152]{1,0:T(8,128)S(1)}, f32[192,1152]{1,0:T(8,128)S(1)}, u32[]{:S(2)}, u32[]{:S(2)}) collective-permute-start(f32[192,1152]{1,0:T(8,128)S(1)} %get-tuple-element.184), channel_id=1, source_target_pairs={{0,2},{2,0},{4,6},{6,4},{8,10},{10,8},{12,14},{14,12},{16,18},{18,... | collective-permute-start | bytes 2654216 | tf_op jit(solution)/shard_map/ppermute | solution.py:323
  98.1 21.0 %collective-permute-start.23 = (f32[96,1536]{1,0:T(8,128)S(1)}, f32[96,1536]{1,0:T(8,128)S(1)}, u32[]{:S(2)}, u32[]{:S(2)}) collective-permute-start(f32[96,1536]{1,0:T(8,128)S(1)} %sum.26), channel_id=1, source_target_pairs={{8,16},{10,18},{12,20},{14,22},{16,8},{18,10},{20,12},{22,14},{9,1... | collective-permute-start | bytes 1769480 | tf_op jit(solution)/shard_map/ppermute | solution.py:323
  103.1 14.5 %collective-permute-start.25 = (f32[16,768]{1,0:T(8,128)S(1)}, f32[16,768]{1,0:T(8,128)S(1)}, u32[]{:S(2)}, u32[]{:S(2)}) collective-permute-start(f32[16,768]{1,0:T(8,128)S(1)} %small.5.left), channel_id=1, source_target_pairs={{0,8},{2,10},{4,12},{6,14},{8,0},{10,2},{12,4},{14,6},{16,24},{18,... | collective-permute-start | bytes 147464 | tf_op jit(solution)/shard_map/ppermute | solution.py:323
  114.7 69.3 %collective-permute-start.44 = (f32[512,768]{1,0:T(8,128)}, f32[512,768]{1,0:T(8,128)}, u32[]{:S(2)}, u32[]{:S(2)}) collective-permute-start(f32[512,768]{1,0:T(8,128)} %get-tuple-element.225.own), channel_id=1, source_target_pairs={{0,1},{1,0},{2,3},{3,2},{4,5},{5,4},{6,7},{7,6},{8,9},{9,8},{10,11... | collective-permute-start | bytes 4718600 | tf_op jit(solution)/shard_map/ppermute | solution.py:327
  115.0 14.2 %collective-permute-start.26 = (f32[96,1536]{1,0:T(8,128)S(1)}, f32[96,1536]{1,0:T(8,128)S(1)}, u32[]{:S(2)}, u32[]{:S(2)}) collective-permute-start(f32[96,1536]{1,0:T(8,128)S(1)} %sum.27), channel_id=1, source_target_pairs={{0,8},{2,10},{4,12},{6,14},{8,0},{10,2},{12,4},{14,6},{16,24},{18,... | collective-permute-start | bytes 1769480 | tf_op jit(solution)/shard_map/ppermute | solution.py:323
  117.5 31.7 %collective-permute-start.34 = (f32[192,1152]{1,0:T(8,128)S(1)}, f32[192,1152]{1,0:T(8,128)S(1)}, u32[]{:S(2)}, u32[]{:S(2)}) collective-permute-start(f32[192,1152]{1,0:T(8,128)S(1)} %get-tuple-element.207), channel_id=1, source_target_pairs={{0,4},{2,6},{4,0},{6,2},{8,12},{10,14},{12,8},{14,10},{16,20},{18,... | collective-permute-start | bytes 2654216 | tf_op jit(solution)/shard_map/ppermute | solution.py:323
  119.4 13.5 %collective-permute-start.24 = (f32[48,1536]{1,0:T(8,128)S(1)}, f32[48,1536]{1,0:T(8,128)S(1)}, u32[]{:S(2)}, u32[]{:S(2)}) collective-permute-start(f32[48,1536]{1,0:T(8,128)S(1)} %sum.28), channel_id=1, source_target_pairs={{8,16},{10,18},{12,20},{14,22},{16,8},{18,10},{20,12},{22,14},{9,1... | collective-permute-start | bytes 884744 | tf_op jit(solution)/shard_map/ppermute | solution.py:323
  120.7 13.9 %collective-permute-start.27 = (f32[48,1536]{1,0:T(8,128)S(1)}, f32[48,1536]{1,0:T(8,128)S(1)}, u32[]{:S(2)}, u32[]{:S(2)}) collective-permute-start(f32[48,1536]{1,0:T(8,128)S(1)} %sum.29), channel_id=1, source_target_pairs={{8,16},{10,18},{12,20},{14,22},{16,8},{18,10},{20,12},{22,14},{9,1... | collective-permute-start | bytes 884744 | tf_op jit(solution)/shard_map/ppermute | solution.py:323
  129.3 12.7 %collective-permute-start.30 = (f32[96,384]{1,0:T(8,128)S(1)}, f32[96,384]{1,0:T(8,128)S(1)}, u32[]{:S(2)}, u32[]{:S(2)}) collective-permute-start(f32[96,384]{1,0:T(8,128)S(1)} %get-tuple-element.202.left), channel_id=1, source_target_pairs={{0,8},{2,10},{4,12},{6,14},{24,16},{26,18},{28,20},{30,22},{1,9},{... | collective-permute-start | bytes 442376 | tf_op jit(solution)/shard_map/ppermute | solution.py:323
  143.4 13.9 %collective-permute-start.35 = (f32[48,1536]{1,0:T(8,128)S(1)}, f32[48,1536]{1,0:T(8,128)S(1)}, u32[]{:S(2)}, u32[]{:S(2)}) collective-permute-start(f32[48,1536]{1,0:T(8,128)S(1)} %sum.31), channel_id=1, source_target_pairs={{0,8},{2,10},{4,12},{6,14},{8,0},{10,2},{12,4},{14,6},{16,24},{18,... | collective-permute-start | bytes 884744 | tf_op jit(solution)/shard_map/ppermute | solution.py:323
  150.0 15.8 %collective-permute-start.37 = (f32[48,1152]{1,0:T(8,128)S(1)}, f32[48,1152]{1,0:T(8,128)S(1)}, u32[]{:S(2)}, u32[]{:S(2)}) collective-permute-start(f32[48,1152]{1,0:T(8,128)S(1)} %get-tuple-element.215.left), channel_id=1, source_target_pairs={{0,8},{2,10},{4,12},{6,14},{24,16},{26,18},{28,20},{30,22},{1,9},{... | collective-permute-start | bytes 663560 | tf_op jit(solution)/shard_map/ppermute | solution.py:323
  167.6 12.3 %collective-permute-start.41 = (f32[48,1152]{1,0:T(8,128)S(1)}, f32[48,1152]{1,0:T(8,128)}, u32[]{:S(2)}, u32[]{:S(2)}) collective-permute-start(f32[48,1152]{1,0:T(8,128)S(1)} %sum.42), channel_id=1, source_target_pairs={{8,16},{10,18},{12,20},{14,22},{16,8},{18,10},{20,12},{22,14},{9,1... | collective-permute-start | bytes 663560 | tf_op jit(solution)/shard_map/ppermute | solution.py:323
  169.7 13.6 %collective-permute-start.43 = (f32[48,1152]{1,0:T(8,128)S(1)}, f32[48,1152]{1,0:T(8,128)S(1)}, u32[]{:S(2)}, u32[]{:S(2)}) collective-permute-start(f32[48,1152]{1,0:T(8,128)S(1)} %sum.44), channel_id=1, source_target_pairs={{0,8},{2,10},{4,12},{6,14},{8,0},{10,2},{12,4},{14,6},{16,24},{18,... | collective-permute-start | bytes 663560 | tf_op jit(solution)/shard_map/ppermute | solution.py:323
  (59 other events, 423.2 us)

commit v2 on v0

v2 whole, which is shorter than its diff:
```python
from functools import partial

import jax
import jax.numpy as jnp
from jax import lax
from jax.experimental import pallas as pl
from jax.experimental.pallas import tpu as pltpu
from jax.sharding import PartitionSpec as P

HEAD_DIM = 64
PAIR = 2 * HEAD_DIM
EPS = 1e-06
NEGATIVE = -1e30
LOW = jnp.bfloat16
HIGH = jnp.float32
VMEM = pl.BlockSpec(memory_space=pltpu.VMEM)
SMALL = 16
GAIN_ATTN, SHIFT_ATTN, BIAS_Q, BIAS_V, BIAS_OUT, GAIN_MLP, SHIFT_MLP, BIAS_DOWN, BIAS_UP = range(9)


def plain_dot(left, right):
    return jnp.dot(left, right, preferred_element_type=HIGH)


def right_trans(left, right):
    return lax.dot_general(left, right, (((1,), (1,)), ((), ())), preferred_element_type=HIGH)


def left_trans(left, right):
    return lax.dot_general(left, right, (((0,), (0,)), ((), ())), preferred_element_type=HIGH)


def unit_rows(values):
    mean = jnp.mean(values, axis=-1, keepdims=True)
    centred = values - mean
    scale = lax.rsqrt(jnp.mean(centred * centred, axis=-1, keepdims=True) + EPS)
    return centred * scale, scale


def norm_back(grad_unit, unit, scale):
    inner = jnp.mean(grad_unit * unit, axis=-1, keepdims=True)
    return scale * (grad_unit - jnp.mean(grad_unit, axis=-1, keepdims=True) - unit * inner)


def half_masks():
    lane = lax.broadcasted_iota(jnp.int32, (1, PAIR), 1)
    first = lane < HEAD_DIM
    return first, (first.astype(HIGH).astype(LOW), (~first).astype(HIGH).astype(LOW))


def col_sum(values):
    return jnp.sum(values, axis=0, keepdims=True)


def row(table, at, size):
    return table[at : at + 1, :size]


def same_crop(table, slot, length):
    ids = row(table, slot, length)
    marks = lax.broadcasted_iota(jnp.int32, (SMALL, length), 0).astype(HIGH) == ids
    marks = marks.astype(HIGH).astype(LOW)
    return left_trans(marks, marks) > 0.5


def copies_of(sources, targets, sems):
    copies = [pltpu.make_async_copy(a, b, sems.at[i]) for i, (a, b) in enumerate(zip(sources, targets))]
    for copy in copies:
        copy.start()
    return copies


def load_kernel(here, w_out, crops, *refs):
    count = (len(refs) - 5) // 2
    vectors, (piece, table), sems = refs[:count], refs[count : count + 2], refs[-1]
    held = refs[count + 2 : -1]
    size = piece.shape[0]
    start = pl.multiple_of((here[0] & 3) * size, size)
    sources = [w_out.at[pl.ds(start, size), :], crops, *vectors]
    copies = copies_of(sources, held, sems)
    copies[0].wait()
    piece[...] = held[0][...].astype(HIGH)
    for copy in copies[1:]:
        copy.wait()
    table[...] = jnp.zeros_like(table)
    at, width = 0, table.shape[1]
    for vector in held[2:]:
        for low in range(0, vector.shape[0], width):
            part = min(width, vector.shape[0] - low)
            table[at : at + 1, :part] = vector[low : low + part].reshape(1, part)
            at += 1
    seqs, length = held[1].shape
    table[at : at + seqs, :length] = held[1][...].astype(HIGH)


def front_kernel(*refs, length, seqs, crops):
    sources, table, held = refs[:4], refs[4], refs[5:9]
    first_out, q, k, v, lse = refs[9:14]
    outs, sems = refs[14:-1], refs[-1]
    copies = copies_of(sources, held, sems)
    tokens, w_q, w_k, w_v = held
    copies[0].wait()
    unit, _ = unit_rows(tokens[...].astype(HIGH))
    local, width = w_q.shape[1], tokens.shape[1]
    first = (unit * row(table, GAIN_ATTN, width) + row(table, SHIFT_ATTN, width)).astype(LOW)
    first_out[...] = first
    for copy in copies[1:]:
        copy.wait()
    q_all = plain_dot(first, w_q[...]) + row(table, BIAS_Q, local)
    q_all = (q_all.astype(LOW) * 0.125).astype(LOW)
    k_all = plain_dot(first, w_k[...]).astype(LOW)
    v_all = (plain_dot(first, w_v[...]) + row(table, BIAS_V, local)).astype(LOW)
    q[...] = q_all
    k[...] = k_all
    v[...] = v_all
    low_half, masks = half_masks()
    for s, o in enumerate(outs):
        rows = slice(s * length, (s + 1) * length)
        same = same_crop(table, crops + s, length)
        for t in range(local // PAIR):
            at = slice(t * PAIR, (t + 1) * PAIR)
            q_pair, k_pair, v_pair = q_all[rows, at], k_all[rows, at], v_all[rows, at]
            got = []
            for half in range(2):
                scores = jnp.where(same, right_trans(q_pair * masks[half], k_pair), NEGATIVE)
                top = jnp.max(scores, axis=-1, keepdims=True)
                expo = jnp.exp(scores - top)
                total = jnp.sum(expo, axis=-1, keepdims=True)
                probs = (expo * (1.0 / total)).astype(LOW)
                got.append(plain_dot(probs, v_pair))
                h = 2 * t + half
                lse[rows, h : h + 1] = top + jnp.log(total)
            o[:, at] = jnp.where(low_half, got[0], got[1])


def relative_rows(here, width, count, bits):
    size = width // count
    place = lax.broadcasted_iota(jnp.int32, (width, 1), 0)
    block = ((place.astype(HIGH) + 0.5) * (1.0 / size)).astype(jnp.int32)
    mask = jnp.zeros_like(block)
    for p, bit in enumerate(bits):
        mask = mask + (((block >> (len(bits) - 1 - p)) & 1) << bit)
    source = (mask ^ here) * size + (place - block * size)
    marks = lax.broadcasted_iota(jnp.int32, (width, width), 1) == source
    return marks.astype(HIGH).astype(LOW)


def turn_kernel(here, first, *refs, count, orders):
    sources, held = refs[:4], refs[4:8]
    order_b, sums, sems = refs[8], refs[9], refs[-1]
    seqs = (len(refs) - 11) // 3
    a1_a, a1_b, cot_a = (refs[10 + i * seqs : 10 + (i + 1) * seqs] for i in range(3))
    length = first.shape[0] // seqs
    copies = copies_of(sources, held, sems)
    width = first.shape[1]
    order_a = relative_rows(here[0], width, count, orders[0])
    order = relative_rows(here[0], width, count, orders[1])
    order_b[...] = order
    for s in range(seqs):
        part = first[s * length : (s + 1) * length, :]
        a1_a[s][...] = right_trans(order_a, part).astype(LOW)
        a1_b[s][...] = right_trans(order, part).astype(LOW)
    for copy in copies:
        copy.wait()
    cot = held[0][...]
    for s in range(seqs):
        part = cot[s * length : (s + 1) * length, :]
        cot_a[s][...] = right_trans(order_a, part).astype(LOW)
    sums[...] = col_sum(cot.astype(HIGH))


def middle_kernel(*refs, blocks, seq, length):
    here, tokens, o_own, o_other, w_out, table, w_up, w_down, cotangent, order = refs[:10]
    hidden, a2_t, active, g_pre, g_bias, g_second, w_low = refs[-7:]
    rows = slice(seq * length, (seq + 1) * length)
    if seq:
        bias_before, second_before, w_before = refs[10:13]
        g_second[: seq * length, :] = second_before[...]
        w_low[...] = w_before[...]
    else:
        for b, piece in enumerate(refs[10:14]):
            size = piece.shape[0]
            start = pl.multiple_of(((here[0] & 3) ^ b) * size, size)
            w_low[pl.ds(start, size), :] = piece[...].astype(LOW)
    attn = plain_dot(o_own[...].astype(LOW), w_out[...])
    attn = attn + plain_dot(o_other[...].astype(LOW), w_low[...])
    width = tokens.shape[1]
    values = tokens[rows, :].astype(HIGH) + (attn + row(table, BIAS_OUT, width))
    hidden[...] = values
    unit, _ = unit_rows(values)
    second = (unit * row(table, GAIN_MLP, width) + row(table, SHIFT_MLP, width)).astype(LOW)
    cot = cotangent[rows, :]
    size = w_up.shape[1] // blocks
    total = None
    for b in range(blocks):
        at = slice(b * size, (b + 1) * size)
        low = b * size % width
        at_row = BIAS_UP + b * size // width
        bias_up = table[at_row : at_row + 1, low : low + size]
        pre = plain_dot(second, w_up[:, at]) + bias_up
        cdf = 0.5 * (1.0 + lax.erf(pre * 0.7071067811865476))
        active[:, at] = (pre * cdf).astype(LOW)
        slope = cdf + pre * (0.3989422804014327 * jnp.exp(-0.5 * (pre * pre)))
        grad = (right_trans(cot, w_down[at, :]) * slope).astype(LOW)
        g_pre[:, at] = grad
        bias = col_sum(grad.astype(HIGH))
        g_bias[:, at] = bias_before[:, at] + bias if seq else bias
        part = right_trans(grad, w_up[:, at])
        total = part if total is None else total + part
    g_second[rows, :] = total
    a2_t[...] = right_trans(order[...], second).astype(LOW)


def turn_back_kernel(*refs, seqs, length):
    table, cotangent, own, other, order, g_bias, cot_sum = refs[:7]
    hidden = refs[7 : 7 + seqs]
    g_hidden, gh, sums = refs[7 + seqs : 10 + seqs]
    gh_t = refs[10 + seqs :]
    width = cotangent.shape[1]
    totals = [0.0, 0.0, 0.0]
    for s in range(seqs):
        rows = slice(s * length, (s + 1) * length)
        unit, scale = unit_rows(hidden[s][...])
        grad = own[rows, :] + other[rows, :]
        values = norm_back(grad * row(table, GAIN_MLP, width), unit, scale)
        values = cotangent[rows, :].astype(HIGH) + values
        g_hidden[rows, :] = values
        low = values.astype(LOW)
        gh[rows, :] = low
        gh_t[s][...] = right_trans(order[...], low).astype(LOW)
        parts = (col_sum(grad * unit), col_sum(grad), col_sum(values))
        totals = [a + b for a, b in zip(totals, parts)]
    for i, total in enumerate(totals):
        sums[i : i + 1, :] = total
    sums[3:6, :] = jnp.zeros((3, width), HIGH)
    sums[6:7, :] = g_bias[:, :width]
    sums[7:8, :] = g_bias[:, width:]
    sums[8:9, :] = cot_sum[...]
    sums[9:, :] = jnp.zeros_like(sums[9:, :])


def back_kernel(*refs, seqs, length, crops):
    tokens, table, gh, w_out, w_q, w_k, w_v, q, k, v, lse, _ = refs[:12]
    sums, g_first = refs[12:14]
    g_qk, g_val = (refs[14 + i * seqs : 14 + (i + 1) * seqs] for i in range(2))
    width, local = tokens.shape[1], q.shape[1]
    low_half, masks = half_masks()
    full = slice(0, width)
    before = refs[11]
    sums[:3, :] = before[:3, :]
    sums[6:, :] = before[6:, :]

    def put(s, r, at, value):
        sums[r : r + 1, at] = sums[r : r + 1, at] + value if s else value

    for s in range(seqs):
        rows = slice(s * length, (s + 1) * length)
        g_o = right_trans(gh[rows, :], w_out[...]).astype(LOW)
        same = same_crop(table, crops + s, length)
        for t in range(local // PAIR):
            at = slice(t * PAIR, (t + 1) * PAIR)
            q_pair, k_pair, v_pair, o_pair = q[rows, at], k[rows, at], v[rows, at], g_o[:, at]
            got = []
            for half in range(2):
                h = 2 * t + half
                scores = right_trans(q_pair * masks[half], k_pair)
                probs = jnp.exp(jnp.where(same, scores, NEGATIVE) - lse[rows, h : h + 1])
                g_probs = right_trans(o_pair * masks[half], v_pair)
                inner = jnp.sum(g_probs * probs, axis=-1, keepdims=True)
                g_scores = (probs * (g_probs - inner)).astype(LOW)
                got.append(
                    (
                        plain_dot(g_scores, k_pair),
                        left_trans(g_scores, q_pair),
                        left_trans(probs.astype(LOW), o_pair),
                    )
                )
            g_q = (jnp.where(low_half, got[0][0], got[1][0]) * 0.125).astype(LOW)
            g_k = jnp.where(low_half, got[0][1], got[1][1]).astype(LOW)
            g_v = jnp.where(low_half, got[0][2], got[1][2]).astype(LOW)
            beside = slice(local + t * PAIR, local + (t + 1) * PAIR)
            g_qk[s][:, at] = g_q
            g_qk[s][:, beside] = g_k
            g_val[s][:, at] = g_v
            put(s, 5, at, col_sum(g_q.astype(HIGH)))
            put(s, 5, beside, col_sum(g_v.astype(HIGH)))
        part = right_trans(g_qk[s][:, :local], w_q[...])
        part = part + right_trans(g_qk[s][:, local:], w_k[...])
        part = part + right_trans(g_val[s][...], w_v[...])
        g_first[rows, :] = part
        unit_one, _ = unit_rows(tokens[rows, :].astype(HIGH))
        put(s, 3, full, col_sum(part * unit_one))
        put(s, 4, full, col_sum(part))


def base_kernel(table, tokens, g_hidden, own, base, unit_out, scale_out, *, length):
    gain = row(table, GAIN_ATTN, tokens.shape[1])
    for s in range(tokens.shape[0] // length):
        rows = slice(s * length, (s + 1) * length)
        part = own[rows, :]
        unit, scale = unit_rows(tokens[rows, :].astype(HIGH))
        base[rows, :] = g_hidden[rows, :] + norm_back(part * gain, unit, scale)
        unit_out[rows, :] = unit
        scale_out[rows, :] = scale


def last_kernel(table, base, unit, scale, other, g_tokens, *, length):
    gain = row(table, GAIN_ATTN, base.shape[1])
    for s in range(base.shape[0] // length):
        rows = slice(s * length, (s + 1) * length)
        grad = norm_back(other[rows, :] * gain, unit[rows, :], scale[rows, :])
        g_tokens[rows, :] = base[rows, :] + grad


def out_kernel(*refs, seqs, length):
    table, own, other = refs[:3]
    for s in range(seqs):
        rows = slice(s * length, (s + 1) * length)
        total = refs[3 + s][...] + (own[rows, :] + other[rows, :])
        refs[3 + seqs][rows, :] = (total + row(table, BIAS_DOWN, total.shape[1])).astype(LOW)


def mlp_kernel(w_down, *refs):
    length = refs[0].shape[0]
    for s, active in enumerate(refs[:-1]):
        refs[-1][s * length : (s + 1) * length, :] = plain_dot(active[...], w_down[...])


def products(plan, refs, at):
    for lefts, rights, column in plan:
        wide = refs[rights[0]].shape[1]
        step = min(512, wide)
        for n in range(0, wide, step):
            value = None
            for left, right in zip(lefts, rights):
                part = plain_dot(refs[left][at, :], refs[right][:, n : n + step].astype(LOW))
                value = part if value is None else value + part
            yield slice(column + n, column + n + step), value


def far_kernel(*refs, plan, start, pieces, small):
    outs = refs[-pieces:]
    size = start // pieces
    for o, out in enumerate(outs):
        at = slice(start + o * size, start + (o + 1) * size)
        for columns, value in products(plan, refs, at):
            out[:size, columns] = value
    if small:
        outs[0][size:, :] = refs[-pieces - 1][...]


def near_kernel(*refs, plan, pieces, small):
    outs, got = refs[-2:], refs[-2 - pieces - small :]
    half = outs[0].shape[0]
    for o, out in enumerate(outs):
        at = slice(o * half, (o + 1) * half)
        size = 2 * half // pieces
        low = o * half % size
        for columns, value in products(plan, refs, at):
            out[:half, columns] = value + got[o * half // size][low : low + half, columns]
    if small:
        outs[1][half:, :] = got[pieces][...] + got[0][2 * half // pieces :, :]


def step_kernel(*refs, small, joined):
    count = 2 if joined else 1
    keeps, sents, gots = (refs[i * count : (i + 1) * count] for i in range(3))
    outs = refs[3 * count :]
    at = 0
    for i in range(count):
        half = outs[i].shape[0]
        got = gots[i]
        outs[i][...] = keeps[i][:half, :] + got[:half, :]
        outs[count][at : at + half, :] = keeps[i][half:, :] + got[half : 2 * half, :]
        at += half
        if small and not i:
            outs[count][at : at + SMALL, :] = sents[i][2 * half :, :] + got[2 * half :, :]
            at += SMALL


def end_kernel(*refs, wide, small):
    keeps, (sent, got), outs = refs[:2], refs[2:4], refs[4:]
    at = o = 0
    for keep in keeps:
        size, each = keep.shape[0], keep.shape[1] // wide
        for w in range(wide):
            columns = slice(w * each, (w + 1) * each)
            outs[o][...] = keep[:, columns] + got[at : at + size, columns]
            o += 1
        at += size
        if small and at == size:
            total = sent[at : at + SMALL, :] + got[at : at + SMALL, :]
            outs[-2][...] = total
            outs[-1][...] = total[3:5, :]
            at += SMALL


def gain_kernel(small, other, out):
    out[...] = small[...]
    out[3:5, :] = small[3:5, :] + other[...]


class Steps:
    def __init__(self):
        self.last = None

    def __call__(
        self, kernel, name, outs, args, scratch=(), limit=12, smem=0, whole=0, tie=0, alias=None, cost=0
    ):
        args = list(args)
        if self.last is not None:
            args[tie], _ = lax.optimization_barrier((args[tie], self.last))
        result = pl.pallas_call(
            kernel,
            name=name,
            out_shape=[jax.ShapeDtypeStruct(s, d) for s, d in outs],
            in_specs=[pl.BlockSpec(memory_space=pltpu.SMEM)] * smem
            + [pl.BlockSpec(memory_space=pl.ANY) if i in whole else VMEM for i in range(smem, len(args))]
            if whole
            else [pl.BlockSpec(memory_space=pltpu.SMEM)] * smem + [VMEM] * (len(args) - smem),
            out_specs=[VMEM] * len(outs),
            scratch_shapes=list(scratch),
            input_output_aliases=alias or {},
            compiler_params=pltpu.CompilerParams(vmem_limit_bytes=limit << 20),
            cost_estimate=pl.CostEstimate(flops=1000 + cost, bytes_accessed=1000, transcendentals=0),
        )(*args)
        self.last = result[0]
        return result


def send(values, bit, count):
    return lax.ppermute(values, "dp", [(i, i ^ (1 << bit)) for i in range(count)])


def swap(values):
    return lax.ppermute(values, "mp", [(0, 1), (1, 0)])


class Scatter:
    def __init__(self, steps, count, bits, plan, pieces=2, wide=1, small=None):
        self.steps, self.count, self.bits = steps, count, bits
        self.pieces, self.wide, self.small = pieces, wide, small
        self.plan, self.arrays, self.columns = [], [], 0
        for lefts, rights in plan:
            at, each = len(self.arrays), len(lefts)
            self.arrays += lefts + rights
            places = list(range(at, at + each)), list(range(at + each, at + 2 * each))
            self.plan.append((*places, self.columns))
            self.columns += rights[0].shape[1]
        self.rows = plan[0][0][0].shape[0] // 2
        self.extra = SMALL if small is not None else 0
        self.at = 1

    def shapes(self, *sizes):
        return [((n, self.columns), HIGH) for n in sizes]

    def far(self):
        size = self.rows // self.pieces
        kernel = partial(
            far_kernel,
            plan=self.plan,
            start=self.rows,
            pieces=self.pieces,
            small=bool(self.extra),
        )
        held = self.arrays + ([self.small] if self.extra else [])
        outs = self.shapes(size + self.extra, *[size] * (self.pieces - 1))
        outs = self.steps(kernel, "far", outs, held)
        self.got = [send(o, self.bits[0], self.count) for o in outs]

    def near(self):
        kernel = partial(
            near_kernel,
            plan=self.plan,
            pieces=self.pieces,
            small=bool(self.extra),
        )
        held = self.arrays + self.got + ([self.small] if self.extra else [])
        self.rows //= 2
        outs = self.shapes(self.rows, self.rows + self.extra)
        self.keep, self.sent = self.steps(kernel, "near", outs, held)
        self.got = send(self.sent, self.bits[1], self.count)

    def step(self):
        self.at += 1
        self.rows //= 2
        outs = self.shapes(self.rows, self.rows + self.extra)
        kernel = partial(step_kernel, small=bool(self.extra), joined=False)
        self.keep, self.sent = self.steps(kernel, "sum", outs, [self.keep, self.sent, self.got])
        self.got = send(self.sent, self.bits[self.at], self.count)


def join(one, two):
    for part in (one, two):
        part.at += 1
        part.rows //= 2
    outs = one.shapes(one.rows) + two.shapes(two.rows) + one.shapes(one.rows + two.rows + one.extra)
    kernel = partial(step_kernel, small=bool(one.extra), joined=True)
    held = [one.keep, two.keep, one.sent, two.sent, one.got, two.got]
    one.keep, two.keep, sent = one.steps(kernel, "sums", outs, held)
    got = send(sent, one.bits[one.at], one.count)
    while one.at + 1 < len(one.bits):
        one.at += 1
        half = one.rows // 2
        starts = (0, one.rows + one.extra)
        keeps, sents = [], []
        for part, start in zip((one, two), starts):
            total = part.keep + got[start : start + part.rows]
            keeps.append(total[:half])
            sents.append(total[half:])
        if one.extra:
            at = slice(one.rows, one.rows + one.extra)
            sents.insert(1, sent[at] + got[at])
        one.keep, two.keep = keeps
        one.rows = two.rows = half
        sent = jnp.concatenate(sents)
        got = send(sent, one.bits[one.at], one.count)
    return sent, got


def finish(one, two, sent, got):
    outs = []
    for part in (one, two):
        outs += [((part.rows, part.columns // part.wide), HIGH)] * part.wide
    if one.extra:
        outs += [((SMALL, one.columns), HIGH), ((2, one.columns), HIGH)]
    kernel = partial(end_kernel, wide=one.wide, small=bool(one.extra))
    return one.steps(kernel, "end", outs, [one.keep, two.keep, sent, got])


def body(
    tokens,
    crop_ids,
    w_query,
    w_key,
    w_value,
    bias_query,
    bias_value,
    w_out,
    bias_out,
    gain_attn,
    shift_attn,
    gain_mlp,
    shift_mlp,
    w_up,
    bias_up,
    w_down,
    bias_down,
    cotangent,
    count,
):
    width = tokens.shape[1]
    local = w_query.shape[1]
    hidden_units = w_up.shape[1]
    seqs, length = crop_ids.shape
    rows = seqs * length
    here = lax.axis_index("dp")
    scalar = here.reshape(1)
    bits = list(range(count.bit_length() - 1))
    orders = (bits, [0, 2, 1] + bits[3:])
    steps = Steps()
    piece = local // 4
    lines = [gain_attn, shift_attn, bias_query, bias_value, bias_out, gain_mlp, shift_mlp]
    lines += [bias_down, bias_up]
    crops = BIAS_UP + hidden_units // width
    held = [((piece, width), LOW), (crop_ids.shape, jnp.int32)] + [(v.shape, HIGH) for v in lines]
    mine, table = steps(
        load_kernel,
        "load",
        [((piece, width), HIGH), ((crops + seqs, width), HIGH)],
        [scalar, w_out, crop_ids] + lines,
        scratch=[pltpu.VMEM(*h) for h in held] + [pltpu.SemaphoreType.DMA((len(held),))],
        smem=1,
        whole=range(1, 3 + len(lines)),
        limit=63,
    )
    got = swap(mine)

    def like(*arrays):
        return [(a.shape, a.dtype) for a in arrays]

    front = steps(
        partial(front_kernel, length=length, seqs=seqs, crops=crops),
        "front",
        like(tokens, w_query, w_key, w_value)
        + [((rows, width), LOW)]
        + [((rows, local), LOW)] * 3
        + [((rows, 128), HIGH)]
        + [((length, local), HIGH)] * seqs,
        [tokens, w_query, w_key, w_value, table],
        scratch=[pltpu.SemaphoreType.DMA((4,))],
        whole=range(4),
        limit=58,
    )
    tokens, w_query, w_key, w_value, first, query, key_rows, value_rows, log_total = front[:9]
    mixed = list(front[9:])
    mixed_other = [swap(o) for o in mixed]

    got, _ = lax.optimization_barrier((got, first))
    beside = send(got, 1, count)
    pieces = [got, send(got, 0, count), beside, send(beside, 0, count)]
    turned = steps(
        partial(turn_kernel, count=count, orders=orders),
        "turn",
        like(cotangent, w_up, w_down, w_out)
        + [((width, width), LOW), ((1, width), HIGH)]
        + [((width, length), LOW)] * (3 * seqs),
        [scalar, first, cotangent, w_up, w_down, w_out],
        scratch=[pltpu.SemaphoreType.DMA((4,))],
        whole=range(2, 6),
        smem=1,
        tie=1,
        limit=44,
    )

    cotangent, w_up, w_down, w_out, order_b, cot_sum = turned[:6]
    a1_a, a1_b, cot_a = (list(turned[6 + i * seqs : 6 + (i + 1) * seqs]) for i in range(3))
    hidden, a2_b, active, g_pre, carried = [], [], [], [], []
    for s in range(seqs):
        result = steps(
            partial(middle_kernel, blocks=4, seq=s, length=length),
            "middle",
            [
                ((length, width), HIGH),
                ((width, length), LOW),
                ((length, hidden_units), LOW),
                ((length, hidden_units), LOW),
                ((1, hidden_units), HIGH),
                (((s + 1) * length, width), HIGH),
                ((local, width), LOW),
            ],
            [
                scalar,
                tokens,
                mixed[s],
                mixed_other[s],
                w_out,
                table,
                w_up,
                w_down,
                cotangent,
                order_b,
            ]
            + (carried if s else pieces),
            smem=1,
            tie=2,
        )
        for held, value in zip((hidden, a2_b, active, g_pre), result):
            held.append(value)
        carried = list(result[4:])
    bias_sum, second, _ = carried
    second_other = swap(second)

    down = Scatter(steps, count, orders[0], [(cot_a, active)])
    up = Scatter(steps, count, orders[1], [(a2_b, g_pre)])
    down.far()
    up.far()
    mlp_part = steps(mlp_kernel, "mlp", [((rows, width), HIGH)], [w_down] + active, tie=1)[0]
    mlp_other = swap(mlp_part)
    down.near()
    up.near()
    g_hidden, gh, sums, *gh_b = steps(
        partial(turn_back_kernel, seqs=seqs, length=length),
        "turn_back",
        [((rows, width), HIGH), ((rows, width), LOW), ((SMALL, width), HIGH)]
        + [((width, length), LOW)] * seqs,
        [table, cotangent, second, second_other, order_b, bias_sum, cot_sum] + hidden,
        tie=2,
        cost=9 * 10**9,
    )
    down.step()
    up.step()
    sums, g_first, *result = steps(
        partial(back_kernel, seqs=seqs, length=length, crops=crops),
        "back",
        [((SMALL, width), HIGH), ((rows, width), HIGH)]
        + [((length, 2 * local), LOW)] * seqs
        + [((length, local), LOW)] * seqs,
        [tokens, table, gh, w_out, w_query, w_key, w_value, query, key_rows, value_rows]
        + [log_total, sums],
        tie=2,
    )
    g_qk, g_val = (result[i * seqs : (i + 1) * seqs] for i in range(2))
    first_other = swap(g_first)
    mlp_sent = join(down, up)
    heads = Scatter(steps, count, orders[0], [(a1_a, g_qk)], wide=2, small=sums)
    others = Scatter(steps, count, orders[1], [(a1_b, g_val), (gh_b, mixed)], wide=2)
    heads.far()
    others.far()
    heads.near()
    others.near()
    block_out = steps(
        partial(out_kernel, seqs=seqs, length=length),
        "out",
        [((rows, width), LOW)],
        [table, mlp_part, mlp_other] + hidden,
        tie=1,
    )[0]
    heads.step()
    others.step()
    w_down_t, done_w_up = finish(down, up, *mlp_sent)
    head_sent = join(heads, others)
    base, unit, scale = steps(
        partial(base_kernel, length=length),
        "base",
        [((rows, width), HIGH)] * 2 + [((rows, 1), HIGH)],
        [table, tokens, g_hidden, g_first],
        tie=2,
    )
    grad_w_q, grad_w_k, grad_w_v, w_out_t, total, gains = finish(heads, others, *head_sent)
    gain_other = swap(gains)
    packed = steps(gain_kernel, "gains", [((SMALL, width), HIGH)], [total, gain_other])[0]
    size = width // count
    own = lax.dynamic_slice(packed, (0, here * size), (9, size))
    done = [
        w_out_t.T,
        own[2],
        own[3],
        own[4],
        own[0],
        own[1],
        w_down_t.T,
        own[8],
        packed[5, :local],
        packed[5, local:],
        packed[6:8].reshape(-1),
    ]
    first_other, *done = lax.optimization_barrier((first_other, *done))
    grad_tokens = steps(
        partial(last_kernel, length=length),
        "last",
        [((rows, width), HIGH)],
        [table, base, unit, scale, first_other],
        tie=1,
    )[0]
    return (
        block_out,
        grad_tokens,
        grad_w_q,
        grad_w_k,
        grad_w_v,
        done[8],
        done[9],
        *done[:6],
        done_w_up,
        done[10],
        *done[6:8],
    )


def solution(mesh):
    placed = (
        P("dp", None),
        P("dp", None),
        P(None, "mp"),
        P(None, "mp"),
        P(None, "mp"),
        P("mp"),
        P("mp"),
        P("mp", None),
        P(),
        P(),
        P(),
        P(),
        P(),
        P(None, "mp"),
        P("mp"),
        P("mp", None),
        P(),
        P("dp", None),
    )
    return jax.shard_map(
        partial(body, count=mesh.shape["dp"]),
        mesh=mesh,
        in_specs=placed,
        out_specs=(
            P("dp", None),
            P("dp", None),
            P("dp", "mp"),
            P("dp", "mp"),
            P("dp", "mp"),
            P("mp"),
            P("mp"),
            P("mp", "dp"),
            P("dp"),
            P("dp"),
            P("dp"),
            P("dp"),
            P("dp"),
            P("dp", "mp"),
            P("mp"),
            P("mp", "dp"),
            P("dp"),
        ),
        check_vma=False,
    )
```

time: 668 us -> 163 us (0.24)
  waiting for transfers between devices: 493 us -> 77.7 us
  blocking collectives: 61.4 us -> 0 us
  matrix products: 57.7 us -> 0 us
  Pallas kernels: 0 us -> 44 us
  starting transfers between devices: 0.77 us -> 28.6 us
  other arithmetic: 26.4 us -> 0 us
  between operations: 15.2 us -> 1 us
    reduce_scatter x6 -> x0, waiting for transfers between devices: 334 us -> none  [the longest x1 79.5 us: body(): lax.psum_scatter(grad_w_up, 'dp', scatter_dimension=0, tiled=True)]
    psum x3 -> x0, waiting for transfers between devices: 159 us -> none  [the longest x1 60.5 us: body(): mlp_sum = lax.psum(plain_dot(active, w_down), 'mp')]
    ppermute x0 -> x28, waiting for transfers between devices: none -> 77.7 us  [the longest x7 40.1 us: swap(): return lax.ppermute(values, 'mp', [(0, 1), (1, 0)])]
    psum x1 -> x0, blocking collectives: 61.4 us -> none  [body(): lax.psum((grad_bias_query, grad_bias_value, grad_bias_up), 'dp')]
    dot_general x24 -> x0, matrix products: 57.7 us -> none  [the longest x6 22.8 us: left_trans(): lax.dot_general(left, right, (((0,), (0,)), ((), ())), preferred_element_...]
    pallas_call x0 -> x28, Pallas kernels: none -> 44 us  [__call__(): pl.pallas_call(kernel, name=name, out_shape=[jax.ShapeDtypeStruct(s, d) f...]
    ppermute x0 -> x28, starting transfers between devices: none -> 28.6 us  [the longest x21 17.6 us: send(): return lax.ppermute(values, 'dp', [(i, i ^ 1 << bit) for i in range(count)])]
    reduce_sum x8 -> x0, other arithmetic: 14 us -> none  [the longest x1 3.32 us: body(): grad_gain_mlp = jnp.sum(grad_second * unit_two, axis=0)]
  transfers between devices with their start and end apart: 9 -> 28, of which waited for: 8 -> 15; matrix products, arithmetic and copies ran while one was open for 6% -> 1% of each run, Pallas kernels for 0% -> 22%
where the time goes in v2:
time: 163 us
  waiting for transfers between devices  77.7 us (48%)
  Pallas kernels  44 us (27%)
  starting transfers between devices  28.6 us (18%)
  local copies, waits for them, and re-layouts  11.4 us (7%)
    pallas_call x28, Pallas kernels, __call__(): pl.pallas_call(kernel, name=name, out_shape=[jax.ShapeDtypeStruct(s, d) f...  44 us
    ppermute x7, waiting for transfers between devices, swap(): return lax.ppermute(values, 'mp', [(0, 1), (1, 0)])  40.1 us
    ppermute x21, waiting for transfers between devices, send(): return lax.ppermute(values, 'dp', [(i, i ^ 1 << bit) for i in range(count)])  37.6 us
    ppermute x21, starting transfers between devices, send(): return lax.ppermute(values, 'dp', [(i, i ^ 1 << bit) for i in range(count)])  17.6 us
    ppermute x7, starting transfers between devices, swap(): return lax.ppermute(values, 'mp', [(0, 1), (1, 0)])  11 us
    unnamed x44, local copies, waits for them, and re-layouts  9.58 us
  transfers between devices with their start and end apart: 28, of which 15 were waited for; matrix products, arithmetic and copies ran while one was open for 1% of the time, Pallas kernels for 22%

profile of v2, /device:TPU:0, one launch (start us, length us, event | category | flops | bytes accessed | tf_op | source)
XLA Modules:
  0.0 162.7 jit_solution(4929743456852953705)
XLA Ops:
  0.7 1.8 %load.1 = (f32[96,768]{1,0:T(8,128)}, f32[12,768]{1,0:T(8,128)}) custom-call(s32[1]{0:T(128)} %bitcast.here.refs_0_, bf16[384,768]{1,0:T(8,128)(2,1)} %refs_3_.5, s32[2,256]{1,0:T(2,128)} %crops.1, f32[768]{0:T(1024)} %refs_0_.2, f32[768]{0:T(1024)} %refs_1_.3, f32[384]{0:T(512)} %refs_2_.3, f32[384]{0:T(512)} %refs_3_.3, f32[768]{0:T(1024)} %refs_4_.1, ...), custom_call_target="tpu_custom_call" | custom-call | flops 1000 | bytes 1000 | tf_op jit(solution)/shard_map/load/pallas_call | solution.py:413
  2.4 3.0 %collective-permute-start.1 = (f32[96,768]{1,0:T(8,128)}, f32[96,768]{1,0:T(8,128)S(1)}, u32[]{:S(2)}, u32[]{:S(2)}) collective-permute-start(f32[96,768]{1,0:T(8,128)} %get-tuple-element.148), channel_id=1, source_target_pairs={{0,1},{1,0},{2,3},{3,2},{4,5},{5,4},{6,7},{7,6},{8,9},{9,8},{10,11... | collective-permute-start | bytes 884744 | tf_op jit(solution)/shard_map/ppermute | solution.py:436
  5.4 6.8 %front.1 = (bf16[512,768]{1,0:T(8,128)(2,1)}, bf16[768,384]{1,0:T(8,128)(2,1)}, bf16[768,384]{1,0:T(8,128)(2,1)}, bf16[768,384]{1,0:T(8,128)(2,1)}, bf16[512,768...) custom-call(bf16[512,768]{1,0:T(8,128)(2,1)} %refs_0_.3, ...), custom_call_target="tpu_custom_call" | custom-call | flops 1000 | bytes 1000 | tf_op jit(solution)/shard_map/front/pallas_call | solution.py:413
  12.7 1.8 %collective-permute-start.3 = (f32[96,768]{1,0:T(8,128)S(1)}, f32[96,768]{1,0:T(8,128)S(1)}, u32[]{:S(2)}, u32[]{:S(2)}) collective-permute-start(f32[96,768]{1,0:T(8,128)S(1)} %collective-permute-done.1.refs_10_), channel_id=1, source_target_pairs={{0,4},{2,6},{4,0},{6,2},{8,12},{10,14},{12,8},{14,10},{16,20},{18,... | collective-permute-start | bytes 884744 | tf_op jit(solution)/shard_map/ppermute | solution.py:432
  16.5 4.4 %collective-permute-done.3.refs_12_ = f32[96,768]{1,0:T(8,128)S(1)} collective-permute-done((f32[96,768]{1,0:T(8,128)S(1)}, f32[96,768]{1,0:T(8,128)S(1)}, u32[]{:S(2)}, u32[]{:S(2)}) %collective-permute-start.3) | collective-permute-done | bytes 294944 | tf_op jit(solution)/shard_map/ppermute | solution.py:432
  22.0 4.0 %turn.1 = (bf16[512,768]{1,0:T(8,128)(2,1)S(1)}, bf16[768,1536]{1,0:T(8,128)(2,1)S(1)}, bf16[1536,768]{1,0:T(8,128)(2,1)}, bf16[384,768]{1,0:T(8,128)(2,1)S(1)},...) custom-call(s32[1]{0:T(128)} %bitcast.here.refs_0_, ...), custom_call_target="tpu_custom_call" | custom-call | flops 1000 | bytes 1000 | tf_op jit(solution)/shard_map/turn/pallas_call | solution.py:413
  26.7 1.7 %copy-done = bf16[1536,768]{1,0:T(8,128)(2,1)S(1)} copy-done((bf16[1536,768]{1,0:T(8,128)(2,1)S(1)}, bf16[1536,768]{1,0:T(8,128)(2,1)}, u32[]{:S(2)}) %copy-start) | copy-done | bytes 2359320
  28.4 4.3 %middle.2 = (f32[256,768]{1,0:T(8,128)S(1)}, bf16[768,256]{1,0:T(8,128)(2,1)S(1)}, bf16[256,1536]{1,0:T(8,128)(2,1)S(1)}, bf16[256,1536]{1,0:T(8,128)(2,1)S(1)},...) custom-call(s32[1]{0:T(128)} %bitcast.here.refs_0_, bf16[512,768]{1,0:T(8,128)(2,1)S(1)} %copy-done.2, ...), custom_call_target="tpu_custom_call" | custom-call | flops 1000 | bytes 1000 | tf_op jit(solution)/shard_map/middle/pallas_call | solution.py:413
  32.8 4.5 %middle.3 = (f32[256,768]{1,0:T(8,128)S(1)}, bf16[768,256]{1,0:T(8,128)(2,1)S(1)}, bf16[256,1536]{1,0:T(8,128)(2,1)S(1)}, bf16[256,1536]{1,0:T(8,128)(2,1)S(1)},...) custom-call(s32[1]{0:T(128)} %bitcast.here.refs_0_, bf16[512,768]{1,0:T(8,128)(2,1)S(1)} %copy-done.2, ...), custom_call_target="tpu_custom_call" | custom-call | flops 1000 | bytes 1000 | tf_op jit(solution)/shard_map/middle/pallas_call | solution.py:413
  48.4 1.6 %collective-permute-start.12 = (f32[192,1536]{1,0:T(8,128)S(1)}, f32[192,1536]{1,0:T(8,128)S(1)}, u32[]{:S(2)}, u32[]{:S(2)}) collective-permute-start(f32[192,1536]{1,0:T(8,128)S(1)} %get-tuple-element.199.refs_1_), channel_id=1, source_target_pairs={{0,8},{2,10},{4,12},{6,14},{8,0},{10,2},{12,4},{14,6},{16,24},{18,... | collective-permute-start | bytes 3538952 | tf_op jit(solution)/shard_map/ppermute | solution.py:432
  50.0 23.4 %collective-permute-done.10.refs_3_ = f32[512,768]{1,0:T(8,128)S(1)} collective-permute-done((f32[512,768]{1,0:T(8,128)S(1)}, f32[512,768]{1,0:T(8,128)S(1)}, u32[]{:S(2)}, u32[]{:S(2)}) %collective-permute-start.10) | collective-permute-done | bytes 1572896 | tf_op jit(solution)/shard_map/ppermute | solution.py:436
  73.4 2.0 %turn_back.1 = (f32[512,768]{1,0:T(8,128)S(1)}, bf16[512,768]{1,0:T(8,128)(2,1)S(1)}, f32[16,768]{1,0:T(8,128)S(1)}, bf16[768,256]{1,0:T(8,128)(2,1)S(1)}, bf16[768,256]{1,0:T(8,128)(2,1)S(1)}) custom-call(f32[12,768]{1,0:T(8,128)S(1)} %copy-done.5, bf16[512,768]{1,0:T(8,128)(2,1)S(1)} %get-tuple-element.155.refs_8_.refs_1_, ...), custom_call_target="tpu_custom_call" | custom-call | flops 9000000512 | bytes 1000 | tf_op jit(solution)/shard_map/turn_back/pallas_call | solution.py:413
  80.4 7.4 %back.1 = (f32[16,768]{1,0:T(8,128)S(1)}, f32[512,768]{1,0:T(8,128)S(1)}, bf16[256,768]{1,0:T(8,128)(2,1)S(1)}, bf16[256,768]{1,0:T(8,128)(2,1)S(1)}, bf16[256,3...) custom-call(bf16[512,768]{1,0:T(8,128)(2,1)S(1)} %copy-done.2, f32[12,768]{1,0:T(8,128)S(1)} %copy-done.5, ...), custom_call_target="tpu_custom_call" | custom-call | flops 1000 | bytes 1000 | tf_op jit(solution)/shard_map/back/pallas_call | solution.py:413
  87.9 3.3 %collective-permute-done.14.refs_5_ = f32[96,1536]{1,0:T(8,128)S(1)} collective-permute-done((f32[96,1536]{1,0:T(8,128)S(1)}, f32[96,1536]{1,0:T(8,128)S(1)}, u32[]{:S(2)}, u32[]{:S(2)}) %collective-permute-start.14) | collective-permute-done | bytes 589856 | tf_op jit(solution)/shard_map/ppermute | solution.py:432
  100.2 2.6 %collective-permute-start.22 = (f32[96,1536]{1,0:T(8,128)S(1)}, f32[96,1536]{1,0:T(8,128)S(1)}, u32[]{:S(2)}, u32[]{:S(2)}) collective-permute-start(f32[96,1536]{1,0:T(8,128)S(1)} %get-tuple-element.242.refs_2_), channel_id=1, source_target_pairs={{0,16},{2,18},{4,20},{6,22},{8,24},{10,26},{12,28},{14,30},{16,0},... | collective-permute-start | bytes 1769480 | tf_op jit(solution)/shard_map/ppermute | solution.py:432
  102.8 13.5 %collective-permute-done.19.refs_2_ = f32[512,768]{1,0:T(8,128)S(1)} collective-permute-done((f32[512,768]{1,0:T(8,128)S(1)}, f32[512,768]{1,0:T(8,128)S(1)}, u32[]{:S(2)}, u32[]{:S(2)}) %collective-permute-start.19) | collective-permute-done | bytes 1572896 | tf_op jit(solution)/shard_map/ppermute | solution.py:436
  118.1 9.5 %collective-permute-done.21.refs_2_ = f32[192,768]{1,0:T(8,128)S(1)} collective-permute-done((f32[192,768]{1,0:T(8,128)S(1)}, f32[192,768]{1,0:T(8,128)S(1)}, u32[]{:S(2)}, u32[]{:S(2)}) %collective-permute-start.21) | collective-permute-done | bytes 589856 | tf_op jit(solution)/shard_map/ppermute | solution.py:432
  127.7 1.7 %collective-permute-start.24 = (f32[96,768]{1,0:T(8,128)S(1)}, f32[96,768]{1,0:T(8,128)S(1)}, u32[]{:S(2)}, u32[]{:S(2)}) collective-permute-start(f32[96,768]{1,0:T(8,128)S(1)} %get-tuple-element.246.refs_3_), channel_id=1, source_target_pairs={{0,4},{2,6},{4,0},{6,2},{8,12},{10,14},{12,8},{14,10},{16,20},{18,... | collective-permute-start | bytes 884744 | tf_op jit(solution)/shard_map/ppermute | solution.py:432
  130.3 4.2 %collective-permute-done.24.refs_5_ = f32[96,768]{1,0:T(8,128)S(1)} collective-permute-done((f32[96,768]{1,0:T(8,128)S(1)}, f32[96,768]{1,0:T(8,128)S(1)}, u32[]{:S(2)}, u32[]{:S(2)}) %collective-permute-start.24) | collective-permute-done | bytes 294944 | tf_op jit(solution)/shard_map/ppermute | solution.py:432
  134.5 1.7 %collective-permute-start.25 = (f32[112,768]{1,0:T(8,128)S(1)}, f32[112,768]{1,0:T(8,128)S(1)}, u32[]{:S(2)}, u32[]{:S(2)}) collective-permute-start(f32[112,768]{1,0:T(8,128)S(1)} %get-tuple-element.253.refs_2_), channel_id=1, source_target_pairs={{0,16},{2,18},{4,20},{6,22},{8,24},{10,26},{12,28},{14,30},{16,0},... | collective-permute-start | bytes 1032200 | tf_op jit(solution)/shard_map/ppermute | solution.py:432
  139.7 10.8 %collective-permute-done.25.refs_3_ = f32[112,768]{1,0:T(8,128)S(1)} collective-permute-done((f32[112,768]{1,0:T(8,128)S(1)}, f32[112,768]{1,0:T(8,128)S(1)}, u32[]{:S(2)}, u32[]{:S(2)}) %collective-permute-start.25) | collective-permute-done | bytes 344096 | tf_op jit(solution)/shard_map/ppermute | solution.py:432
  151.3 1.6 %collective-permute-start.26 = (f32[2,768]{1,0:T(2,128)S(1)}, f32[2,768]{1,0:T(2,128)S(1)}, u32[]{:S(2)}, u32[]{:S(2)}) collective-permute-start(f32[2,768]{1,0:T(2,128)S(1)} %get-tuple-element.257), channel_id=1, source_target_pairs={{0,1},{1,0},{2,3},{3,2},{4,5},{5,4},{6,7},{7,6},{8,9},{9,8},{10,11... | collective-permute-start | bytes 18440 | tf_op jit(solution)/shard_map/ppermute | solution.py:436
  152.9 2.0 %collective-permute-done.26.other = f32[2,768]{1,0:T(2,128)S(1)} collective-permute-done((f32[2,768]{1,0:T(2,128)S(1)}, f32[2,768]{1,0:T(2,128)S(1)}, u32[]{:S(2)}, u32[]{:S(2)}) %collective-permute-start.26) | collective-permute-done | bytes 6176 | tf_op jit(solution)/shard_map/ppermute | solution.py:436
  160.9 1.9 %last.1 = f32[512,768]{1,0:T(8,128)} custom-call(f32[12,768]{1,0:T(8,128)S(1)} %copy-done.5, f32[512,768]{1,0:T(8,128)S(1)} %copy-done.8, f32[512,768]{1,0:T(8,128)S(1)} %copy-done.10, f32[512,1]{1,0:T(8,128)S(1)} %get-tuple-element.260.scale, f32[512,768]{1,0:T(8,128)S(1)} %collective-permute-done.27.other), custom_call_target="tpu_custom_call" | custom-call | flops 1000 | bytes 1000 | tf_op jit(solution)/shard_map/last/pallas_call | solution.py:413
  (108 shorter events, 42.2 us)
Async XLA Ops:
  2.4 10.2 %collective-permute-start.1 = (f32[96,768]{1,0:T(8,128)}, f32[96,768]{1,0:T(8,128)S(1)}, u32[]{:S(2)}, u32[]{:S(2)}) collective-permute-start(f32[96,768]{1,0:T(8,128)} %get-tuple-element.148), channel_id=1, source_target_pairs={{0,1},{1,0},{2,3},{3,2},{4,5},{5,4},{6,7},{7,6},{8,9},{9,8},{10,11... | collective-permute-start | bytes 884744 | tf_op jit(solution)/shard_map/ppermute | solution.py:436
  12.7 8.2 %collective-permute-start.3 = (f32[96,768]{1,0:T(8,128)S(1)}, f32[96,768]{1,0:T(8,128)S(1)}, u32[]{:S(2)}, u32[]{:S(2)}) collective-permute-start(f32[96,768]{1,0:T(8,128)S(1)} %collective-permute-done.1.refs_10_), channel_id=1, source_target_pairs={{0,4},{2,6},{4,0},{6,2},{8,12},{10,14},{12,8},{14,10},{16,20},{18,... | collective-permute-start | bytes 884744 | tf_op jit(solution)/shard_map/ppermute | solution.py:432
  14.4 12.3 %collective-permute-start = (f32[256,384]{1,0:T(8,128)}, f32[256,384]{1,0:T(8,128)S(1)}, u32[]{:S(2)}, u32[]{:S(2)}) collective-permute-start(f32[256,384]{1,0:T(8,128)} %get-tuple-element.156.refs_2_.refs_6_), channel_id=1, source_target_pairs={{0,1},{1,0},{2,3},{3,2},{4,5},{5,4},{6,7},{7,6},{8,9},{9,8},{10,11... | collective-permute-start | bytes 1179656 | tf_op jit(solution)/shard_map/ppermute | solution.py:436
  15.9 16.8 %collective-permute-start.5 = (f32[256,384]{1,0:T(8,128)}, f32[256,384]{1,0:T(8,128)S(1)}, u32[]{:S(2)}, u32[]{:S(2)}) collective-permute-start(f32[256,384]{1,0:T(8,128)} %get-tuple-element.166.refs_2_.refs_7_), channel_id=1, source_target_pairs={{0,1},{1,0},{2,3},{3,2},{4,5},{5,4},{6,7},{7,6},{8,9},{9,8},{10,11... | collective-permute-start | bytes 1179656 | tf_op jit(solution)/shard_map/ppermute | solution.py:436
  16.5 10.2 %collective-permute-start.2 = (f32[96,768]{1,0:T(8,128)S(1)}, f32[96,768]{1,0:T(8,128)S(1)}, u32[]{:S(2)}, u32[]{:S(2)}) collective-permute-start(f32[96,768]{1,0:T(8,128)S(1)} %collective-permute-done.1.refs_10_), channel_id=1, source_target_pairs={{0,2},{2,0},{4,6},{6,4},{8,10},{10,8},{12,14},{14,12},{16,18},{18,... | collective-permute-start | bytes 884744 | tf_op jit(solution)/shard_map/ppermute | solution.py:432
  20.9 5.8 %collective-permute-start.4 = (f32[96,768]{1,0:T(8,128)S(1)}, f32[96,768]{1,0:T(8,128)S(1)}, u32[]{:S(2)}, u32[]{:S(2)}) collective-permute-start(f32[96,768]{1,0:T(8,128)S(1)} %collective-permute-done.3.refs_12_), channel_id=1, source_target_pairs={{0,2},{2,0},{4,6},{6,4},{8,10},{10,8},{12,14},{14,12},{16,18},{18,... | collective-permute-start | bytes 884744 | tf_op jit(solution)/shard_map/ppermute | solution.py:432
  37.3 36.1 %collective-permute-start.10 = (f32[512,768]{1,0:T(8,128)S(1)}, f32[512,768]{1,0:T(8,128)S(1)}, u32[]{:S(2)}, u32[]{:S(2)}) collective-permute-start(f32[512,768]{1,0:T(8,128)S(1)} %get-tuple-element.190.refs_2_), channel_id=1, source_target_pairs={{0,1},{1,0},{2,3},{3,2},{4,5},{5,4},{6,7},{7,6},{8,9},{9,8},{10,11... | collective-permute-start | bytes 4718600 | tf_op jit(solution)/shard_map/ppermute | solution.py:436
  39.7 4.5 %collective-permute-start.7 = (f32[192,1536]{1,0:T(8,128)S(1)}, f32[192,1536]{1,0:T(8,128)S(1)}, u32[]{:S(2)}, u32[]{:S(2)}) collective-permute-start(f32[192,1536]{1,0:T(8,128)S(1)} %get-tuple-element.184), channel_id=1, source_target_pairs={{0,2},{2,0},{4,6},{6,4},{8,10},{10,8},{12,14},{14,12},{16,18},{18,... | collective-permute-start | bytes 3538952 | tf_op jit(solution)/shard_map/ppermute | solution.py:432
  40.9 5.1 %collective-permute-start.8 = (f32[192,1536]{1,0:T(8,128)S(1)}, f32[192,1536]{1,0:T(8,128)S(1)}, u32[]{:S(2)}, u32[]{:S(2)}) collective-permute-start(f32[192,1536]{1,0:T(8,128)S(1)} %get-tuple-element.179), channel_id=1, source_target_pairs={{0,2},{2,0},{4,6},{6,4},{8,10},{10,8},{12,14},{14,12},{16,18},{18,... | collective-permute-start | bytes 3538952 | tf_op jit(solution)/shard_map/ppermute | solution.py:432
  41.1 6.5 %collective-permute-start.9 = (f32[192,1536]{1,0:T(8,128)S(1)}, f32[192,1536]{1,0:T(8,128)S(1)}, u32[]{:S(2)}, u32[]{:S(2)}) collective-permute-start(f32[192,1536]{1,0:T(8,128)S(1)} %get-tuple-element.188), channel_id=1, source_target_pairs={{0,2},{2,0},{4,6},{6,4},{8,10},{10,8},{12,14},{14,12},{16,18},{18,... | collective-permute-start | bytes 3538952 | tf_op jit(solution)/shard_map/ppermute | solution.py:432
  45.2 30.2 %collective-permute-start.11 = (f32[192,1536]{1,0:T(8,128)S(1)}, f32[192,1536]{1,0:T(8,128)S(1)}, u32[]{:S(2)}, u32[]{:S(2)}) collective-permute-start(f32[192,1536]{1,0:T(8,128)S(1)} %get-tuple-element.195.refs_1_), channel_id=1, source_target_pairs={{0,4},{2,6},{4,0},{6,2},{8,12},{10,14},{12,8},{14,10},{16,20},{18,... | collective-permute-start | bytes 3538952 | tf_op jit(solution)/shard_map/ppermute | solution.py:432
  48.4 28.1 %collective-permute-start.12 = (f32[192,1536]{1,0:T(8,128)S(1)}, f32[192,1536]{1,0:T(8,128)S(1)}, u32[]{:S(2)}, u32[]{:S(2)}) collective-permute-start(f32[192,1536]{1,0:T(8,128)S(1)} %get-tuple-element.199.refs_1_), channel_id=1, source_target_pairs={{0,8},{2,10},{4,12},{6,14},{8,0},{10,2},{12,4},{14,6},{16,24},{18,... | collective-permute-start | bytes 3538952 | tf_op jit(solution)/shard_map/ppermute | solution.py:432
  76.6 14.6 %collective-permute-start.14 = (f32[96,1536]{1,0:T(8,128)S(1)}, f32[96,1536]{1,0:T(8,128)S(1)}, u32[]{:S(2)}, u32[]{:S(2)}) collective-permute-start(f32[96,1536]{1,0:T(8,128)S(1)} %get-tuple-element.213.refs_3_), channel_id=1, source_target_pairs={{0,4},{2,6},{4,0},{6,2},{8,12},{10,14},{12,8},{14,10},{16,20},{18,... | collective-permute-start | bytes 1769480 | tf_op jit(solution)/shard_map/ppermute | solution.py:432
  77.5 14.5 %collective-permute-start.13 = (f32[96,1536]{1,0:T(8,128)S(1)}, f32[96,1536]{1,0:T(8,128)S(1)}, u32[]{:S(2)}, u32[]{:S(2)}) collective-permute-start(f32[96,1536]{1,0:T(8,128)S(1)} %get-tuple-element.212.refs_2_), channel_id=1, source_target_pairs={{0,8},{2,10},{4,12},{6,14},{8,0},{10,2},{12,4},{14,6},{16,24},{18,... | collective-permute-start | bytes 1769480 | tf_op jit(solution)/shard_map/ppermute | solution.py:432
  79.0 37.3 %collective-permute-start.19 = (f32[512,768]{1,0:T(8,128)S(1)}, f32[512,768]{1,0:T(8,128)S(1)}, u32[]{:S(2)}, u32[]{:S(2)}) collective-permute-start(f32[512,768]{1,0:T(8,128)S(1)} %mlp.1.refs_1_), channel_id=1, source_target_pairs={{0,1},{1,0},{2,3},{3,2},{4,5},{5,4},{6,7},{7,6},{8,9},{9,8},{10,11... | collective-permute-start | bytes 4718600 | tf_op jit(solution)/shard_map/ppermute | solution.py:436
  92.6 4.5 %collective-permute-start.15 = (f32[208,768]{1,0:T(8,128)S(1)}, f32[208,768]{1,0:T(8,128)S(1)}, u32[]{:S(2)}, u32[]{:S(2)}) collective-permute-start(f32[208,768]{1,0:T(8,128)S(1)} %get-tuple-element.219), channel_id=1, source_target_pairs={{0,2},{2,0},{4,6},{6,4},{8,10},{10,8},{12,14},{14,12},{16,18},{18,... | collective-permute-start | bytes 1916936 | tf_op jit(solution)/shard_map/ppermute | solution.py:432
  93.8 4.3 %collective-permute-start.17 = (f32[192,768]{1,0:T(8,128)S(1)}, f32[192,768]{1,0:T(8,128)S(1)}, u32[]{:S(2)}, u32[]{:S(2)}) collective-permute-start(f32[192,768]{1,0:T(8,128)S(1)} %get-tuple-element.226), channel_id=1, source_target_pairs={{0,2},{2,0},{4,6},{6,4},{8,10},{10,8},{12,14},{14,12},{16,18},{18,... | collective-permute-start | bytes 1769480 | tf_op jit(solution)/shard_map/ppermute | solution.py:432
  95.6 62.4 %collective-permute-start.27 = (f32[512,768]{1,0:T(8,128)S(1)}, f32[512,768]{1,0:T(8,128)S(1)}, u32[]{:S(2)}, u32[]{:S(2)}) collective-permute-start(f32[512,768]{1,0:T(8,128)S(1)} %get-tuple-element.249.own), channel_id=1, source_target_pairs={{0,1},{1,0},{2,3},{3,2},{4,5},{5,4},{6,7},{7,6},{8,9},{9,8},{10,11... | collective-permute-start | bytes 4718600 | tf_op jit(solution)/shard_map/ppermute | solution.py:436
  97.6 19.9 %collective-permute-start.20 = (f32[208,768]{1,0:T(8,128)S(1)}, f32[208,768]{1,0:T(8,128)S(1)}, u32[]{:S(2)}, u32[]{:S(2)}) collective-permute-start(f32[208,768]{1,0:T(8,128)S(1)} %get-tuple-element.235.refs_1_), channel_id=1, source_target_pairs={{0,4},{2,6},{4,0},{6,2},{8,12},{10,14},{12,8},{14,10},{16,20},{18,... | collective-permute-start | bytes 1916936 | tf_op jit(solution)/shard_map/ppermute | solution.py:432
  98.6 29.0 %collective-permute-start.21 = (f32[192,768]{1,0:T(8,128)S(1)}, f32[192,768]{1,0:T(8,128)S(1)}, u32[]{:S(2)}, u32[]{:S(2)}) collective-permute-start(f32[192,768]{1,0:T(8,128)S(1)} %get-tuple-element.238.refs_1_), channel_id=1, source_target_pairs={{0,8},{2,10},{4,12},{6,14},{8,0},{10,2},{12,4},{14,6},{16,24},{18,... | collective-permute-start | bytes 1769480 | tf_op jit(solution)/shard_map/ppermute | solution.py:432
  100.2 29.2 %collective-permute-start.22 = (f32[96,1536]{1,0:T(8,128)S(1)}, f32[96,1536]{1,0:T(8,128)S(1)}, u32[]{:S(2)}, u32[]{:S(2)}) collective-permute-start(f32[96,1536]{1,0:T(8,128)S(1)} %get-tuple-element.242.refs_2_), channel_id=1, source_target_pairs={{0,16},{2,18},{4,20},{6,22},{8,24},{10,26},{12,28},{14,30},{16,0},... | collective-permute-start | bytes 1769480 | tf_op jit(solution)/shard_map/ppermute | solution.py:432
  117.6 16.9 %collective-permute-start.23 = (f32[112,768]{1,0:T(8,128)S(1)}, f32[112,768]{1,0:T(8,128)S(1)}, u32[]{:S(2)}, u32[]{:S(2)}) collective-permute-start(f32[112,768]{1,0:T(8,128)S(1)} %get-tuple-element.245.refs_2_), channel_id=1, source_target_pairs={{0,8},{2,10},{4,12},{6,14},{8,0},{10,2},{12,4},{14,6},{16,24},{18,... | collective-permute-start | bytes 1032200 | tf_op jit(solution)/shard_map/ppermute | solution.py:432
  127.7 6.8 %collective-permute-start.24 = (f32[96,768]{1,0:T(8,128)S(1)}, f32[96,768]{1,0:T(8,128)S(1)}, u32[]{:S(2)}, u32[]{:S(2)}) collective-permute-start(f32[96,768]{1,0:T(8,128)S(1)} %get-tuple-element.246.refs_3_), channel_id=1, source_target_pairs={{0,4},{2,6},{4,0},{6,2},{8,12},{10,14},{12,8},{14,10},{16,20},{18,... | collective-permute-start | bytes 884744 | tf_op jit(solution)/shard_map/ppermute | solution.py:432
  134.5 16.0 %collective-permute-start.25 = (f32[112,768]{1,0:T(8,128)S(1)}, f32[112,768]{1,0:T(8,128)S(1)}, u32[]{:S(2)}, u32[]{:S(2)}) collective-permute-start(f32[112,768]{1,0:T(8,128)S(1)} %get-tuple-element.253.refs_2_), channel_id=1, source_target_pairs={{0,16},{2,18},{4,20},{6,22},{8,24},{10,26},{12,28},{14,30},{16,0},... | collective-permute-start | bytes 1032200 | tf_op jit(solution)/shard_map/ppermute | solution.py:432
  (26 other events, 108.0 us)

commit v3 on v2

--- a/solution.py
+++ b/solution.py
@@ -378,8 +378,8 @@
             at += SMALL
 
 
-def end_kernel(*refs, wide, small):
-    keeps, (sent, got), outs = refs[:2], refs[2:4], refs[4:]
+def end_kernel(*refs, wide):
+    keeps, got, outs = refs[:2], refs[2], refs[3:]
     at = o = 0
     for keep in keeps:
         size, each = keep.shape[0], keep.shape[1] // wide
@@ -388,16 +388,32 @@
             outs[o][...] = keep[:, columns] + got[at : at + size, columns]
             o += 1
         at += size
-        if small and at == size:
-            total = sent[at : at + SMALL, :] + got[at : at + SMALL, :]
-            outs[-2][...] = total
-            outs[-1][...] = total[3:5, :]
-            at += SMALL
-
-
-def gain_kernel(small, other, out):
-    out[...] = small[...]
-    out[3:5, :] = small[3:5, :] + other[...]
+
+
+def final_kernel(here, one, two, sent, got, *outs):
+    size = one.shape[0]
+    each = one.shape[1] // 2
+    for o, (keep, at) in enumerate(((one, 0), (two, size + SMALL))):
+        for w in range(2):
+            columns = slice(w * each, (w + 1) * each)
+            outs[2 * o + w][...] = keep[:, columns] + got[at : at + size, columns]
+    total = sent[size : size + SMALL, :] + got[size : size + SMALL, :]
+    bias_q, bias_v, bias_up, gain_mlp, shift_mlp, bias_out, bias_down, gains = outs[4:]
+    width = total.shape[1]
+    bias_q[...] = total[5, :each]
+    bias_v[...] = total[5, each:]
+    for i in range(bias_up.shape[0] // width):
+        bias_up[i * width : (i + 1) * width] = total[6 + i, :]
+    turned = pltpu.roll(total, lax.rem(width - here[0] * size, width), 1)
+    for out, at in ((gain_mlp, 0), (shift_mlp, 1), (bias_out, 2), (bias_down, 8)):
+        out[...] = turned[at, :size]
+    gains[...] = turned[:8, : gains.shape[1]]
+
+
+def gain_kernel(own, other, gain, shift):
+    total = own[...] + other[...]
+    gain[...] = total[3, : gain.shape[0]]
+    shift[...] = total[4, : shift.shape[0]]
 
 
 class Steps:
@@ -518,14 +534,12 @@
     return sent, got
 
 
-def finish(one, two, sent, got):
+def finish(one, two, got, cost=0):
     outs = []
     for part in (one, two):
         outs += [((part.rows, part.columns // part.wide), HIGH)] * part.wide
-    if one.extra:
-        outs += [((SMALL, one.columns), HIGH), ((2, one.columns), HIGH)]
-    kernel = partial(end_kernel, wide=one.wide, small=bool(one.extra))
-    return one.steps(kernel, "end", outs, [one.keep, two.keep, sent, got])
+    kernel = partial(end_kernel, wide=one.wide)
+    return one.steps(kernel, "end", outs, [one.keep, two.keep, got], cost=cost)
 
 
 def body(
@@ -682,11 +696,11 @@
     )
     g_qk, g_val = (result[i * seqs : (i + 1) * seqs] for i in range(2))
     first_other = swap(g_first)
-    mlp_sent = join(down, up)
     heads = Scatter(steps, count, orders[0], [(a1_a, g_qk)], wide=2, small=sums)
     others = Scatter(steps, count, orders[1], [(a1_b, g_val), (gh_b, mixed)], wide=2)
     heads.far()
     others.far()
+    _, mlp_got = join(down, up)
     heads.near()
     others.near()
     block_out = steps(
@@ -696,10 +710,10 @@
         [table, mlp_part, mlp_other] + hidden,
         tie=1,
     )[0]
+    w_down_t, done_w_up = finish(down, up, mlp_got, cost=15 * 10**8)
     heads.step()
     others.step()
-    w_down_t, done_w_up = finish(down, up, *mlp_sent)
-    head_sent = join(heads, others)
+    sent, got = join(heads, others)
     base, unit, scale = steps(
         partial(base_kernel, length=length),
         "base",
@@ -707,25 +721,6 @@
         [table, tokens, g_hidden, g_first],
         tie=2,
     )
-    grad_w_q, grad_w_k, grad_w_v, w_out_t, total, gains = finish(heads, others, *head_sent)
-    gain_other = swap(gains)
-    packed = steps(gain_kernel, "gains", [((SMALL, width), HIGH)], [total, gain_other])[0]
-    size = width // count
-    own = lax.dynamic_slice(packed, (0, here * size), (9, size))
-    done = [
-        w_out_t.T,
-        own[2],
-        own[3],
-        own[4],
-        own[0],
-        own[1],
-        w_down_t.T,
-        own[8],
-        packed[5, :local],
-        packed[5, local:],
-        packed[6:8].reshape(-1),
-    ]
-    first_other, *done = lax.optimization_barrier((first_other, *done))
     grad_tokens = steps(
         partial(last_kernel, length=length),
         "last",
@@ -733,18 +728,53 @@
         [table, base, unit, scale, first_other],
         tie=1,
     )[0]
+    size = width // count
+    (
+        grad_w_q,
+        grad_w_k,
+        grad_w_v,
+        w_out_t,
+        done_bias_q,
+        done_bias_v,
+        done_bias_up,
+        done_gain_mlp,
+        done_shift_mlp,
+        done_bias_out,
+        done_bias_down,
+        gains,
+    ) = steps(
+        final_kernel,
+        "final",
+        [((size, local), HIGH)] * 4
+        + [((local,), HIGH)] * 2
+        + [((hidden_units,), HIGH)]
+        + [((size,), HIGH)] * 4
+        + [((8, 128), HIGH)],
+        [scalar, heads.keep, others.keep, sent, got],
+        smem=1,
+        tie=1,
+    )
+    done_gain_attn, done_shift_attn = steps(
+        gain_kernel, "gains", [((size,), HIGH)] * 2, [gains, swap(gains)]
+    )
     return (
         block_out,
         grad_tokens,
         grad_w_q,
         grad_w_k,
         grad_w_v,
-        done[8],
-        done[9],
-        *done[:6],
+        done_bias_q,
+        done_bias_v,
+        w_out_t.T,
+        done_bias_out,
+        done_gain_attn,
+        done_shift_attn,
+        done_gain_mlp,
+        done_shift_mlp,
         done_w_up,
-        done[10],
-        *done[6:8],
+        done_bias_up,
+        w_down_t.T,
+        done_bias_down,
     )
 
 

time: 163 us -> 156 us (0.957)
  local copies, waits for them, and re-layouts: 11.4 us -> 3.15 us
    ppermute x21, waiting for transfers between devices: 37.6 us -> 23.2 us  [send(): return lax.ppermute(values, 'dp', [(i, i ^ 1 << bit) for i in range(count)])]
    ppermute x7, waiting for transfers between devices: 40.1 us -> 54 us  [swap(): return lax.ppermute(values, 'mp', [(0, 1), (1, 0)])]
    unnamed x44 -> x32, local copies, waits for them, and re-layouts: 9.58 us -> 3.15 us
    ppermute x21, starting transfers between devices: 17.6 us -> 20.2 us  [send(): return lax.ppermute(values, 'dp', [(i, i ^ 1 << bit) for i in range(count)])]
  transfers between devices with their start and end apart: 28 -> 28, of which waited for: 15 -> 17; matrix products, arithmetic and copies ran while one was open for 1% -> 0% of each run, Pallas kernels for 22% -> 24%
where the time goes in v3:
time: 156 us
  waiting for transfers between devices  77.2 us (49%)
  Pallas kernels  44.8 us (29%)
  starting transfers between devices  30.1 us (19%)
  local copies, waits for them, and re-layouts  3.15 us (2%)
    ppermute x7, waiting for transfers between devices, swap(): return lax.ppermute(values, 'mp', [(0, 1), (1, 0)])  54 us
    pallas_call x28, Pallas kernels, __call__(): pl.pallas_call(kernel, name=name, out_shape=[jax.ShapeDtypeStruct(s, d) f...  44.8 us
    ppermute x21, waiting for transfers between devices, send(): return lax.ppermute(values, 'dp', [(i, i ^ 1 << bit) for i in range(count)])  23.2 us
    ppermute x21, starting transfers between devices, send(): return lax.ppermute(values, 'dp', [(i, i ^ 1 << bit) for i in range(count)])  20.2 us
    ppermute x7, starting transfers between devices, swap(): return lax.ppermute(values, 'mp', [(0, 1), (1, 0)])  9.94 us
    unnamed x32, local copies, waits for them, and re-layouts  3.15 us
  transfers between devices with their start and end apart: 28, of which 17 were waited for; matrix products, arithmetic and copies ran while one was open for 0% of the time, Pallas kernels for 24%

profile of v3, /device:TPU:0, one launch (start us, length us, event | category | flops | bytes accessed | tf_op | source)
XLA Modules:
  0.0 156.2 jit_solution(5477360080420505263)
XLA Ops:
  0.7 1.8 %load.1 = (f32[96,768]{1,0:T(8,128)}, f32[12,768]{1,0:T(8,128)}) custom-call(s32[1]{0:T(128)} %bitcast.here.refs_0_, bf16[384,768]{1,0:T(8,128)(2,1)} %refs_3_.5, s32[2,256]{1,0:T(2,128)} %crops.1, f32[768]{0:T(1024)} %refs_0_.2, f32[768]{0:T(1024)} %refs_1_.3, f32[384]{0:T(512)} %refs_2_.3, f32[384]{0:T(512)} %refs_3_.3, f32[768]{0:T(1024)} %refs_4_.1, ...), custom_call_target="tpu_custom_call" | custom-call | flops 1000 | bytes 1000 | tf_op jit(solution)/shard_map/load/pallas_call | solution.py:429
  2.4 3.0 %collective-permute-start.1 = (f32[96,768]{1,0:T(8,128)}, f32[96,768]{1,0:T(8,128)S(1)}, u32[]{:S(2)}, u32[]{:S(2)}) collective-permute-start(f32[96,768]{1,0:T(8,128)} %get-tuple-element.143), channel_id=1, source_target_pairs={{0,1},{1,0},{2,3},{3,2},{4,5},{5,4},{6,7},{7,6},{8,9},{9,8},{10,11... | collective-permute-start | bytes 884744 | tf_op jit(solution)/shard_map/ppermute | solution.py:452
  5.4 6.8 %front.1 = (bf16[512,768]{1,0:T(8,128)(2,1)}, bf16[768,384]{1,0:T(8,128)(2,1)}, bf16[768,384]{1,0:T(8,128)(2,1)}, bf16[768,384]{1,0:T(8,128)(2,1)}, bf16[512,768...) custom-call(bf16[512,768]{1,0:T(8,128)(2,1)} %refs_0_.3, ...), custom_call_target="tpu_custom_call" | custom-call | flops 1000 | bytes 1000 | tf_op jit(solution)/shard_map/front/pallas_call | solution.py:429
  12.7 1.8 %collective-permute-start.3 = (f32[96,768]{1,0:T(8,128)S(1)}, f32[96,768]{1,0:T(8,128)S(1)}, u32[]{:S(2)}, u32[]{:S(2)}) collective-permute-start(f32[96,768]{1,0:T(8,128)S(1)} %collective-permute-done.1.refs_10_), channel_id=1, source_target_pairs={{0,4},{2,6},{4,0},{6,2},{8,12},{10,14},{12,8},{14,10},{16,20},{18,... | collective-permute-start | bytes 884744 | tf_op jit(solution)/shard_map/ppermute | solution.py:448
  16.5 4.4 %collective-permute-done.3.refs_12_ = f32[96,768]{1,0:T(8,128)S(1)} collective-permute-done((f32[96,768]{1,0:T(8,128)S(1)}, f32[96,768]{1,0:T(8,128)S(1)}, u32[]{:S(2)}, u32[]{:S(2)}) %collective-permute-start.3) | collective-permute-done | bytes 294944 | tf_op jit(solution)/shard_map/ppermute | solution.py:448
  22.0 4.0 %turn.1 = (bf16[512,768]{1,0:T(8,128)(2,1)S(1)}, bf16[768,1536]{1,0:T(8,128)(2,1)S(1)}, bf16[1536,768]{1,0:T(8,128)(2,1)}, bf16[384,768]{1,0:T(8,128)(2,1)S(1)},...) custom-call(s32[1]{0:T(128)} %bitcast.here.refs_0_, ...), custom_call_target="tpu_custom_call" | custom-call | flops 1000 | bytes 1000 | tf_op jit(solution)/shard_map/turn/pallas_call | solution.py:429
  26.7 1.7 %copy-done = bf16[1536,768]{1,0:T(8,128)(2,1)S(1)} copy-done((bf16[1536,768]{1,0:T(8,128)(2,1)S(1)}, bf16[1536,768]{1,0:T(8,128)(2,1)}, u32[]{:S(2)}) %copy-start) | copy-done | bytes 2359320
  28.4 4.3 %middle.2 = (f32[256,768]{1,0:T(8,128)S(1)}, bf16[768,256]{1,0:T(8,128)(2,1)S(1)}, bf16[256,1536]{1,0:T(8,128)(2,1)S(1)}, bf16[256,1536]{1,0:T(8,128)(2,1)S(1)},...) custom-call(s32[1]{0:T(128)} %bitcast.here.refs_0_, bf16[512,768]{1,0:T(8,128)(2,1)S(1)} %copy-done.2, ...), custom_call_target="tpu_custom_call" | custom-call | flops 1000 | bytes 1000 | tf_op jit(solution)/shard_map/middle/pallas_call | solution.py:429
  32.8 4.5 %middle.3 = (f32[256,768]{1,0:T(8,128)S(1)}, bf16[768,256]{1,0:T(8,128)(2,1)S(1)}, bf16[256,1536]{1,0:T(8,128)(2,1)S(1)}, bf16[256,1536]{1,0:T(8,128)(2,1)S(1)},...) custom-call(s32[1]{0:T(128)} %bitcast.here.refs_0_, bf16[512,768]{1,0:T(8,128)(2,1)S(1)} %copy-done.2, ...), custom_call_target="tpu_custom_call" | custom-call | flops 1000 | bytes 1000 | tf_op jit(solution)/shard_map/middle/pallas_call | solution.py:429
  48.4 1.6 %collective-permute-start.12 = (f32[192,1536]{1,0:T(8,128)S(1)}, f32[192,1536]{1,0:T(8,128)S(1)}, u32[]{:S(2)}, u32[]{:S(2)}) collective-permute-start(f32[192,1536]{1,0:T(8,128)S(1)} %get-tuple-element.194.refs_1_), channel_id=1, source_target_pairs={{0,8},{2,10},{4,12},{6,14},{8,0},{10,2},{12,4},{14,6},{16,24},{18,... | collective-permute-start | bytes 3538952 | tf_op jit(solution)/shard_map/ppermute | solution.py:448
  50.0 23.4 %collective-permute-done.10.refs_3_ = f32[512,768]{1,0:T(8,128)S(1)} collective-permute-done((f32[512,768]{1,0:T(8,128)S(1)}, f32[512,768]{1,0:T(8,128)S(1)}, u32[]{:S(2)}, u32[]{:S(2)}) %collective-permute-start.10) | collective-permute-done | bytes 1572896 | tf_op jit(solution)/shard_map/ppermute | solution.py:452
  73.4 2.0 %turn_back.1 = (f32[512,768]{1,0:T(8,128)S(1)}, bf16[512,768]{1,0:T(8,128)(2,1)S(1)}, f32[16,768]{1,0:T(8,128)S(1)}, bf16[768,256]{1,0:T(8,128)(2,1)S(1)}, bf16[768,256]{1,0:T(8,128)(2,1)S(1)}) custom-call(f32[12,768]{1,0:T(8,128)S(1)} %copy-done.5, bf16[512,768]{1,0:T(8,128)(2,1)S(1)} %get-tuple-element.150.refs_8_.refs_1_, ...), custom_call_target="tpu_custom_call" | custom-call | flops 9000000512 | bytes 1000 | tf_op jit(solution)/shard_map/turn_back/pallas_call | solution.py:429
  80.5 7.5 %back.1 = (f32[16,768]{1,0:T(8,128)S(1)}, f32[512,768]{1,0:T(8,128)S(1)}, bf16[256,768]{1,0:T(8,128)(2,1)S(1)}, bf16[256,768]{1,0:T(8,128)(2,1)S(1)}, bf16[256,3...) custom-call(bf16[512,768]{1,0:T(8,128)(2,1)S(1)} %copy-done.2, f32[12,768]{1,0:T(8,128)S(1)} %copy-done.5, ...), custom_call_target="tpu_custom_call" | custom-call | flops 1000 | bytes 1000 | tf_op jit(solution)/shard_map/back/pallas_call | solution.py:429
  89.6 1.6 %collective-permute-done.14.refs_5_ = f32[96,1536]{1,0:T(8,128)S(1)} collective-permute-done((f32[96,1536]{1,0:T(8,128)S(1)}, f32[96,1536]{1,0:T(8,128)S(1)}, u32[]{:S(2)}, u32[]{:S(2)}) %collective-permute-start.14) | collective-permute-done | bytes 589856 | tf_op jit(solution)/shard_map/ppermute | solution.py:448
  93.7 2.6 %collective-permute-start.20 = (f32[96,1536]{1,0:T(8,128)S(1)}, f32[96,1536]{1,0:T(8,128)S(1)}, u32[]{:S(2)}, u32[]{:S(2)}) collective-permute-start(f32[96,1536]{1,0:T(8,128)S(1)} %get-tuple-element.231), channel_id=1, source_target_pairs={{0,16},{2,18},{4,20},{6,22},{8,24},{10,26},{12,28},{14,30},{16,0},... | collective-permute-start | bytes 1769480 | tf_op jit(solution)/shard_map/ppermute | solution.py:448
  98.3 1.9 %collective-permute-start.22 = (f32[192,768]{1,0:T(8,128)S(1)}, f32[192,768]{1,0:T(8,128)S(1)}, u32[]{:S(2)}, u32[]{:S(2)}) collective-permute-start(f32[192,768]{1,0:T(8,128)S(1)} %get-tuple-element.237.refs_1_), channel_id=1, source_target_pairs={{0,8},{2,10},{4,12},{6,14},{8,0},{10,2},{12,4},{14,6},{16,24},{18,... | collective-permute-start | bytes 1769480 | tf_op jit(solution)/shard_map/ppermute | solution.py:448
  100.2 16.2 %collective-permute-done.19.refs_2_ = f32[512,768]{1,0:T(8,128)S(1)} collective-permute-done((f32[512,768]{1,0:T(8,128)S(1)}, f32[512,768]{1,0:T(8,128)S(1)}, u32[]{:S(2)}, u32[]{:S(2)}) %collective-permute-start.19) | collective-permute-done | bytes 1572896 | tf_op jit(solution)/shard_map/ppermute | solution.py:452
  117.6 5.2 %collective-permute-done.20.refs_2_ = f32[96,1536]{1,0:T(8,128)S(1)} collective-permute-done((f32[96,1536]{1,0:T(8,128)S(1)}, f32[96,1536]{1,0:T(8,128)S(1)}, u32[]{:S(2)}, u32[]{:S(2)}) %collective-permute-start.20) | collective-permute-done | bytes 589856 | tf_op jit(solution)/shard_map/ppermute | solution.py:448
  124.7 2.2 %collective-permute-start.24 = (f32[96,768]{1,0:T(8,128)S(1)}, f32[96,768]{1,0:T(8,128)S(1)}, u32[]{:S(2)}, u32[]{:S(2)}) collective-permute-start(f32[96,768]{1,0:T(8,128)S(1)} %get-tuple-element.241.refs_3_), channel_id=1, source_target_pairs={{0,4},{2,6},{4,0},{6,2},{8,12},{10,14},{12,8},{14,10},{16,20},{18,... | collective-permute-start | bytes 884744 | tf_op jit(solution)/shard_map/ppermute | solution.py:448
  126.9 6.4 %collective-permute-done.24.refs_5_ = f32[96,768]{1,0:T(8,128)S(1)} collective-permute-done((f32[96,768]{1,0:T(8,128)S(1)}, f32[96,768]{1,0:T(8,128)S(1)}, u32[]{:S(2)}, u32[]{:S(2)}) %collective-permute-start.24) | collective-permute-done | bytes 294944 | tf_op jit(solution)/shard_map/ppermute | solution.py:448
  133.3 3.4 %collective-permute-start.26 = (f32[112,768]{1,0:T(8,128)S(1)}, f32[112,768]{1,0:T(8,128)S(1)}, u32[]{:S(2)}, u32[]{:S(2)}) collective-permute-start(f32[112,768]{1,0:T(8,128)S(1)} %get-tuple-element.250.sent), channel_id=1, source_target_pairs={{0,16},{2,18},{4,20},{6,22},{8,24},{10,26},{12,28},{14,30},{16,0},... | collective-permute-start | bytes 1032200 | tf_op jit(solution)/shard_map/ppermute | solution.py:448
  137.9 10.2 %collective-permute-done.25.other = f32[512,768]{1,0:T(8,128)S(1)} collective-permute-done((f32[512,768]{1,0:T(8,128)S(1)}, f32[512,768]{1,0:T(8,128)S(1)}, u32[]{:S(2)}, u32[]{:S(2)}) %collective-permute-start.25) | collective-permute-done | bytes 1572896 | tf_op jit(solution)/shard_map/ppermute | solution.py:452
  148.1 1.9 %last.1 = f32[512,768]{1,0:T(8,128)} custom-call(f32[12,768]{1,0:T(8,128)S(1)} %copy-done.5, f32[512,768]{1,0:T(8,128)S(1)} %get-tuple-element.245.base, f32[512,768]{1,0:T(8,128)S(1)} %get-tuple-element.246.unit, f32[512,1]{1,0:T(8,128)S(1)} %get-tuple-element.247.scale, f32[512,768]{1,0:T(8,128)S(1)} %collective-permute-done.25.other), custom_call_target="tpu_custom_call" | custom-call | flops 1000 | bytes 1000 | tf_op jit(solution)/shard_map/last/pallas_call | solution.py:429
  152.6 3.0 %collective-permute-done.27.other = f32[8,128]{1,0:T(8,128)S(1)} collective-permute-done((f32[8,128]{1,0:T(8,128)S(1)}, f32[8,128]{1,0:T(8,128)S(1)}, u32[]{:S(2)}, u32[]{:S(2)}) %collective-permute-start.27) | collective-permute-done | bytes 4128 | tf_op jit(solution)/shard_map/ppermute | solution.py:452
  (92 shorter events, 33.7 us)
Async XLA Ops:
  2.4 10.2 %collective-permute-start.1 = (f32[96,768]{1,0:T(8,128)}, f32[96,768]{1,0:T(8,128)S(1)}, u32[]{:S(2)}, u32[]{:S(2)}) collective-permute-start(f32[96,768]{1,0:T(8,128)} %get-tuple-element.143), channel_id=1, source_target_pairs={{0,1},{1,0},{2,3},{3,2},{4,5},{5,4},{6,7},{7,6},{8,9},{9,8},{10,11... | collective-permute-start | bytes 884744 | tf_op jit(solution)/shard_map/ppermute | solution.py:452
  12.7 8.2 %collective-permute-start.3 = (f32[96,768]{1,0:T(8,128)S(1)}, f32[96,768]{1,0:T(8,128)S(1)}, u32[]{:S(2)}, u32[]{:S(2)}) collective-permute-start(f32[96,768]{1,0:T(8,128)S(1)} %collective-permute-done.1.refs_10_), channel_id=1, source_target_pairs={{0,4},{2,6},{4,0},{6,2},{8,12},{10,14},{12,8},{14,10},{16,20},{18,... | collective-permute-start | bytes 884744 | tf_op jit(solution)/shard_map/ppermute | solution.py:448
  14.4 12.3 %collective-permute-start = (f32[256,384]{1,0:T(8,128)}, f32[256,384]{1,0:T(8,128)S(1)}, u32[]{:S(2)}, u32[]{:S(2)}) collective-permute-start(f32[256,384]{1,0:T(8,128)} %get-tuple-element.151.refs_2_.refs_6_), channel_id=1, source_target_pairs={{0,1},{1,0},{2,3},{3,2},{4,5},{5,4},{6,7},{7,6},{8,9},{9,8},{10,11... | collective-permute-start | bytes 1179656 | tf_op jit(solution)/shard_map/ppermute | solution.py:452
  15.9 16.9 %collective-permute-start.5 = (f32[256,384]{1,0:T(8,128)}, f32[256,384]{1,0:T(8,128)S(1)}, u32[]{:S(2)}, u32[]{:S(2)}) collective-permute-start(f32[256,384]{1,0:T(8,128)} %get-tuple-element.161.refs_2_.refs_7_), channel_id=1, source_target_pairs={{0,1},{1,0},{2,3},{3,2},{4,5},{5,4},{6,7},{7,6},{8,9},{9,8},{10,11... | collective-permute-start | bytes 1179656 | tf_op jit(solution)/shard_map/ppermute | solution.py:452
  16.5 10.2 %collective-permute-start.2 = (f32[96,768]{1,0:T(8,128)S(1)}, f32[96,768]{1,0:T(8,128)S(1)}, u32[]{:S(2)}, u32[]{:S(2)}) collective-permute-start(f32[96,768]{1,0:T(8,128)S(1)} %collective-permute-done.1.refs_10_), channel_id=1, source_target_pairs={{0,2},{2,0},{4,6},{6,4},{8,10},{10,8},{12,14},{14,12},{16,18},{18,... | collective-permute-start | bytes 884744 | tf_op jit(solution)/shard_map/ppermute | solution.py:448
  20.9 5.8 %collective-permute-start.4 = (f32[96,768]{1,0:T(8,128)S(1)}, f32[96,768]{1,0:T(8,128)S(1)}, u32[]{:S(2)}, u32[]{:S(2)}) collective-permute-start(f32[96,768]{1,0:T(8,128)S(1)} %collective-permute-done.3.refs_12_), channel_id=1, source_target_pairs={{0,2},{2,0},{4,6},{6,4},{8,10},{10,8},{12,14},{14,12},{16,18},{18,... | collective-permute-start | bytes 884744 | tf_op jit(solution)/shard_map/ppermute | solution.py:448
  37.3 36.1 %collective-permute-start.10 = (f32[512,768]{1,0:T(8,128)S(1)}, f32[512,768]{1,0:T(8,128)S(1)}, u32[]{:S(2)}, u32[]{:S(2)}) collective-permute-start(f32[512,768]{1,0:T(8,128)S(1)} %get-tuple-element.185.refs_2_), channel_id=1, source_target_pairs={{0,1},{1,0},{2,3},{3,2},{4,5},{5,4},{6,7},{7,6},{8,9},{9,8},{10,11... | collective-permute-start | bytes 4718600 | tf_op jit(solution)/shard_map/ppermute | solution.py:452
  40.9 5.1 %collective-permute-start.8 = (f32[192,1536]{1,0:T(8,128)S(1)}, f32[192,1536]{1,0:T(8,128)S(1)}, u32[]{:S(2)}, u32[]{:S(2)}) collective-permute-start(f32[192,1536]{1,0:T(8,128)S(1)} %get-tuple-element.174), channel_id=1, source_target_pairs={{0,2},{2,0},{4,6},{6,4},{8,10},{10,8},{12,14},{14,12},{16,18},{18,... | collective-permute-start | bytes 3538952 | tf_op jit(solution)/shard_map/ppermute | solution.py:448
  41.1 6.5 %collective-permute-start.9 = (f32[192,1536]{1,0:T(8,128)S(1)}, f32[192,1536]{1,0:T(8,128)S(1)}, u32[]{:S(2)}, u32[]{:S(2)}) collective-permute-start(f32[192,1536]{1,0:T(8,128)S(1)} %get-tuple-element.183), channel_id=1, source_target_pairs={{0,2},{2,0},{4,6},{6,4},{8,10},{10,8},{12,14},{14,12},{16,18},{18,... | collective-permute-start | bytes 3538952 | tf_op jit(solution)/shard_map/ppermute | solution.py:448
  45.2 30.2 %collective-permute-start.11 = (f32[192,1536]{1,0:T(8,128)S(1)}, f32[192,1536]{1,0:T(8,128)S(1)}, u32[]{:S(2)}, u32[]{:S(2)}) collective-permute-start(f32[192,1536]{1,0:T(8,128)S(1)} %get-tuple-element.190.refs_1_), channel_id=1, source_target_pairs={{0,4},{2,6},{4,0},{6,2},{8,12},{10,14},{12,8},{14,10},{16,20},{18,... | collective-permute-start | bytes 3538952 | tf_op jit(solution)/shard_map/ppermute | solution.py:448
  48.4 28.1 %collective-permute-start.12 = (f32[192,1536]{1,0:T(8,128)S(1)}, f32[192,1536]{1,0:T(8,128)S(1)}, u32[]{:S(2)}, u32[]{:S(2)}) collective-permute-start(f32[192,1536]{1,0:T(8,128)S(1)} %get-tuple-element.194.refs_1_), channel_id=1, source_target_pairs={{0,8},{2,10},{4,12},{6,14},{8,0},{10,2},{12,4},{14,6},{16,24},{18,... | collective-permute-start | bytes 3538952 | tf_op jit(solution)/shard_map/ppermute | solution.py:448
  76.6 14.6 %collective-permute-start.14 = (f32[96,1536]{1,0:T(8,128)S(1)}, f32[96,1536]{1,0:T(8,128)S(1)}, u32[]{:S(2)}, u32[]{:S(2)}) collective-permute-start(f32[96,1536]{1,0:T(8,128)S(1)} %get-tuple-element.220.refs_3_), channel_id=1, source_target_pairs={{0,4},{2,6},{4,0},{6,2},{8,12},{10,14},{12,8},{14,10},{16,20},{18,... | collective-permute-start | bytes 1769480 | tf_op jit(solution)/shard_map/ppermute | solution.py:448
  77.5 14.5 %collective-permute-start.13 = (f32[96,1536]{1,0:T(8,128)S(1)}, f32[96,1536]{1,0:T(8,128)S(1)}, u32[]{:S(2)}, u32[]{:S(2)}) collective-permute-start(f32[96,1536]{1,0:T(8,128)S(1)} %get-tuple-element.219.refs_2_), channel_id=1, source_target_pairs={{0,8},{2,10},{4,12},{6,14},{8,0},{10,2},{12,4},{14,6},{16,24},{18,... | collective-permute-start | bytes 1769480 | tf_op jit(solution)/shard_map/ppermute | solution.py:448
  79.1 37.3 %collective-permute-start.19 = (f32[512,768]{1,0:T(8,128)S(1)}, f32[512,768]{1,0:T(8,128)S(1)}, u32[]{:S(2)}, u32[]{:S(2)}) collective-permute-start(f32[512,768]{1,0:T(8,128)S(1)} %mlp.1.refs_1_), channel_id=1, source_target_pairs={{0,1},{1,0},{2,3},{3,2},{4,5},{5,4},{6,7},{7,6},{8,9},{9,8},{10,11... | collective-permute-start | bytes 4718600 | tf_op jit(solution)/shard_map/ppermute | solution.py:452
  88.5 5.2 %collective-permute-start.15 = (f32[208,768]{1,0:T(8,128)S(1)}, f32[208,768]{1,0:T(8,128)S(1)}, u32[]{:S(2)}, u32[]{:S(2)}) collective-permute-start(f32[208,768]{1,0:T(8,128)S(1)} %get-tuple-element.210), channel_id=1, source_target_pairs={{0,2},{2,0},{4,6},{6,4},{8,10},{10,8},{12,14},{14,12},{16,18},{18,... | collective-permute-start | bytes 1916936 | tf_op jit(solution)/shard_map/ppermute | solution.py:448
  91.2 5.6 %collective-permute-start.17 = (f32[192,768]{1,0:T(8,128)S(1)}, f32[192,768]{1,0:T(8,128)S(1)}, u32[]{:S(2)}, u32[]{:S(2)}) collective-permute-start(f32[192,768]{1,0:T(8,128)S(1)} %get-tuple-element.217), channel_id=1, source_target_pairs={{0,2},{2,0},{4,6},{6,4},{8,10},{10,8},{12,14},{14,12},{16,18},{18,... | collective-permute-start | bytes 1769480 | tf_op jit(solution)/shard_map/ppermute | solution.py:448
  92.0 5.6 %collective-permute-start.18 = (f32[192,768]{1,0:T(8,128)S(1)}, f32[192,768]{1,0:T(8,128)S(1)}, u32[]{:S(2)}, u32[]{:S(2)}) collective-permute-start(f32[192,768]{1,0:T(8,128)S(1)} %get-tuple-element.226), channel_id=1, source_target_pairs={{0,2},{2,0},{4,6},{6,4},{8,10},{10,8},{12,14},{14,12},{16,18},{18,... | collective-permute-start | bytes 1769480 | tf_op jit(solution)/shard_map/ppermute | solution.py:448
  92.0 56.1 %collective-permute-start.25 = (f32[512,768]{1,0:T(8,128)S(1)}, f32[512,768]{1,0:T(8,128)S(1)}, u32[]{:S(2)}, u32[]{:S(2)}) collective-permute-start(f32[512,768]{1,0:T(8,128)S(1)} %get-tuple-element.244.own), channel_id=1, source_target_pairs={{0,1},{1,0},{2,3},{3,2},{4,5},{5,4},{6,7},{7,6},{8,9},{9,8},{10,11... | collective-permute-start | bytes 4718600 | tf_op jit(solution)/shard_map/ppermute | solution.py:452
  93.7 29.2 %collective-permute-start.20 = (f32[96,1536]{1,0:T(8,128)S(1)}, f32[96,1536]{1,0:T(8,128)S(1)}, u32[]{:S(2)}, u32[]{:S(2)}) collective-permute-start(f32[96,1536]{1,0:T(8,128)S(1)} %get-tuple-element.231), channel_id=1, source_target_pairs={{0,16},{2,18},{4,20},{6,22},{8,24},{10,26},{12,28},{14,30},{16,0},... | collective-permute-start | bytes 1769480 | tf_op jit(solution)/shard_map/ppermute | solution.py:448
  96.8 26.9 %collective-permute-start.21 = (f32[208,768]{1,0:T(8,128)S(1)}, f32[208,768]{1,0:T(8,128)S(1)}, u32[]{:S(2)}, u32[]{:S(2)}) collective-permute-start(f32[208,768]{1,0:T(8,128)S(1)} %get-tuple-element.234.refs_1_), channel_id=1, source_target_pairs={{0,4},{2,6},{4,0},{6,2},{8,12},{10,14},{12,8},{14,10},{16,20},{18,... | collective-permute-start | bytes 1916936 | tf_op jit(solution)/shard_map/ppermute | solution.py:448
  98.3 26.3 %collective-permute-start.22 = (f32[192,768]{1,0:T(8,128)S(1)}, f32[192,768]{1,0:T(8,128)S(1)}, u32[]{:S(2)}, u32[]{:S(2)}) collective-permute-start(f32[192,768]{1,0:T(8,128)S(1)} %get-tuple-element.237.refs_1_), channel_id=1, source_target_pairs={{0,8},{2,10},{4,12},{6,14},{8,0},{10,2},{12,4},{14,6},{16,24},{18,... | collective-permute-start | bytes 1769480 | tf_op jit(solution)/shard_map/ppermute | solution.py:448
  123.8 9.5 %collective-permute-start.23 = (f32[112,768]{1,0:T(8,128)S(1)}, f32[112,768]{1,0:T(8,128)S(1)}, u32[]{:S(2)}, u32[]{:S(2)}) collective-permute-start(f32[112,768]{1,0:T(8,128)S(1)} %get-tuple-element.240.refs_2_), channel_id=1, source_target_pairs={{0,8},{2,10},{4,12},{6,14},{8,0},{10,2},{12,4},{14,6},{16,24},{18,... | collective-permute-start | bytes 1032200 | tf_op jit(solution)/shard_map/ppermute | solution.py:448
  124.7 8.6 %collective-permute-start.24 = (f32[96,768]{1,0:T(8,128)S(1)}, f32[96,768]{1,0:T(8,128)S(1)}, u32[]{:S(2)}, u32[]{:S(2)}) collective-permute-start(f32[96,768]{1,0:T(8,128)S(1)} %get-tuple-element.241.refs_3_), channel_id=1, source_target_pairs={{0,4},{2,6},{4,0},{6,2},{8,12},{10,14},{12,8},{14,10},{16,20},{18,... | collective-permute-start | bytes 884744 | tf_op jit(solution)/shard_map/ppermute | solution.py:448
  133.3 17.9 %collective-permute-start.26 = (f32[112,768]{1,0:T(8,128)S(1)}, f32[112,768]{1,0:T(8,128)S(1)}, u32[]{:S(2)}, u32[]{:S(2)}) collective-permute-start(f32[112,768]{1,0:T(8,128)S(1)} %get-tuple-element.250.sent), channel_id=1, source_target_pairs={{0,16},{2,18},{4,20},{6,22},{8,24},{10,26},{12,28},{14,30},{16,0},... | collective-permute-start | bytes 1032200 | tf_op jit(solution)/shard_map/ppermute | solution.py:448
  (20 other events, 102.8 us)

commit v4 on v3

--- a/solution.py
+++ b/solution.py
@@ -171,11 +171,10 @@
 
 def middle_kernel(*refs, blocks, seq, length):
     here, tokens, o_own, o_other, w_out, table, w_up, w_down, cotangent, order = refs[:10]
-    hidden, a2_t, active, g_pre, g_bias, g_second, w_low = refs[-7:]
+    hidden, a2_t, active, g_pre, g_second, g_bias, w_low = refs[-7:]
     rows = slice(seq * length, (seq + 1) * length)
     if seq:
-        bias_before, second_before, w_before = refs[10:13]
-        g_second[: seq * length, :] = second_before[...]
+        bias_before, w_before = refs[10:12]
         w_low[...] = w_before[...]
     else:
         for b, piece in enumerate(refs[10:14]):
@@ -207,99 +206,89 @@
         g_bias[:, at] = bias_before[:, at] + bias if seq else bias
         part = right_trans(grad, w_up[:, at])
         total = part if total is None else total + part
-    g_second[rows, :] = total
+    g_second[...] = total
     a2_t[...] = right_trans(order[...], second).astype(LOW)
 
 
-def turn_back_kernel(*refs, seqs, length):
-    table, cotangent, own, other, order, g_bias, cot_sum = refs[:7]
-    hidden = refs[7 : 7 + seqs]
-    g_hidden, gh, sums = refs[7 + seqs : 10 + seqs]
-    gh_t = refs[10 + seqs :]
-    width = cotangent.shape[1]
-    totals = [0.0, 0.0, 0.0]
-    for s in range(seqs):
-        rows = slice(s * length, (s + 1) * length)
-        unit, scale = unit_rows(hidden[s][...])
-        grad = own[rows, :] + other[rows, :]
-        values = norm_back(grad * row(table, GAIN_MLP, width), unit, scale)
-        values = cotangent[rows, :].astype(HIGH) + values
-        g_hidden[rows, :] = values
-        low = values.astype(LOW)
-        gh[rows, :] = low
-        gh_t[s][...] = right_trans(order[...], low).astype(LOW)
-        parts = (col_sum(grad * unit), col_sum(grad), col_sum(values))
-        totals = [a + b for a, b in zip(totals, parts)]
-    for i, total in enumerate(totals):
-        sums[i : i + 1, :] = total
-    sums[3:6, :] = jnp.zeros((3, width), HIGH)
-    sums[6:7, :] = g_bias[:, :width]
-    sums[7:8, :] = g_bias[:, width:]
-    sums[8:9, :] = cot_sum[...]
-    sums[9:, :] = jnp.zeros_like(sums[9:, :])
-
-
-def back_kernel(*refs, seqs, length, crops):
-    tokens, table, gh, w_out, w_q, w_k, w_v, q, k, v, lse, _ = refs[:12]
-    sums, g_first = refs[12:14]
-    g_qk, g_val = (refs[14 + i * seqs : 14 + (i + 1) * seqs] for i in range(2))
+def back_kernel(*refs, seq, length, crops):
+    tokens, table, cotangent, hidden, own, other, order = refs[:7]
+    w_out, w_q, w_k, w_v, q, k, v, lse = refs[7:15]
+    before = refs[15:17]
+    g_hidden, gh_t, g_qk, g_val, sums, g_first = refs[17:]
     width, local = tokens.shape[1], q.shape[1]
+    rows = slice(seq * length, (seq + 1) * length)
+    full = slice(0, width)
+    if seq:
+        sums_before, first_before = before
+        g_first[: seq * length, :] = first_before[...]
+        sums[6:, :] = sums_before[6:, :]
+    else:
+        g_bias, cot_sum = before
+        sums[6:7, :] = g_bias[:, :width]
+        sums[7:8, :] = g_bias[:, width:]
+        sums[8:9, :] = cot_sum[...]
+        sums[9:, :] = jnp.zeros_like(sums[9:, :])
+
+    def put(r, at, value):
+        sums[r : r + 1, at] = sums_before[r : r + 1, at] + value if seq else value
+
+    unit, scale = unit_rows(hidden[...])
+    grad = own[...] + other[...]
+    put(0, full, col_sum(grad * unit))
+    put(1, full, col_sum(grad))
+    values = norm_back(grad * row(table, GAIN_MLP, width), unit, scale)
+    values = cotangent[rows, :].astype(HIGH) + values
+    g_hidden[...] = values
+    put(2, full, col_sum(values))
+    low = values.astype(LOW)
+    gh_t[...] = right_trans(order[...], low).astype(LOW)
+    g_o = right_trans(low, w_out[...]).astype(LOW)
+    same = same_crop(table, crops + seq, length)
     low_half, masks = half_masks()
-    full = slice(0, width)
-    before = refs[11]
-    sums[:3, :] = before[:3, :]
-    sums[6:, :] = before[6:, :]
-
-    def put(s, r, at, value):
-        sums[r : r + 1, at] = sums[r : r + 1, at] + value if s else value
-
-    for s in range(seqs):
-        rows = slice(s * length, (s + 1) * length)
-        g_o = right_trans(gh[rows, :], w_out[...]).astype(LOW)
-        same = same_crop(table, crops + s, length)
-        for t in range(local // PAIR):
-            at = slice(t * PAIR, (t + 1) * PAIR)
-            q_pair, k_pair, v_pair, o_pair = q[rows, at], k[rows, at], v[rows, at], g_o[:, at]
-            got = []
-            for half in range(2):
-                h = 2 * t + half
-                scores = right_trans(q_pair * masks[half], k_pair)
-                probs = jnp.exp(jnp.where(same, scores, NEGATIVE) - lse[rows, h : h + 1])
-                g_probs = right_trans(o_pair * masks[half], v_pair)
-                inner = jnp.sum(g_probs * probs, axis=-1, keepdims=True)
-                g_scores = (probs * (g_probs - inner)).astype(LOW)
-                got.append(
-                    (
-                        plain_dot(g_scores, k_pair),
-                        left_trans(g_scores, q_pair),
-                        left_trans(probs.astype(LOW), o_pair),
-                    )
+    for t in range(local // PAIR):
+        at = slice(t * PAIR, (t + 1) * PAIR)
+        q_pair, k_pair, v_pair, o_pair = q[rows, at], k[rows, at], v[rows, at], g_o[:, at]
+        got = []
+        for half in range(2):
+            h = 2 * t + half
+            scores = right_trans(q_pair * masks[half], k_pair)
+            probs = jnp.exp(jnp.where(same, scores, NEGATIVE) - lse[rows, h : h + 1])
+            g_probs = right_trans(o_pair * masks[half], v_pair)
+            inner = jnp.sum(g_probs * probs, axis=-1, keepdims=True)
+            g_scores = (probs * (g_probs - inner)).astype(LOW)
+            got.append(
+                (
+                    plain_dot(g_scores, k_pair),
+                    left_trans(g_scores, q_pair),
+                    left_trans(probs.astype(LOW), o_pair),
                 )
-            g_q = (jnp.where(low_half, got[0][0], got[1][0]) * 0.125).astype(LOW)
-            g_k = jnp.where(low_half, got[0][1], got[1][1]).astype(LOW)
-            g_v = jnp.where(low_half, got[0][2], got[1][2]).astype(LOW)
-            beside = slice(local + t * PAIR, local + (t + 1) * PAIR)
-            g_qk[s][:, at] = g_q
-            g_qk[s][:, beside] = g_k
-            g_val[s][:, at] = g_v
-            put(s, 5, at, col_sum(g_q.astype(HIGH)))
-            put(s, 5, beside, col_sum(g_v.astype(HIGH)))
-        part = right_trans(g_qk[s][:, :local], w_q[...])
-        part = part + right_trans(g_qk[s][:, local:], w_k[...])
-        part = part + right_trans(g_val[s][...], w_v[...])
-        g_first[rows, :] = part
-        unit_one, _ = unit_rows(tokens[rows, :].astype(HIGH))
-        put(s, 3, full, col_sum(part * unit_one))
-        put(s, 4, full, col_sum(part))
-
-
-def base_kernel(table, tokens, g_hidden, own, base, unit_out, scale_out, *, length):
+            )
+        g_q = (jnp.where(low_half, got[0][0], got[1][0]) * 0.125).astype(LOW)
+        g_k = jnp.where(low_half, got[0][1], got[1][1]).astype(LOW)
+        g_v = jnp.where(low_half, got[0][2], got[1][2]).astype(LOW)
+        beside = slice(local + t * PAIR, local + (t + 1) * PAIR)
+        g_qk[:, at] = g_q
+        g_qk[:, beside] = g_k
+        g_val[:, at] = g_v
+        put(5, at, col_sum(g_q.astype(HIGH)))
+        put(5, beside, col_sum(g_v.astype(HIGH)))
+    part = right_trans(g_qk[:, :local], w_q[...])
+    part = part + right_trans(g_qk[:, local:], w_k[...])
+    part = part + right_trans(g_val[...], w_v[...])
+    g_first[rows, :] = part
+    unit_one, _ = unit_rows(tokens[rows, :].astype(HIGH))
+    put(3, full, col_sum(part * unit_one))
+    put(4, full, col_sum(part))
+
+
+def base_kernel(table, tokens, own, *refs, length):
+    g_hidden, (base, unit_out, scale_out) = refs[:-3], refs[-3:]
     gain = row(table, GAIN_ATTN, tokens.shape[1])
     for s in range(tokens.shape[0] // length):
         rows = slice(s * length, (s + 1) * length)
         part = own[rows, :]
         unit, scale = unit_rows(tokens[rows, :].astype(HIGH))
-        base[rows, :] = g_hidden[rows, :] + norm_back(part * gain, unit, scale)
+        base[rows, :] = g_hidden[s][...] + norm_back(part * gain, unit, scale)
         unit_out[rows, :] = unit
         scale_out[rows, :] = scale
 
@@ -379,7 +368,8 @@
 
 
 def end_kernel(*refs, wide):
-    keeps, got, outs = refs[:2], refs[2], refs[3:]
+    count = (len(refs) - 1) // (1 + wide)
+    keeps, got, outs = refs[:count], refs[count], refs[count + 1 :]
     at = o = 0
     for keep in keeps:
         size, each = keep.shape[0], keep.shape[1] // wide
@@ -390,15 +380,14 @@
         at += size
 
 
-def final_kernel(here, one, two, sent, got, *outs):
-    size = one.shape[0]
-    each = one.shape[1] // 2
-    for o, (keep, at) in enumerate(((one, 0), (two, size + SMALL))):
-        for w in range(2):
-            columns = slice(w * each, (w + 1) * each)
-            outs[2 * o + w][...] = keep[:, columns] + got[at : at + size, columns]
+def final_kernel(here, keep, sent, got, *outs):
+    size = keep.shape[0]
+    each = keep.shape[1] // 2
+    for w in range(2):
+        columns = slice(w * each, (w + 1) * each)
+        outs[w][...] = keep[:, columns] + got[:size, columns]
     total = sent[size : size + SMALL, :] + got[size : size + SMALL, :]
-    bias_q, bias_v, bias_up, gain_mlp, shift_mlp, bias_out, bias_down, gains = outs[4:]
+    bias_q, bias_v, bias_up, gain_mlp, shift_mlp, bias_out, bias_down, gains = outs[2:]
     width = total.shape[1]
     bias_q[...] = total[5, :each]
     bias_v[...] = total[5, each:]
@@ -496,6 +485,10 @@
         outs = self.shapes(self.rows, self.rows + self.extra)
         self.keep, self.sent = self.steps(kernel, "near", outs, held)
         self.got = send(self.sent, self.bits[1], self.count)
+
+    def rest(self):
+        while self.at + 1 < len(self.bits):
+            self.step()
 
     def step(self):
         self.at += 1
@@ -534,12 +527,13 @@
     return sent, got
 
 
-def finish(one, two, got, cost=0):
+def finish(parts, got, cost=0):
     outs = []
-    for part in (one, two):
+    for part in parts:
         outs += [((part.rows, part.columns // part.wide), HIGH)] * part.wide
-    kernel = partial(end_kernel, wide=one.wide)
-    return one.steps(kernel, "end", outs, [one.keep, two.keep, got], cost=cost)
+    kernel = partial(end_kernel, wide=parts[0].wide)
+    held = [part.keep for part in parts] + [got]
+    return parts[0].steps(kernel, "end", outs, held, cost=cost)
 
 
 def body(
@@ -629,7 +623,7 @@
 
     cotangent, w_up, w_down, w_out, order_b, cot_sum = turned[:6]
     a1_a, a1_b, cot_a = (list(turned[6 + i * seqs : 6 + (i + 1) * seqs]) for i in range(3))
-    hidden, a2_b, active, g_pre, carried = [], [], [], [], []
+    hidden, a2_b, active, g_pre, second, carried = [], [], [], [], [], []
     for s in range(seqs):
         result = steps(
             partial(middle_kernel, blocks=4, seq=s, length=length),
@@ -639,8 +633,8 @@
                 ((width, length), LOW),
                 ((length, hidden_units), LOW),
                 ((length, hidden_units), LOW),
+                ((length, width), HIGH),
                 ((1, hidden_units), HIGH),
-                (((s + 1) * length, width), HIGH),
                 ((local, width), LOW),
             ],
             [
@@ -659,11 +653,11 @@
             smem=1,
             tie=2,
         )
-        for held, value in zip((hidden, a2_b, active, g_pre), result):
+        for held, value in zip((hidden, a2_b, active, g_pre, second), result):
             held.append(value)
-        carried = list(result[4:])
-    bias_sum, second, _ = carried
-    second_other = swap(second)
+        carried = list(result[5:])
+    bias_sum = carried[0]
+    second_other = [swap(g) for g in second]
 
     down = Scatter(steps, count, orders[0], [(cot_a, active)])
     up = Scatter(steps, count, orders[1], [(a2_b, g_pre)])
@@ -673,28 +667,32 @@
     mlp_other = swap(mlp_part)
     down.near()
     up.near()
-    g_hidden, gh, sums, *gh_b = steps(
-        partial(turn_back_kernel, seqs=seqs, length=length),
-        "turn_back",
-        [((rows, width), HIGH), ((rows, width), LOW), ((SMALL, width), HIGH)]
-        + [((width, length), LOW)] * seqs,
-        [table, cotangent, second, second_other, order_b, bias_sum, cot_sum] + hidden,
-        tie=2,
-        cost=9 * 10**9,
-    )
-    down.step()
-    up.step()
-    sums, g_first, *result = steps(
-        partial(back_kernel, seqs=seqs, length=length, crops=crops),
-        "back",
-        [((SMALL, width), HIGH), ((rows, width), HIGH)]
-        + [((length, 2 * local), LOW)] * seqs
-        + [((length, local), LOW)] * seqs,
-        [tokens, table, gh, w_out, w_query, w_key, w_value, query, key_rows, value_rows]
-        + [log_total, sums],
-        tie=2,
-    )
-    g_qk, g_val = (result[i * seqs : (i + 1) * seqs] for i in range(2))
+    g_hidden, gh_b, g_qk, g_val, carried = [], [], [], [], [bias_sum, cot_sum]
+    for s in range(seqs):
+        if s == seqs - 1:
+            down.step()
+            up.step()
+        result = steps(
+            partial(back_kernel, seq=s, length=length, crops=crops),
+            "back",
+            [
+                ((length, width), HIGH),
+                ((width, length), LOW),
+                ((length, 2 * local), LOW),
+                ((length, local), LOW),
+                ((SMALL, width), HIGH),
+                (((s + 1) * length, width), HIGH),
+            ],
+            [tokens, table, cotangent, hidden[s], second[s], second_other[s], order_b]
+            + [w_out, w_query, w_key, w_value, query, key_rows, value_rows, log_total]
+            + carried,
+            tie=4,
+            cost=0 if s else 6 * 10**9,
+        )
+        for held, value in zip((g_hidden, gh_b, g_qk, g_val), result):
+            held.append(value)
+        carried = list(result[4:])
+    sums, g_first = carried
     first_other = swap(g_first)
     heads = Scatter(steps, count, orders[0], [(a1_a, g_qk)], wide=2, small=sums)
     others = Scatter(steps, count, orders[1], [(a1_b, g_val), (gh_b, mixed)], wide=2)
@@ -709,16 +707,18 @@
         [((rows, width), LOW)],
         [table, mlp_part, mlp_other] + hidden,
         tie=1,
+        cost=3 * 10**9,
     )[0]
-    w_down_t, done_w_up = finish(down, up, mlp_got, cost=15 * 10**8)
     heads.step()
     others.step()
-    sent, got = join(heads, others)
+    w_down_t, done_w_up = finish([down, up], mlp_got, 15 * 10**8)
+    heads.rest()
+    others.rest()
     base, unit, scale = steps(
         partial(base_kernel, length=length),
         "base",
         [((rows, width), HIGH)] * 2 + [((rows, 1), HIGH)],
-        [table, tokens, g_hidden, g_first],
+        [table, tokens, g_first] + g_hidden,
         tie=2,
     )
     grad_tokens = steps(
@@ -732,8 +732,6 @@
     (
         grad_w_q,
         grad_w_k,
-        grad_w_v,
-        w_out_t,
         done_bias_q,
         done_bias_v,
         done_bias_up,
@@ -745,17 +743,19 @@
     ) = steps(
         final_kernel,
         "final",
-        [((size, local), HIGH)] * 4
+        [((size, local), HIGH)] * 2
         + [((local,), HIGH)] * 2
         + [((hidden_units,), HIGH)]
         + [((size,), HIGH)] * 4
         + [((8, 128), HIGH)],
-        [scalar, heads.keep, others.keep, sent, got],
+        [scalar, heads.keep, heads.sent, heads.got],
         smem=1,
         tie=1,
     )
+    gains_other = swap(gains)
+    grad_w_v, w_out_t = finish([others], others.got)
     done_gain_attn, done_shift_attn = steps(
-        gain_kernel, "gains", [((size,), HIGH)] * 2, [gains, swap(gains)]
+        gain_kernel, "gains", [((size,), HIGH)] * 2, [gains, gains_other]
     )
     return (
         block_out,

time: 156 us -> 151 us (0.968)
  waiting for transfers between devices: 77.2 us -> 69.3 us
    ppermute x7 -> x8, waiting for transfers between devices: 54 us -> 34.3 us  [swap(): return lax.ppermute(values, 'mp', [(0, 1), (1, 0)])]
    ppermute x21 -> x22, waiting for transfers between devices: 23.2 us -> 35.1 us  [send(): return lax.ppermute(values, 'dp', [(i, i ^ 1 << bit) for i in range(count)])]
    ppermute x7 -> x8, starting transfers between devices: 9.94 us -> 11.5 us  [swap(): return lax.ppermute(values, 'mp', [(0, 1), (1, 0)])]
    pallas_call x28 -> x30, Pallas kernels: 44.8 us -> 46 us  [__call__(): pl.pallas_call(kernel, name=name, out_shape=[jax.ShapeDtypeStruct(s, d) f...]
    ppermute x21 -> x22, starting transfers between devices: 20.2 us -> 19.7 us  [send(): return lax.ppermute(values, 'dp', [(i, i ^ 1 << bit) for i in range(count)])]
  transfers between devices with their start and end apart: 28 -> 30, of which waited for: 17 -> 14; matrix products, arithmetic and copies ran while one was open for 0% -> 0% of each run, Pallas kernels for 24% -> 26%
where the time goes in v4:
time: 151 us; the launch traced here: 150 us
  waiting for transfers between devices  69.3 us (46%)
  Pallas kernels  46 us (30%)
  starting transfers between devices  31.3 us (21%)
  local copies, waits for them, and re-layouts  2.84 us (2%)
    pallas_call x30, Pallas kernels, __call__(): pl.pallas_call(kernel, name=name, out_shape=[jax.ShapeDtypeStruct(s, d) f...  46 us
    ppermute x22, waiting for transfers between devices, send(): return lax.ppermute(values, 'dp', [(i, i ^ 1 << bit) for i in range(count)])  35.1 us
    ppermute x8, waiting for transfers between devices, swap(): return lax.ppermute(values, 'mp', [(0, 1), (1, 0)])  34.3 us
    ppermute x22, starting transfers between devices, send(): return lax.ppermute(values, 'dp', [(i, i ^ 1 << bit) for i in range(count)])  19.7 us
    ppermute x8, starting transfers between devices, swap(): return lax.ppermute(values, 'mp', [(0, 1), (1, 0)])  11.5 us
  transfers between devices with their start and end apart: 30, of which 14 were waited for; matrix products, arithmetic and copies ran while one was open for 0% of the time, Pallas kernels for 26%

profile of v4, /device:TPU:0, one launch (start us, length us, event | category | flops | bytes accessed | tf_op | source)
XLA Modules:
  0.0 150.5 jit_solution(18051564735554237037)
XLA Ops:
  0.7 1.8 %load.1 = (f32[96,768]{1,0:T(8,128)}, f32[12,768]{1,0:T(8,128)}) custom-call(s32[1]{0:T(128)} %bitcast.here.refs_0_, bf16[384,768]{1,0:T(8,128)(2,1)} %refs_3_.5, s32[2,256]{1,0:T(2,128)} %crops.1, f32[768]{0:T(1024)} %refs_0_.2, f32[768]{0:T(1024)} %refs_1_.3, f32[384]{0:T(512)} %refs_2_.3, f32[384]{0:T(512)} %refs_3_.3, f32[768]{0:T(1024)} %refs_4_.1, ...), custom_call_target="tpu_custom_call" | custom-call | flops 1000 | bytes 1000 | tf_op jit(solution)/shard_map/load/pallas_call | solution.py:418
  2.4 3.0 %collective-permute-start.1 = (f32[96,768]{1,0:T(8,128)}, f32[96,768]{1,0:T(8,128)S(1)}, u32[]{:S(2)}, u32[]{:S(2)}) collective-permute-start(f32[96,768]{1,0:T(8,128)} %get-tuple-element.147), channel_id=1, source_target_pairs={{0,1},{1,0},{2,3},{3,2},{4,5},{5,4},{6,7},{7,6},{8,9},{9,8},{10,11... | collective-permute-start | bytes 884744 | tf_op jit(solution)/shard_map/ppermute | solution.py:441
  5.4 6.8 %front.1 = (bf16[512,768]{1,0:T(8,128)(2,1)}, bf16[768,384]{1,0:T(8,128)(2,1)}, bf16[768,384]{1,0:T(8,128)(2,1)}, bf16[768,384]{1,0:T(8,128)(2,1)}, bf16[512,768...) custom-call(bf16[512,768]{1,0:T(8,128)(2,1)} %refs_0_.3, ...), custom_call_target="tpu_custom_call" | custom-call | flops 1000 | bytes 1000 | tf_op jit(solution)/shard_map/front/pallas_call | solution.py:418
  12.7 1.8 %collective-permute-start.3 = (f32[96,768]{1,0:T(8,128)S(1)}, f32[96,768]{1,0:T(8,128)S(1)}, u32[]{:S(2)}, u32[]{:S(2)}) collective-permute-start(f32[96,768]{1,0:T(8,128)S(1)} %collective-permute-done.1.refs_10_), channel_id=1, source_target_pairs={{0,4},{2,6},{4,0},{6,2},{8,12},{10,14},{12,8},{14,10},{16,20},{18,... | collective-permute-start | bytes 884744 | tf_op jit(solution)/shard_map/ppermute | solution.py:437
  16.5 4.4 %collective-permute-done.3.refs_12_ = f32[96,768]{1,0:T(8,128)S(1)} collective-permute-done((f32[96,768]{1,0:T(8,128)S(1)}, f32[96,768]{1,0:T(8,128)S(1)}, u32[]{:S(2)}, u32[]{:S(2)}) %collective-permute-start.3) | collective-permute-done | bytes 294944 | tf_op jit(solution)/shard_map/ppermute | solution.py:437
  22.0 4.0 %turn.1 = (bf16[512,768]{1,0:T(8,128)(2,1)S(1)}, bf16[768,1536]{1,0:T(8,128)(2,1)S(1)}, bf16[1536,768]{1,0:T(8,128)(2,1)}, bf16[384,768]{1,0:T(8,128)(2,1)S(1)},...) custom-call(s32[1]{0:T(128)} %bitcast.here.refs_0_, ...), custom_call_target="tpu_custom_call" | custom-call | flops 1000 | bytes 1000 | tf_op jit(solution)/shard_map/turn/pallas_call | solution.py:418
  26.7 1.7 %copy-done = bf16[1536,768]{1,0:T(8,128)(2,1)S(1)} copy-done((bf16[1536,768]{1,0:T(8,128)(2,1)S(1)}, bf16[1536,768]{1,0:T(8,128)(2,1)}, u32[]{:S(2)}) %copy-start) | copy-done | bytes 2359320
  28.4 4.3 %middle.2 = (f32[256,768]{1,0:T(8,128)S(1)}, bf16[768,256]{1,0:T(8,128)(2,1)S(1)}, bf16[256,1536]{1,0:T(8,128)(2,1)S(1)}, bf16[256,1536]{1,0:T(8,128)(2,1)S(1)},...) custom-call(s32[1]{0:T(128)} %bitcast.here.refs_0_, bf16[512,768]{1,0:T(8,128)(2,1)S(1)} %copy-done.2, ...), custom_call_target="tpu_custom_call" | custom-call | flops 1000 | bytes 1000 | tf_op jit(solution)/shard_map/middle/pallas_call | solution.py:418
  32.8 4.5 %middle.3 = (f32[256,768]{1,0:T(8,128)S(1)}, bf16[768,256]{1,0:T(8,128)(2,1)S(1)}, bf16[256,1536]{1,0:T(8,128)(2,1)S(1)}, bf16[256,1536]{1,0:T(8,128)(2,1)S(1)},...) custom-call(s32[1]{0:T(128)} %bitcast.here.refs_0_, bf16[512,768]{1,0:T(8,128)(2,1)S(1)} %copy-done.2, ...), custom_call_target="tpu_custom_call" | custom-call | flops 1000 | bytes 1000 | tf_op jit(solution)/shard_map/middle/pallas_call | solution.py:418
  46.8 1.6 %collective-permute-start.12 = (f32[192,1536]{1,0:T(8,128)S(1)}, f32[192,1536]{1,0:T(8,128)S(1)}, u32[]{:S(2)}, u32[]{:S(2)}) collective-permute-start(f32[192,1536]{1,0:T(8,128)S(1)} %get-tuple-element.204.refs_1_), channel_id=1, source_target_pairs={{0,8},{2,10},{4,12},{6,14},{8,0},{10,2},{12,4},{14,6},{16,24},{18,... | collective-permute-start | bytes 3538952 | tf_op jit(solution)/shard_map/ppermute | solution.py:437
  50.5 9.9 %collective-permute-done.10.refs_5_ = f32[256,768]{1,0:T(8,128)S(1)} collective-permute-done((f32[256,768]{1,0:T(8,128)S(1)}, f32[256,768]{1,0:T(8,128)S(1)}, u32[]{:S(2)}, u32[]{:S(2)}) %collective-permute-start.10) | collective-permute-done | bytes 786464 | tf_op jit(solution)/shard_map/ppermute | solution.py:441
  60.4 4.9 %back.2 = (f32[256,768]{1,0:T(8,128)S(1)}, bf16[768,256]{1,0:T(8,128)(2,1)S(1)}, bf16[256,768]{1,0:T(8,128)(2,1)S(1)}, bf16[256,384]{1,0:T(8,128)(2,1)S(1)}, f32...) custom-call(bf16[512,768]{1,0:T(8,128)(2,1)S(1)} %copy-done.2, f32[12,768]{1,0:T(8,128)S(1)} %copy-done.6, ...), custom_call_target="tpu_custom_call" | custom-call | flops 6000001024 | bytes 1000 | tf_op jit(solution)/shard_map/back/pallas_call | solution.py:418
  65.3 6.5 %collective-permute-done.11.refs_2_ = f32[192,1536]{1,0:T(8,128)S(1)} collective-permute-done((f32[192,1536]{1,0:T(8,128)S(1)}, f32[192,1536]{1,0:T(8,128)S(1)}, u32[]{:S(2)}, u32[]{:S(2)}) %collective-permute-start.11) | collective-permute-done | bytes 1179680 | tf_op jit(solution)/shard_map/ppermute | solution.py:437
  72.0 2.9 %collective-permute-done.12.refs_2_ = f32[192,1536]{1,0:T(8,128)S(1)} collective-permute-done((f32[192,1536]{1,0:T(8,128)S(1)}, f32[192,1536]{1,0:T(8,128)S(1)}, u32[]{:S(2)}, u32[]{:S(2)}) %collective-permute-start.12) | collective-permute-done | bytes 1179680 | tf_op jit(solution)/shard_map/ppermute | solution.py:437
  77.8 5.0 %back.3 = (f32[256,768]{1,0:T(8,128)S(1)}, bf16[768,256]{1,0:T(8,128)(2,1)S(1)}, bf16[256,768]{1,0:T(8,128)(2,1)S(1)}, bf16[256,384]{1,0:T(8,128)(2,1)S(1)}, f32...) custom-call(bf16[512,768]{1,0:T(8,128)(2,1)S(1)} %copy-done.2, f32[12,768]{1,0:T(8,128)S(1)} %copy-done.6, ...), custom_call_target="tpu_custom_call" | custom-call | flops 1000 | bytes 1000 | tf_op jit(solution)/shard_map/back/pallas_call | solution.py:418
  84.5 5.2 %collective-permute-done.15.refs_5_ = f32[96,1536]{1,0:T(8,128)S(1)} collective-permute-done((f32[96,1536]{1,0:T(8,128)S(1)}, f32[96,1536]{1,0:T(8,128)S(1)}, u32[]{:S(2)}, u32[]{:S(2)}) %collective-permute-start.15) | collective-permute-done | bytes 589856 | tf_op jit(solution)/shard_map/ppermute | solution.py:437
  94.7 1.6 %collective-permute-start.22 = (f32[192,768]{1,0:T(8,128)S(1)}, f32[192,768]{1,0:T(8,128)S(1)}, u32[]{:S(2)}, u32[]{:S(2)}) collective-permute-start(f32[192,768]{1,0:T(8,128)S(1)} %get-tuple-element.239.refs_1_), channel_id=1, source_target_pairs={{0,8},{2,10},{4,12},{6,14},{8,0},{10,2},{12,4},{14,6},{16,24},{18,... | collective-permute-start | bytes 1769480 | tf_op jit(solution)/shard_map/ppermute | solution.py:437
  96.3 2.6 %collective-permute-start.23 = (f32[96,1536]{1,0:T(8,128)S(1)}, f32[96,1536]{1,0:T(8,128)S(1)}, u32[]{:S(2)}, u32[]{:S(2)}) collective-permute-start(f32[96,1536]{1,0:T(8,128)S(1)} %get-tuple-element.243), channel_id=1, source_target_pairs={{0,16},{2,18},{4,20},{6,22},{8,24},{10,26},{12,28},{14,30},{16,0},... | collective-permute-start | bytes 1769480 | tf_op jit(solution)/shard_map/ppermute | solution.py:437
  98.9 12.0 %collective-permute-done.20.refs_2_ = f32[512,768]{1,0:T(8,128)S(1)} collective-permute-done((f32[512,768]{1,0:T(8,128)S(1)}, f32[512,768]{1,0:T(8,128)S(1)}, u32[]{:S(2)}, u32[]{:S(2)}) %collective-permute-start.20) | collective-permute-done | bytes 1572896 | tf_op jit(solution)/shard_map/ppermute | solution.py:441
  113.9 9.7 %collective-permute-done.22.refs_2_ = f32[192,768]{1,0:T(8,128)S(1)} collective-permute-done((f32[192,768]{1,0:T(8,128)S(1)}, f32[192,768]{1,0:T(8,128)S(1)}, u32[]{:S(2)}, u32[]{:S(2)}) %collective-permute-start.22) | collective-permute-done | bytes 589856 | tf_op jit(solution)/shard_map/ppermute | solution.py:437
  125.7 4.1 %collective-permute-done.24.refs_2_ = f32[112,768]{1,0:T(8,128)S(1)} collective-permute-done((f32[112,768]{1,0:T(8,128)S(1)}, f32[112,768]{1,0:T(8,128)S(1)}, u32[]{:S(2)}, u32[]{:S(2)}) %collective-permute-start.24) | collective-permute-done | bytes 344096 | tf_op jit(solution)/shard_map/ppermute | solution.py:437
  129.8 2.7 %collective-permute-start.27 = (f32[64,768]{1,0:T(8,128)S(1)}, f32[64,768]{1,0:T(8,128)S(1)}, u32[]{:S(2)}, u32[]{:S(2)}) collective-permute-start(f32[64,768]{1,0:T(8,128)S(1)} %get-tuple-element.256.sent), channel_id=1, source_target_pairs={{0,16},{2,18},{4,20},{6,22},{8,24},{10,26},{12,28},{14,30},{16,0},... | collective-permute-start | bytes 589832 | tf_op jit(solution)/shard_map/ppermute | solution.py:437
  134.0 9.8 %collective-permute-done.26.other = f32[512,768]{1,0:T(8,128)S(1)} collective-permute-done((f32[512,768]{1,0:T(8,128)S(1)}, f32[512,768]{1,0:T(8,128)S(1)}, u32[]{:S(2)}, u32[]{:S(2)}) %collective-permute-start.26) | collective-permute-done | bytes 1572896 | tf_op jit(solution)/shard_map/ppermute | solution.py:441
  143.8 1.9 %last.1 = f32[512,768]{1,0:T(8,128)} custom-call(f32[12,768]{1,0:T(8,128)S(1)} %copy-done.6, f32[512,768]{1,0:T(8,128)S(1)} %get-tuple-element.252.base, f32[512,768]{1,0:T(8,128)S(1)} %get-tuple-element.253.unit, f32[512,1]{1,0:T(8,128)S(1)} %get-tuple-element.254.scale, f32[512,768]{1,0:T(8,128)S(1)} %collective-permute-done.26.other), custom_call_target="tpu_custom_call" | custom-call | flops 1000 | bytes 1000 | tf_op jit(solution)/shard_map/last/pallas_call | solution.py:418
  (98 shorter events, 37.0 us)
Async XLA Ops:
  2.4 10.2 %collective-permute-start.1 = (f32[96,768]{1,0:T(8,128)}, f32[96,768]{1,0:T(8,128)S(1)}, u32[]{:S(2)}, u32[]{:S(2)}) collective-permute-start(f32[96,768]{1,0:T(8,128)} %get-tuple-element.147), channel_id=1, source_target_pairs={{0,1},{1,0},{2,3},{3,2},{4,5},{5,4},{6,7},{7,6},{8,9},{9,8},{10,11... | collective-permute-start | bytes 884744 | tf_op jit(solution)/shard_map/ppermute | solution.py:441
  12.7 8.2 %collective-permute-start.3 = (f32[96,768]{1,0:T(8,128)S(1)}, f32[96,768]{1,0:T(8,128)S(1)}, u32[]{:S(2)}, u32[]{:S(2)}) collective-permute-start(f32[96,768]{1,0:T(8,128)S(1)} %collective-permute-done.1.refs_10_), channel_id=1, source_target_pairs={{0,4},{2,6},{4,0},{6,2},{8,12},{10,14},{12,8},{14,10},{16,20},{18,... | collective-permute-start | bytes 884744 | tf_op jit(solution)/shard_map/ppermute | solution.py:437
  14.4 12.3 %collective-permute-start = (f32[256,384]{1,0:T(8,128)}, f32[256,384]{1,0:T(8,128)S(1)}, u32[]{:S(2)}, u32[]{:S(2)}) collective-permute-start(f32[256,384]{1,0:T(8,128)} %get-tuple-element.155.refs_2_.refs_6_), channel_id=1, source_target_pairs={{0,1},{1,0},{2,3},{3,2},{4,5},{5,4},{6,7},{7,6},{8,9},{9,8},{10,11... | collective-permute-start | bytes 1179656 | tf_op jit(solution)/shard_map/ppermute | solution.py:441
  15.9 16.8 %collective-permute-start.5 = (f32[256,384]{1,0:T(8,128)}, f32[256,384]{1,0:T(8,128)S(1)}, u32[]{:S(2)}, u32[]{:S(2)}) collective-permute-start(f32[256,384]{1,0:T(8,128)} %get-tuple-element.165.refs_2_.refs_7_), channel_id=1, source_target_pairs={{0,1},{1,0},{2,3},{3,2},{4,5},{5,4},{6,7},{7,6},{8,9},{9,8},{10,11... | collective-permute-start | bytes 1179656 | tf_op jit(solution)/shard_map/ppermute | solution.py:441
  16.5 10.2 %collective-permute-start.2 = (f32[96,768]{1,0:T(8,128)S(1)}, f32[96,768]{1,0:T(8,128)S(1)}, u32[]{:S(2)}, u32[]{:S(2)}) collective-permute-start(f32[96,768]{1,0:T(8,128)S(1)} %collective-permute-done.1.refs_10_), channel_id=1, source_target_pairs={{0,2},{2,0},{4,6},{6,4},{8,10},{10,8},{12,14},{14,12},{16,18},{18,... | collective-permute-start | bytes 884744 | tf_op jit(solution)/shard_map/ppermute | solution.py:437
  20.9 5.8 %collective-permute-start.4 = (f32[96,768]{1,0:T(8,128)S(1)}, f32[96,768]{1,0:T(8,128)S(1)}, u32[]{:S(2)}, u32[]{:S(2)}) collective-permute-start(f32[96,768]{1,0:T(8,128)S(1)} %collective-permute-done.3.refs_12_), channel_id=1, source_target_pairs={{0,2},{2,0},{4,6},{6,4},{8,10},{10,8},{12,14},{14,12},{16,18},{18,... | collective-permute-start | bytes 884744 | tf_op jit(solution)/shard_map/ppermute | solution.py:437
  39.5 6.5 %collective-permute-start.9 = (f32[192,1536]{1,0:T(8,128)S(1)}, f32[192,1536]{1,0:T(8,128)S(1)}, u32[]{:S(2)}, u32[]{:S(2)}) collective-permute-start(f32[192,1536]{1,0:T(8,128)S(1)} %get-tuple-element.186), channel_id=1, source_target_pairs={{0,2},{2,0},{4,6},{6,4},{8,10},{10,8},{12,14},{14,12},{16,18},{18,... | collective-permute-start | bytes 3538952 | tf_op jit(solution)/shard_map/ppermute | solution.py:437
  40.0 20.4 %collective-permute-start.10 = (f32[256,768]{1,0:T(8,128)S(1)}, f32[256,768]{1,0:T(8,128)S(1)}, u32[]{:S(2)}, u32[]{:S(2)}) collective-permute-start(f32[256,768]{1,0:T(8,128)S(1)} %get-tuple-element.188.refs_4_), channel_id=1, source_target_pairs={{0,1},{1,0},{2,3},{3,2},{4,5},{5,4},{6,7},{7,6},{8,9},{9,8},{10,11... | collective-permute-start | bytes 2359304 | tf_op jit(solution)/shard_map/ppermute | solution.py:441
  44.0 27.8 %collective-permute-start.11 = (f32[192,1536]{1,0:T(8,128)S(1)}, f32[192,1536]{1,0:T(8,128)S(1)}, u32[]{:S(2)}, u32[]{:S(2)}) collective-permute-start(f32[192,1536]{1,0:T(8,128)S(1)} %get-tuple-element.200.refs_1_), channel_id=1, source_target_pairs={{0,4},{2,6},{4,0},{6,2},{8,12},{10,14},{12,8},{14,10},{16,20},{18,... | collective-permute-start | bytes 3538952 | tf_op jit(solution)/shard_map/ppermute | solution.py:437
  46.8 28.1 %collective-permute-start.12 = (f32[192,1536]{1,0:T(8,128)S(1)}, f32[192,1536]{1,0:T(8,128)S(1)}, u32[]{:S(2)}, u32[]{:S(2)}) collective-permute-start(f32[192,1536]{1,0:T(8,128)S(1)} %get-tuple-element.204.refs_1_), channel_id=1, source_target_pairs={{0,8},{2,10},{4,12},{6,14},{8,0},{10,2},{12,4},{14,6},{16,24},{18,... | collective-permute-start | bytes 3538952 | tf_op jit(solution)/shard_map/ppermute | solution.py:437
  48.5 29.4 %collective-permute-start.13 = (f32[256,768]{1,0:T(8,128)S(1)}, f32[256,768]{1,0:T(8,128)S(1)}, u32[]{:S(2)}, u32[]{:S(2)}) collective-permute-start(f32[256,768]{1,0:T(8,128)S(1)} %get-tuple-element.206.refs_4_), channel_id=1, source_target_pairs={{0,1},{1,0},{2,3},{3,2},{4,5},{5,4},{6,7},{7,6},{8,9},{9,8},{10,11... | collective-permute-start | bytes 2359304 | tf_op jit(solution)/shard_map/ppermute | solution.py:441
  50.0 61.0 %collective-permute-start.20 = (f32[512,768]{1,0:T(8,128)S(1)}, f32[512,768]{1,0:T(8,128)S(1)}, u32[]{:S(2)}, u32[]{:S(2)}) collective-permute-start(f32[512,768]{1,0:T(8,128)S(1)} %mlp.1.refs_1_), channel_id=1, source_target_pairs={{0,1},{1,0},{2,3},{3,2},{4,5},{5,4},{6,7},{7,6},{8,9},{9,8},{10,11... | collective-permute-start | bytes 4718600 | tf_op jit(solution)/shard_map/ppermute | solution.py:441
  75.1 14.6 %collective-permute-start.15 = (f32[96,1536]{1,0:T(8,128)S(1)}, f32[96,1536]{1,0:T(8,128)S(1)}, u32[]{:S(2)}, u32[]{:S(2)}) collective-permute-start(f32[96,1536]{1,0:T(8,128)S(1)} %get-tuple-element.225.refs_3_), channel_id=1, source_target_pairs={{0,4},{2,6},{4,0},{6,2},{8,12},{10,14},{12,8},{14,10},{16,20},{18,... | collective-permute-start | bytes 1769480 | tf_op jit(solution)/shard_map/ppermute | solution.py:437
  76.2 14.5 %collective-permute-start.14 = (f32[96,1536]{1,0:T(8,128)S(1)}, f32[96,1536]{1,0:T(8,128)S(1)}, u32[]{:S(2)}, u32[]{:S(2)}) collective-permute-start(f32[96,1536]{1,0:T(8,128)S(1)} %get-tuple-element.224.refs_2_), channel_id=1, source_target_pairs={{0,8},{2,10},{4,12},{6,14},{8,0},{10,2},{12,4},{14,6},{16,24},{18,... | collective-permute-start | bytes 1769480 | tf_op jit(solution)/shard_map/ppermute | solution.py:437
  83.3 7.5 %collective-permute-start.17 = (f32[192,768]{1,0:T(8,128)S(1)}, f32[192,768]{1,0:T(8,128)S(1)}, u32[]{:S(2)}, u32[]{:S(2)}) collective-permute-start(f32[192,768]{1,0:T(8,128)S(1)} %get-tuple-element.228), channel_id=1, source_target_pairs={{0,2},{2,0},{4,6},{6,4},{8,10},{10,8},{12,14},{14,12},{16,18},{18,... | collective-permute-start | bytes 1769480 | tf_op jit(solution)/shard_map/ppermute | solution.py:437
  83.4 9.0 %collective-permute-start.16 = (f32[208,768]{1,0:T(8,128)S(1)}, f32[208,768]{1,0:T(8,128)S(1)}, u32[]{:S(2)}, u32[]{:S(2)}) collective-permute-start(f32[208,768]{1,0:T(8,128)S(1)} %get-tuple-element.215), channel_id=1, source_target_pairs={{0,2},{2,0},{4,6},{6,4},{8,10},{10,8},{12,14},{14,12},{16,18},{18,... | collective-permute-start | bytes 1916936 | tf_op jit(solution)/shard_map/ppermute | solution.py:437
  90.8 53.0 %collective-permute-start.26 = (f32[512,768]{1,0:T(8,128)S(1)}, f32[512,768]{1,0:T(8,128)S(1)}, u32[]{:S(2)}, u32[]{:S(2)}) collective-permute-start(f32[512,768]{1,0:T(8,128)S(1)} %get-tuple-element.251.own), channel_id=1, source_target_pairs={{0,1},{1,0},{2,3},{3,2},{4,5},{5,4},{6,7},{7,6},{8,9},{9,8},{10,11... | collective-permute-start | bytes 4718600 | tf_op jit(solution)/shard_map/ppermute | solution.py:441
  92.9 19.2 %collective-permute-start.21 = (f32[208,768]{1,0:T(8,128)S(1)}, f32[208,768]{1,0:T(8,128)S(1)}, u32[]{:S(2)}, u32[]{:S(2)}) collective-permute-start(f32[208,768]{1,0:T(8,128)S(1)} %get-tuple-element.236.refs_1_), channel_id=1, source_target_pairs={{0,4},{2,6},{4,0},{6,2},{8,12},{10,14},{12,8},{14,10},{16,20},{18,... | collective-permute-start | bytes 1916936 | tf_op jit(solution)/shard_map/ppermute | solution.py:437
  94.7 28.9 %collective-permute-start.22 = (f32[192,768]{1,0:T(8,128)S(1)}, f32[192,768]{1,0:T(8,128)S(1)}, u32[]{:S(2)}, u32[]{:S(2)}) collective-permute-start(f32[192,768]{1,0:T(8,128)S(1)} %get-tuple-element.239.refs_1_), channel_id=1, source_target_pairs={{0,8},{2,10},{4,12},{6,14},{8,0},{10,2},{12,4},{14,6},{16,24},{18,... | collective-permute-start | bytes 1769480 | tf_op jit(solution)/shard_map/ppermute | solution.py:437
  96.3 28.5 %collective-permute-start.23 = (f32[96,1536]{1,0:T(8,128)S(1)}, f32[96,1536]{1,0:T(8,128)S(1)}, u32[]{:S(2)}, u32[]{:S(2)}) collective-permute-start(f32[96,1536]{1,0:T(8,128)S(1)} %get-tuple-element.243), channel_id=1, source_target_pairs={{0,16},{2,18},{4,20},{6,22},{8,24},{10,26},{12,28},{14,30},{16,0},... | collective-permute-start | bytes 1769480 | tf_op jit(solution)/shard_map/ppermute | solution.py:437
  112.2 17.6 %collective-permute-start.24 = (f32[112,768]{1,0:T(8,128)S(1)}, f32[112,768]{1,0:T(8,128)S(1)}, u32[]{:S(2)}, u32[]{:S(2)}) collective-permute-start(f32[112,768]{1,0:T(8,128)S(1)} %get-tuple-element.246.refs_1_), channel_id=1, source_target_pairs={{0,8},{2,10},{4,12},{6,14},{8,0},{10,2},{12,4},{14,6},{16,24},{18,... | collective-permute-start | bytes 1032200 | tf_op jit(solution)/shard_map/ppermute | solution.py:437
  123.6 8.9 %collective-permute-start.25 = (f32[96,768]{1,0:T(8,128)S(1)}, f32[96,768]{1,0:T(8,128)S(1)}, u32[]{:S(2)}, u32[]{:S(2)}) collective-permute-start(f32[96,768]{1,0:T(8,128)S(1)} %get-tuple-element.249.refs_1_), channel_id=1, source_target_pairs={{0,4},{2,6},{4,0},{6,2},{8,12},{10,14},{12,8},{14,10},{16,20},{18,... | collective-permute-start | bytes 884744 | tf_op jit(solution)/shard_map/ppermute | solution.py:437
  129.8 15.8 %collective-permute-start.27 = (f32[64,768]{1,0:T(8,128)S(1)}, f32[64,768]{1,0:T(8,128)S(1)}, u32[]{:S(2)}, u32[]{:S(2)}) collective-permute-start(f32[64,768]{1,0:T(8,128)S(1)} %get-tuple-element.256.sent), channel_id=1, source_target_pairs={{0,16},{2,18},{4,20},{6,22},{8,24},{10,26},{12,28},{14,30},{16,0},... | collective-permute-start | bytes 589832 | tf_op jit(solution)/shard_map/ppermute | solution.py:437
  132.6 15.3 %collective-permute-start.28 = (f32[48,768]{1,0:T(8,128)S(1)}, f32[48,768]{1,0:T(8,128)S(1)}, u32[]{:S(2)}, u32[]{:S(2)}) collective-permute-start(f32[48,768]{1,0:T(8,128)S(1)} %get-tuple-element.260), channel_id=1, source_target_pairs={{0,16},{2,18},{4,20},{6,22},{8,24},{10,26},{12,28},{14,30},{16,0},... | collective-permute-start | bytes 442376 | tf_op jit(solution)/shard_map/ppermute | solution.py:437
  (22 other events, 195.9 us)

commit v5 on v4

--- a/solution.py
+++ b/solution.py
@@ -145,42 +145,47 @@
     return marks.astype(HIGH).astype(LOW)
 
 
-def turn_kernel(here, first, *refs, count, orders):
-    sources, held = refs[:4], refs[4:8]
-    order_b, sums, sems = refs[8], refs[9], refs[-1]
+def turn_kernel(here, *refs, count, orders):
+    sources, held = refs[:4], (refs[-2], *refs[4:7])
+    order_b, sums, sems = refs[7], refs[8], refs[-1]
     seqs = (len(refs) - 11) // 3
-    a1_a, a1_b, cot_a = (refs[10 + i * seqs : 10 + (i + 1) * seqs] for i in range(3))
+    a1_a, a1_b, cot_a = (refs[9 + i * seqs : 9 + (i + 1) * seqs] for i in range(3))
+    first = refs[-2]
     length = first.shape[0] // seqs
     copies = copies_of(sources, held, sems)
     width = first.shape[1]
     order_a = relative_rows(here[0], width, count, orders[0])
     order = relative_rows(here[0], width, count, orders[1])
     order_b[...] = order
+    copies[0].wait()
     for s in range(seqs):
         part = first[s * length : (s + 1) * length, :]
         a1_a[s][...] = right_trans(order_a, part).astype(LOW)
         a1_b[s][...] = right_trans(order, part).astype(LOW)
-    for copy in copies:
+    for copy in copies[1:]:
         copy.wait()
-    cot = held[0][...]
+    cot = held[1][...]
     for s in range(seqs):
         part = cot[s * length : (s + 1) * length, :]
         cot_a[s][...] = right_trans(order_a, part).astype(LOW)
     sums[...] = col_sum(cot.astype(HIGH))
 
 
+def low_kernel(values, out):
+    out[...] = values[...].astype(LOW)
+
+
+def gather_kernel(here, *refs):
+    for b, piece in enumerate(refs[:-1]):
+        size = piece.shape[0]
+        start = pl.multiple_of(((here[0] & 3) ^ b) * size, size)
+        refs[-1][pl.ds(start, size), :] = piece[...].astype(LOW)
+
+
 def middle_kernel(*refs, blocks, seq, length):
-    here, tokens, o_own, o_other, w_out, table, w_up, w_down, cotangent, order = refs[:10]
-    hidden, a2_t, active, g_pre, g_second, g_bias, w_low = refs[-7:]
+    tokens, o_own, o_other, w_out, w_low, table, w_up, w_down, cotangent, order = refs[:10]
+    hidden, a2_t, active, g_pre, g_second, g_bias = refs[-6:]
     rows = slice(seq * length, (seq + 1) * length)
-    if seq:
-        bias_before, w_before = refs[10:12]
-        w_low[...] = w_before[...]
-    else:
-        for b, piece in enumerate(refs[10:14]):
-            size = piece.shape[0]
-            start = pl.multiple_of(((here[0] & 3) ^ b) * size, size)
-            w_low[pl.ds(start, size), :] = piece[...].astype(LOW)
     attn = plain_dot(o_own[...].astype(LOW), w_out[...])
     attn = attn + plain_dot(o_other[...].astype(LOW), w_low[...])
     width = tokens.shape[1]
@@ -203,7 +208,7 @@
         grad = (right_trans(cot, w_down[at, :]) * slope).astype(LOW)
         g_pre[:, at] = grad
         bias = col_sum(grad.astype(HIGH))
-        g_bias[:, at] = bias_before[:, at] + bias if seq else bias
+        g_bias[:, at] = refs[10][:, at] + bias if seq else bias
         part = right_trans(grad, w_up[:, at])
         total = part if total is None else total + part
     g_second[...] = total
@@ -380,15 +385,10 @@
         at += size
 
 
-def final_kernel(here, keep, sent, got, *outs):
-    size = keep.shape[0]
-    each = keep.shape[1] // 2
-    for w in range(2):
-        columns = slice(w * each, (w + 1) * each)
-        outs[w][...] = keep[:, columns] + got[:size, columns]
+def vector_kernel(here, sent, got, *outs, size):
     total = sent[size : size + SMALL, :] + got[size : size + SMALL, :]
-    bias_q, bias_v, bias_up, gain_mlp, shift_mlp, bias_out, bias_down, gains = outs[2:]
-    width = total.shape[1]
+    bias_q, bias_v, bias_up, gain_mlp, shift_mlp, bias_out, bias_down, gains = outs
+    width, each = total.shape[1], bias_q.shape[0]
     bias_q[...] = total[5, :each]
     bias_v[...] = total[5, each:]
     for i in range(bias_up.shape[0] // width):
@@ -606,23 +606,29 @@
 
     got, _ = lax.optimization_barrier((got, first))
     beside = send(got, 1, count)
-    pieces = [got, send(got, 0, count), beside, send(beside, 0, count)]
+    pieces = [got, send(got, 0, count), beside]
     turned = steps(
         partial(turn_kernel, count=count, orders=orders),
         "turn",
-        like(cotangent, w_up, w_down, w_out)
+        like(cotangent, w_up, w_out)
         + [((width, width), LOW), ((1, width), HIGH)]
         + [((width, length), LOW)] * (3 * seqs),
-        [scalar, first, cotangent, w_up, w_down, w_out],
-        scratch=[pltpu.SemaphoreType.DMA((4,))],
-        whole=range(2, 6),
+        [scalar, first, cotangent, w_up, w_out],
+        scratch=[pltpu.VMEM((rows, width), LOW), pltpu.SemaphoreType.DMA((4,))],
+        whole=range(1, 5),
         smem=1,
         tie=1,
         limit=44,
     )
 
-    cotangent, w_up, w_down, w_out, order_b, cot_sum = turned[:6]
-    a1_a, a1_b, cot_a = (list(turned[6 + i * seqs : 6 + (i + 1) * seqs]) for i in range(3))
+    cotangent, w_up, w_out, order_b, cot_sum = turned[:5]
+    a1_a, a1_b, cot_a = (list(turned[5 + i * seqs : 5 + (i + 1) * seqs]) for i in range(3))
+    beside, _ = lax.optimization_barrier((beside, order_b))
+    pieces.append(send(beside, 0, count))
+    mixed_other[0] = steps(low_kernel, "low", [((length, local), LOW)], [mixed_other[0]], cost=31 * 10**8)[0]
+    w_low = steps(
+        gather_kernel, "gather", [((local, width), LOW)], [scalar] + pieces, smem=1, tie=1
+    )[0]
     hidden, a2_b, active, g_pre, second, carried = [], [], [], [], [], []
     for s in range(seqs):
         result = steps(
@@ -635,23 +641,21 @@
                 ((length, hidden_units), LOW),
                 ((length, width), HIGH),
                 ((1, hidden_units), HIGH),
-                ((local, width), LOW),
             ],
             [
-                scalar,
                 tokens,
                 mixed[s],
                 mixed_other[s],
                 w_out,
+                w_low,
                 table,
                 w_up,
                 w_down,
                 cotangent,
                 order_b,
             ]
-            + (carried if s else pieces),
-            smem=1,
-            tie=2,
+            + carried,
+            tie=1,
         )
         for held, value in zip((hidden, a2_b, active, g_pre, second), result):
             held.append(value)
@@ -730,8 +734,6 @@
     )[0]
     size = width // count
     (
-        grad_w_q,
-        grad_w_k,
         done_bias_q,
         done_bias_v,
         done_bias_up,
@@ -741,18 +743,18 @@
         done_bias_down,
         gains,
     ) = steps(
-        final_kernel,
-        "final",
-        [((size, local), HIGH)] * 2
-        + [((local,), HIGH)] * 2
+        partial(vector_kernel, size=size),
+        "vectors",
+        [((local,), HIGH)] * 2
         + [((hidden_units,), HIGH)]
         + [((size,), HIGH)] * 4
         + [((8, 128), HIGH)],
-        [scalar, heads.keep, heads.sent, heads.got],
+        [scalar, heads.sent, heads.got],
         smem=1,
         tie=1,
     )
     gains_other = swap(gains)
+    grad_w_q, grad_w_k = finish([heads], heads.got)
     grad_w_v, w_out_t = finish([others], others.got)
     done_gain_attn, done_shift_attn = steps(
         gain_kernel, "gains", [((size,), HIGH)] * 2, [gains, gains_other]

time: 151 us -> 149 us (0.987)
  starting transfers between devices: 31.3 us -> 29.3 us
    ppermute x8, waiting for transfers between devices: 34.3 us -> 39.6 us  [swap(): return lax.ppermute(values, 'mp', [(0, 1), (1, 0)])]
    ppermute x22, waiting for transfers between devices: 35.1 us -> 30.2 us  [send(): return lax.ppermute(values, 'dp', [(i, i ^ 1 << bit) for i in range(count)])]
    ppermute x8, starting transfers between devices: 11.5 us -> 7.81 us  [swap(): return lax.ppermute(values, 'mp', [(0, 1), (1, 0)])]
    ppermute x22, starting transfers between devices: 19.7 us -> 21.5 us  [send(): return lax.ppermute(values, 'dp', [(i, i ^ 1 << bit) for i in range(count)])]
    pallas_call x30 -> x33, Pallas kernels: 46 us -> 45.9 us  [__call__(): pl.pallas_call(kernel, name=name, out_shape=[jax.ShapeDtypeStruct(s, d) f...]
  transfers between devices with their start and end apart: 30 -> 30, of which waited for: 14 -> 15; matrix products, arithmetic and copies ran while one was open for 0% -> 0% of each run, Pallas kernels for 26% -> 26%
where the time goes in v5:
time: 149 us
  waiting for transfers between devices  69.8 us (47%)
  Pallas kernels  45.9 us (31%)
  starting transfers between devices  29.3 us (20%)
  local copies, waits for them, and re-layouts  2.98 us (2%)
    pallas_call x33, Pallas kernels, __call__(): pl.pallas_call(kernel, name=name, out_shape=[jax.ShapeDtypeStruct(s, d) f...  45.9 us
    ppermute x8, waiting for transfers between devices, swap(): return lax.ppermute(values, 'mp', [(0, 1), (1, 0)])  39.6 us
    ppermute x22, waiting for transfers between devices, send(): return lax.ppermute(values, 'dp', [(i, i ^ 1 << bit) for i in range(count)])  30.2 us
    ppermute x22, starting transfers between devices, send(): return lax.ppermute(values, 'dp', [(i, i ^ 1 << bit) for i in range(count)])  21.5 us
    ppermute x8, starting transfers between devices, swap(): return lax.ppermute(values, 'mp', [(0, 1), (1, 0)])  7.81 us
  transfers between devices with their start and end apart: 30, of which 15 were waited for; matrix products, arithmetic and copies ran while one was open for 0% of the time, Pallas kernels for 26%

profile of v5, /device:TPU:0, one launch (start us, length us, event | category | flops | bytes accessed | tf_op | source)
XLA Modules:
  0.0 148.9 jit_solution(8040524360945719423)
XLA Ops:
  0.7 1.8 %load.1 = (f32[96,768]{1,0:T(8,128)}, f32[12,768]{1,0:T(8,128)}) custom-call(s32[1]{0:T(128)} %bitcast.here, bf16[384,768]{1,0:T(8,128)(2,1)} %refs_3_.5, s32[2,256]{1,0:T(2,128)} %crops.1, f32[768]{0:T(1024)} %refs_0_.1, f32[768]{0:T(1024)} %refs_1_.3, f32[384]{0:T(512)} %refs_2_.3, f32[384]{0:T(512)} %refs_3_.3, f32[768]{0:T(1024)} %refs_4_.1, ...), custom_call_target="tpu_custom_call" | custom-call | flops 1000 | bytes 1000 | tf_op jit(solution)/shard_map/load/pallas_call | solution.py:418
  2.4 3.0 %collective-permute-start = (f32[96,768]{1,0:T(8,128)}, f32[96,768]{1,0:T(8,128)S(1)}, u32[]{:S(2)}, u32[]{:S(2)}) collective-permute-start(f32[96,768]{1,0:T(8,128)} %get-tuple-element.149), channel_id=1, source_target_pairs={{0,1},{1,0},{2,3},{3,2},{4,5},{5,4},{6,7},{7,6},{8,9},{9,8},{10,11... | collective-permute-start | bytes 884744 | tf_op jit(solution)/shard_map/ppermute | solution.py:441
  5.4 6.8 %front.1 = (bf16[512,768]{1,0:T(8,128)(2,1)}, bf16[768,384]{1,0:T(8,128)(2,1)}, bf16[768,384]{1,0:T(8,128)(2,1)}, bf16[768,384]{1,0:T(8,128)(2,1)}, bf16[512,768...) custom-call(bf16[512,768]{1,0:T(8,128)(2,1)} %refs_0_.2, ...), custom_call_target="tpu_custom_call" | custom-call | flops 1000 | bytes 1000 | tf_op jit(solution)/shard_map/front/pallas_call | solution.py:418
  12.7 1.8 %collective-permute-start.3 = (f32[96,768]{1,0:T(8,128)S(1)}, f32[96,768]{1,0:T(8,128)S(1)}, u32[]{:S(2)}, u32[]{:S(2)}) collective-permute-start(f32[96,768]{1,0:T(8,128)S(1)} %collective-permute-done.refs_0_), channel_id=1, source_target_pairs={{0,4},{2,6},{4,0},{6,2},{8,12},{10,14},{12,8},{14,10},{16,20},{18,... | collective-permute-start | bytes 884744 | tf_op jit(solution)/shard_map/ppermute | solution.py:437
  17.1 3.7 %turn.1 = (bf16[512,768]{1,0:T(8,128)(2,1)S(1)}, bf16[768,1536]{1,0:T(8,128)(2,1)S(1)}, bf16[384,768]{1,0:T(8,128)(2,1)S(1)}, bf16[768,768]{1,0:T(8,128)(2,1)S(1...) custom-call(s32[1]{0:T(128)} %bitcast.here, ...), custom_call_target="tpu_custom_call" | custom-call | flops 1000 | bytes 1000 | tf_op jit(solution)/shard_map/turn/pallas_call | solution.py:418
  21.4 3.2 %collective-permute-done.1.values = f32[256,384]{1,0:T(8,128)S(1)} collective-permute-done((f32[256,384]{1,0:T(8,128)}, f32[256,384]{1,0:T(8,128)S(1)}, u32[]{:S(2)}, u32[]{:S(2)}) %collective-permute-start.1) | collective-permute-done | bytes 393248 | tf_op jit(solution)/shard_map/ppermute | solution.py:441
  26.5 4.2 %middle.2 = (f32[256,768]{1,0:T(8,128)S(1)}, bf16[768,256]{1,0:T(8,128)(2,1)S(1)}, bf16[256,1536]{1,0:T(8,128)(2,1)S(1)}, bf16[256,1536]{1,0:T(8,128)(2,1)S(1)},...) custom-call(bf16[512,768]{1,0:T(8,128)(2,1)S(1)} %copy-done.1, f32[256,384]{1,0:T(8,128)S(1)} %copy-done.2, ...), custom_call_target="tpu_custom_call" | custom-call | flops 1000 | bytes 1000 | tf_op jit(solution)/shard_map/middle/pallas_call | solution.py:418
  31.5 4.3 %middle.3 = (f32[256,768]{1,0:T(8,128)S(1)}, bf16[768,256]{1,0:T(8,128)(2,1)S(1)}, bf16[256,1536]{1,0:T(8,128)(2,1)S(1)}, bf16[256,1536]{1,0:T(8,128)(2,1)S(1)},...) custom-call(bf16[512,768]{1,0:T(8,128)(2,1)S(1)} %copy-done.1, f32[256,384]{1,0:T(8,128)S(1)} %copy-done.3, ...), custom_call_target="tpu_custom_call" | custom-call | flops 1000 | bytes 1000 | tf_op jit(solution)/shard_map/middle/pallas_call | solution.py:418
  45.3 1.7 %collective-permute-start.12 = (f32[192,1536]{1,0:T(8,128)S(1)}, f32[192,1536]{1,0:T(8,128)S(1)}, u32[]{:S(2)}, u32[]{:S(2)}) collective-permute-start(f32[192,1536]{1,0:T(8,128)S(1)} %get-tuple-element.207.refs_1_), channel_id=1, source_target_pairs={{0,8},{2,10},{4,12},{6,14},{8,0},{10,2},{12,4},{14,6},{16,24},{18,... | collective-permute-start | bytes 3538952 | tf_op jit(solution)/shard_map/ppermute | solution.py:437
  49.0 9.9 %collective-permute-done.10.refs_5_ = f32[256,768]{1,0:T(8,128)S(1)} collective-permute-done((f32[256,768]{1,0:T(8,128)S(1)}, f32[256,768]{1,0:T(8,128)S(1)}, u32[]{:S(2)}, u32[]{:S(2)}) %collective-permute-start.10) | collective-permute-done | bytes 786464 | tf_op jit(solution)/shard_map/ppermute | solution.py:441
  58.9 4.9 %back.2 = (f32[256,768]{1,0:T(8,128)S(1)}, bf16[768,256]{1,0:T(8,128)(2,1)S(1)}, bf16[256,768]{1,0:T(8,128)(2,1)S(1)}, bf16[256,384]{1,0:T(8,128)(2,1)S(1)}, f32...) custom-call(bf16[512,768]{1,0:T(8,128)(2,1)S(1)} %copy-done.1, f32[12,768]{1,0:T(8,128)S(1)} %copy-done.5, ...), custom_call_target="tpu_custom_call" | custom-call | flops 6000001024 | bytes 1000 | tf_op jit(solution)/shard_map/back/pallas_call | solution.py:418
  63.8 6.3 %collective-permute-done.11.refs_2_ = f32[192,1536]{1,0:T(8,128)S(1)} collective-permute-done((f32[192,1536]{1,0:T(8,128)S(1)}, f32[192,1536]{1,0:T(8,128)S(1)}, u32[]{:S(2)}, u32[]{:S(2)}) %collective-permute-start.11) | collective-permute-done | bytes 1179680 | tf_op jit(solution)/shard_map/ppermute | solution.py:437
  70.2 3.2 %collective-permute-done.12.refs_2_ = f32[192,1536]{1,0:T(8,128)S(1)} collective-permute-done((f32[192,1536]{1,0:T(8,128)S(1)}, f32[192,1536]{1,0:T(8,128)S(1)}, u32[]{:S(2)}, u32[]{:S(2)}) %collective-permute-start.12) | collective-permute-done | bytes 1179680 | tf_op jit(solution)/shard_map/ppermute | solution.py:437
  76.7 4.9 %back.3 = (f32[256,768]{1,0:T(8,128)S(1)}, bf16[768,256]{1,0:T(8,128)(2,1)S(1)}, bf16[256,768]{1,0:T(8,128)(2,1)S(1)}, bf16[256,384]{1,0:T(8,128)(2,1)S(1)}, f32...) custom-call(bf16[512,768]{1,0:T(8,128)(2,1)S(1)} %copy-done.1, f32[12,768]{1,0:T(8,128)S(1)} %copy-done.5, ...), custom_call_target="tpu_custom_call" | custom-call | flops 1000 | bytes 1000 | tf_op jit(solution)/shard_map/back/pallas_call | solution.py:418
  83.3 4.8 %collective-permute-done.15.refs_5_ = f32[96,1536]{1,0:T(8,128)S(1)} collective-permute-done((f32[96,1536]{1,0:T(8,128)S(1)}, f32[96,1536]{1,0:T(8,128)S(1)}, u32[]{:S(2)}, u32[]{:S(2)}) %collective-permute-start.15) | collective-permute-done | bytes 589856 | tf_op jit(solution)/shard_map/ppermute | solution.py:437
  92.3 1.7 %collective-permute-start.22 = (f32[192,768]{1,0:T(8,128)S(1)}, f32[192,768]{1,0:T(8,128)S(1)}, u32[]{:S(2)}, u32[]{:S(2)}) collective-permute-start(f32[192,768]{1,0:T(8,128)S(1)} %get-tuple-element.242.refs_1_), channel_id=1, source_target_pairs={{0,8},{2,10},{4,12},{6,14},{8,0},{10,2},{12,4},{14,6},{16,24},{18,... | collective-permute-start | bytes 1769480 | tf_op jit(solution)/shard_map/ppermute | solution.py:437
  93.9 2.6 %collective-permute-start.23 = (f32[96,1536]{1,0:T(8,128)S(1)}, f32[96,1536]{1,0:T(8,128)S(1)}, u32[]{:S(2)}, u32[]{:S(2)}) collective-permute-start(f32[96,1536]{1,0:T(8,128)S(1)} %get-tuple-element.246), channel_id=1, source_target_pairs={{0,16},{2,18},{4,20},{6,22},{8,24},{10,26},{12,28},{14,30},{16,0},... | collective-permute-start | bytes 1769480 | tf_op jit(solution)/shard_map/ppermute | solution.py:437
  96.5 12.9 %collective-permute-done.20.refs_2_ = f32[512,768]{1,0:T(8,128)S(1)} collective-permute-done((f32[512,768]{1,0:T(8,128)S(1)}, f32[512,768]{1,0:T(8,128)S(1)}, u32[]{:S(2)}, u32[]{:S(2)}) %collective-permute-start.20) | collective-permute-done | bytes 1572896 | tf_op jit(solution)/shard_map/ppermute | solution.py:441
  112.3 8.9 %collective-permute-done.22.refs_2_ = f32[192,768]{1,0:T(8,128)S(1)} collective-permute-done((f32[192,768]{1,0:T(8,128)S(1)}, f32[192,768]{1,0:T(8,128)S(1)}, u32[]{:S(2)}, u32[]{:S(2)}) %collective-permute-start.22) | collective-permute-done | bytes 589856 | tf_op jit(solution)/shard_map/ppermute | solution.py:437
  123.3 4.1 %collective-permute-done.24.refs_2_ = f32[112,768]{1,0:T(8,128)S(1)} collective-permute-done((f32[112,768]{1,0:T(8,128)S(1)}, f32[112,768]{1,0:T(8,128)S(1)}, u32[]{:S(2)}, u32[]{:S(2)}) %collective-permute-start.24) | collective-permute-done | bytes 344096 | tf_op jit(solution)/shard_map/ppermute | solution.py:437
  127.5 2.7 %collective-permute-start.27 = (f32[64,768]{1,0:T(8,128)S(1)}, f32[64,768]{1,0:T(8,128)S(1)}, u32[]{:S(2)}, u32[]{:S(2)}) collective-permute-start(f32[64,768]{1,0:T(8,128)S(1)} %get-tuple-element.259.sent), channel_id=1, source_target_pairs={{0,16},{2,18},{4,20},{6,22},{8,24},{10,26},{12,28},{14,30},{16,0},... | collective-permute-start | bytes 589832 | tf_op jit(solution)/shard_map/ppermute | solution.py:437
  131.7 10.6 %collective-permute-done.26.other = f32[512,768]{1,0:T(8,128)S(1)} collective-permute-done((f32[512,768]{1,0:T(8,128)S(1)}, f32[512,768]{1,0:T(8,128)S(1)}, u32[]{:S(2)}, u32[]{:S(2)}) %collective-permute-start.26) | collective-permute-done | bytes 1572896 | tf_op jit(solution)/shard_map/ppermute | solution.py:441
  142.3 1.9 %last.1 = f32[512,768]{1,0:T(8,128)} custom-call(f32[12,768]{1,0:T(8,128)S(1)} %copy-done.5, f32[512,768]{1,0:T(8,128)S(1)} %get-tuple-element.255.base, f32[512,768]{1,0:T(8,128)S(1)} %get-tuple-element.256.unit, f32[512,1]{1,0:T(8,128)S(1)} %get-tuple-element.257.scale, f32[512,768]{1,0:T(8,128)S(1)} %collective-permute-done.26.other), custom_call_target="tpu_custom_call" | custom-call | flops 1000 | bytes 1000 | tf_op jit(solution)/shard_map/last/pallas_call | solution.py:418
  146.5 1.9 %collective-permute-done.29.other = f32[8,128]{1,0:T(8,128)S(1)} collective-permute-done((f32[8,128]{1,0:T(8,128)S(1)}, f32[8,128]{1,0:T(8,128)S(1)}, u32[]{:S(2)}, u32[]{:S(2)}) %collective-permute-start.29) | collective-permute-done | bytes 4128 | tf_op jit(solution)/shard_map/ppermute | solution.py:441
  (99 shorter events, 36.3 us)
Async XLA Ops:
  2.4 10.2 %collective-permute-start = (f32[96,768]{1,0:T(8,128)}, f32[96,768]{1,0:T(8,128)S(1)}, u32[]{:S(2)}, u32[]{:S(2)}) collective-permute-start(f32[96,768]{1,0:T(8,128)} %get-tuple-element.149), channel_id=1, source_target_pairs={{0,1},{1,0},{2,3},{3,2},{4,5},{5,4},{6,7},{7,6},{8,9},{9,8},{10,11... | collective-permute-start | bytes 884744 | tf_op jit(solution)/shard_map/ppermute | solution.py:441
  12.2 12.3 %collective-permute-start.1 = (f32[256,384]{1,0:T(8,128)}, f32[256,384]{1,0:T(8,128)S(1)}, u32[]{:S(2)}, u32[]{:S(2)}) collective-permute-start(f32[256,384]{1,0:T(8,128)} %get-tuple-element.161.refs_1_.refs_6_), channel_id=1, source_target_pairs={{0,1},{1,0},{2,3},{3,2},{4,5},{5,4},{6,7},{7,6},{8,9},{9,8},{10,11... | collective-permute-start | bytes 1179656 | tf_op jit(solution)/shard_map/ppermute | solution.py:441
  12.7 8.2 %collective-permute-start.3 = (f32[96,768]{1,0:T(8,128)S(1)}, f32[96,768]{1,0:T(8,128)S(1)}, u32[]{:S(2)}, u32[]{:S(2)}) collective-permute-start(f32[96,768]{1,0:T(8,128)S(1)} %collective-permute-done.refs_0_), channel_id=1, source_target_pairs={{0,4},{2,6},{4,0},{6,2},{8,12},{10,14},{12,8},{14,10},{16,20},{18,... | collective-permute-start | bytes 884744 | tf_op jit(solution)/shard_map/ppermute | solution.py:437
  14.4 17.1 %collective-permute-start.5 = (f32[256,384]{1,0:T(8,128)}, f32[256,384]{1,0:T(8,128)S(1)}, u32[]{:S(2)}, u32[]{:S(2)}) collective-permute-start(f32[256,384]{1,0:T(8,128)} %get-tuple-element.169.refs_1_.refs_7_), channel_id=1, source_target_pairs={{0,1},{1,0},{2,3},{3,2},{4,5},{5,4},{6,7},{7,6},{8,9},{9,8},{10,11... | collective-permute-start | bytes 1179656 | tf_op jit(solution)/shard_map/ppermute | solution.py:441
  36.6 4.5 %collective-permute-start.7 = (f32[192,1536]{1,0:T(8,128)S(1)}, f32[192,1536]{1,0:T(8,128)S(1)}, u32[]{:S(2)}, u32[]{:S(2)}) collective-permute-start(f32[192,1536]{1,0:T(8,128)S(1)} %get-tuple-element.185), channel_id=1, source_target_pairs={{0,2},{2,0},{4,6},{6,4},{8,10},{10,8},{12,14},{14,12},{16,18},{18,... | collective-permute-start | bytes 3538952 | tf_op jit(solution)/shard_map/ppermute | solution.py:437
  37.9 5.7 %collective-permute-start.8 = (f32[192,1536]{1,0:T(8,128)S(1)}, f32[192,1536]{1,0:T(8,128)S(1)}, u32[]{:S(2)}, u32[]{:S(2)}) collective-permute-start(f32[192,1536]{1,0:T(8,128)S(1)} %get-tuple-element.180), channel_id=1, source_target_pairs={{0,2},{2,0},{4,6},{6,4},{8,10},{10,8},{12,14},{14,12},{16,18},{18,... | collective-permute-start | bytes 3538952 | tf_op jit(solution)/shard_map/ppermute | solution.py:437
  38.1 6.5 %collective-permute-start.9 = (f32[192,1536]{1,0:T(8,128)S(1)}, f32[192,1536]{1,0:T(8,128)S(1)}, u32[]{:S(2)}, u32[]{:S(2)}) collective-permute-start(f32[192,1536]{1,0:T(8,128)S(1)} %get-tuple-element.189), channel_id=1, source_target_pairs={{0,2},{2,0},{4,6},{6,4},{8,10},{10,8},{12,14},{14,12},{16,18},{18,... | collective-permute-start | bytes 3538952 | tf_op jit(solution)/shard_map/ppermute | solution.py:437
  38.5 20.4 %collective-permute-start.10 = (f32[256,768]{1,0:T(8,128)S(1)}, f32[256,768]{1,0:T(8,128)S(1)}, u32[]{:S(2)}, u32[]{:S(2)}) collective-permute-start(f32[256,768]{1,0:T(8,128)S(1)} %get-tuple-element.191.refs_4_), channel_id=1, source_target_pairs={{0,1},{1,0},{2,3},{3,2},{4,5},{5,4},{6,7},{7,6},{8,9},{9,8},{10,11... | collective-permute-start | bytes 2359304 | tf_op jit(solution)/shard_map/ppermute | solution.py:441
  42.0 28.1 %collective-permute-start.11 = (f32[192,1536]{1,0:T(8,128)S(1)}, f32[192,1536]{1,0:T(8,128)S(1)}, u32[]{:S(2)}, u32[]{:S(2)}) collective-permute-start(f32[192,1536]{1,0:T(8,128)S(1)} %get-tuple-element.203.refs_1_), channel_id=1, source_target_pairs={{0,4},{2,6},{4,0},{6,2},{8,12},{10,14},{12,8},{14,10},{16,20},{18,... | collective-permute-start | bytes 3538952 | tf_op jit(solution)/shard_map/ppermute | solution.py:437
  45.3 28.1 %collective-permute-start.12 = (f32[192,1536]{1,0:T(8,128)S(1)}, f32[192,1536]{1,0:T(8,128)S(1)}, u32[]{:S(2)}, u32[]{:S(2)}) collective-permute-start(f32[192,1536]{1,0:T(8,128)S(1)} %get-tuple-element.207.refs_1_), channel_id=1, source_target_pairs={{0,8},{2,10},{4,12},{6,14},{8,0},{10,2},{12,4},{14,6},{16,24},{18,... | collective-permute-start | bytes 3538952 | tf_op jit(solution)/shard_map/ppermute | solution.py:437
  47.0 29.7 %collective-permute-start.13 = (f32[256,768]{1,0:T(8,128)S(1)}, f32[256,768]{1,0:T(8,128)S(1)}, u32[]{:S(2)}, u32[]{:S(2)}) collective-permute-start(f32[256,768]{1,0:T(8,128)S(1)} %get-tuple-element.209.refs_4_), channel_id=1, source_target_pairs={{0,1},{1,0},{2,3},{3,2},{4,5},{5,4},{6,7},{7,6},{8,9},{9,8},{10,11... | collective-permute-start | bytes 2359304 | tf_op jit(solution)/shard_map/ppermute | solution.py:441
  47.5 61.9 %collective-permute-start.20 = (f32[512,768]{1,0:T(8,128)S(1)}, f32[512,768]{1,0:T(8,128)S(1)}, u32[]{:S(2)}, u32[]{:S(2)}) collective-permute-start(f32[512,768]{1,0:T(8,128)S(1)} %mlp.1.refs_1_), channel_id=1, source_target_pairs={{0,1},{1,0},{2,3},{3,2},{4,5},{5,4},{6,7},{7,6},{8,9},{9,8},{10,11... | collective-permute-start | bytes 4718600 | tf_op jit(solution)/shard_map/ppermute | solution.py:441
  73.5 14.6 %collective-permute-start.15 = (f32[96,1536]{1,0:T(8,128)S(1)}, f32[96,1536]{1,0:T(8,128)S(1)}, u32[]{:S(2)}, u32[]{:S(2)}) collective-permute-start(f32[96,1536]{1,0:T(8,128)S(1)} %get-tuple-element.228.refs_3_), channel_id=1, source_target_pairs={{0,4},{2,6},{4,0},{6,2},{8,12},{10,14},{12,8},{14,10},{16,20},{18,... | collective-permute-start | bytes 1769480 | tf_op jit(solution)/shard_map/ppermute | solution.py:437
  75.1 14.3 %collective-permute-start.14 = (f32[96,1536]{1,0:T(8,128)S(1)}, f32[96,1536]{1,0:T(8,128)S(1)}, u32[]{:S(2)}, u32[]{:S(2)}) collective-permute-start(f32[96,1536]{1,0:T(8,128)S(1)} %get-tuple-element.227.refs_2_), channel_id=1, source_target_pairs={{0,8},{2,10},{4,12},{6,14},{8,0},{10,2},{12,4},{14,6},{16,24},{18,... | collective-permute-start | bytes 1769480 | tf_op jit(solution)/shard_map/ppermute | solution.py:437
  82.2 7.2 %collective-permute-start.17 = (f32[192,768]{1,0:T(8,128)S(1)}, f32[192,768]{1,0:T(8,128)S(1)}, u32[]{:S(2)}, u32[]{:S(2)}) collective-permute-start(f32[192,768]{1,0:T(8,128)S(1)} %get-tuple-element.231), channel_id=1, source_target_pairs={{0,2},{2,0},{4,6},{6,4},{8,10},{10,8},{12,14},{14,12},{16,18},{18,... | collective-permute-start | bytes 1769480 | tf_op jit(solution)/shard_map/ppermute | solution.py:437
  82.2 7.8 %collective-permute-start.16 = (f32[208,768]{1,0:T(8,128)S(1)}, f32[208,768]{1,0:T(8,128)S(1)}, u32[]{:S(2)}, u32[]{:S(2)}) collective-permute-start(f32[208,768]{1,0:T(8,128)S(1)} %get-tuple-element.218), channel_id=1, source_target_pairs={{0,2},{2,0},{4,6},{6,4},{8,10},{10,8},{12,14},{14,12},{16,18},{18,... | collective-permute-start | bytes 1916936 | tf_op jit(solution)/shard_map/ppermute | solution.py:437
  89.4 52.9 %collective-permute-start.26 = (f32[512,768]{1,0:T(8,128)S(1)}, f32[512,768]{1,0:T(8,128)S(1)}, u32[]{:S(2)}, u32[]{:S(2)}) collective-permute-start(f32[512,768]{1,0:T(8,128)S(1)} %get-tuple-element.254.own), channel_id=1, source_target_pairs={{0,1},{1,0},{2,3},{3,2},{4,5},{5,4},{6,7},{7,6},{8,9},{9,8},{10,11... | collective-permute-start | bytes 4718600 | tf_op jit(solution)/shard_map/ppermute | solution.py:441
  90.8 19.7 %collective-permute-start.21 = (f32[208,768]{1,0:T(8,128)S(1)}, f32[208,768]{1,0:T(8,128)S(1)}, u32[]{:S(2)}, u32[]{:S(2)}) collective-permute-start(f32[208,768]{1,0:T(8,128)S(1)} %get-tuple-element.239.refs_1_), channel_id=1, source_target_pairs={{0,4},{2,6},{4,0},{6,2},{8,12},{10,14},{12,8},{14,10},{16,20},{18,... | collective-permute-start | bytes 1916936 | tf_op jit(solution)/shard_map/ppermute | solution.py:437
  92.3 28.9 %collective-permute-start.22 = (f32[192,768]{1,0:T(8,128)S(1)}, f32[192,768]{1,0:T(8,128)S(1)}, u32[]{:S(2)}, u32[]{:S(2)}) collective-permute-start(f32[192,768]{1,0:T(8,128)S(1)} %get-tuple-element.242.refs_1_), channel_id=1, source_target_pairs={{0,8},{2,10},{4,12},{6,14},{8,0},{10,2},{12,4},{14,6},{16,24},{18,... | collective-permute-start | bytes 1769480 | tf_op jit(solution)/shard_map/ppermute | solution.py:437
  93.9 28.5 %collective-permute-start.23 = (f32[96,1536]{1,0:T(8,128)S(1)}, f32[96,1536]{1,0:T(8,128)S(1)}, u32[]{:S(2)}, u32[]{:S(2)}) collective-permute-start(f32[96,1536]{1,0:T(8,128)S(1)} %get-tuple-element.246), channel_id=1, source_target_pairs={{0,16},{2,18},{4,20},{6,22},{8,24},{10,26},{12,28},{14,30},{16,0},... | collective-permute-start | bytes 1769480 | tf_op jit(solution)/shard_map/ppermute | solution.py:437
  110.6 16.8 %collective-permute-start.24 = (f32[112,768]{1,0:T(8,128)S(1)}, f32[112,768]{1,0:T(8,128)S(1)}, u32[]{:S(2)}, u32[]{:S(2)}) collective-permute-start(f32[112,768]{1,0:T(8,128)S(1)} %get-tuple-element.249.refs_1_), channel_id=1, source_target_pairs={{0,8},{2,10},{4,12},{6,14},{8,0},{10,2},{12,4},{14,6},{16,24},{18,... | collective-permute-start | bytes 1032200 | tf_op jit(solution)/shard_map/ppermute | solution.py:437
  121.2 8.9 %collective-permute-start.25 = (f32[96,768]{1,0:T(8,128)S(1)}, f32[96,768]{1,0:T(8,128)S(1)}, u32[]{:S(2)}, u32[]{:S(2)}) collective-permute-start(f32[96,768]{1,0:T(8,128)S(1)} %get-tuple-element.252.refs_1_), channel_id=1, source_target_pairs={{0,4},{2,6},{4,0},{6,2},{8,12},{10,14},{12,8},{14,10},{16,20},{18,... | collective-permute-start | bytes 884744 | tf_op jit(solution)/shard_map/ppermute | solution.py:437
  127.5 16.7 %collective-permute-start.27 = (f32[64,768]{1,0:T(8,128)S(1)}, f32[64,768]{1,0:T(8,128)S(1)}, u32[]{:S(2)}, u32[]{:S(2)}) collective-permute-start(f32[64,768]{1,0:T(8,128)S(1)} %get-tuple-element.259.sent), channel_id=1, source_target_pairs={{0,16},{2,18},{4,20},{6,22},{8,24},{10,26},{12,28},{14,30},{16,0},... | collective-permute-start | bytes 589832 | tf_op jit(solution)/shard_map/ppermute | solution.py:437
  130.2 15.6 %collective-permute-start.28 = (f32[48,768]{1,0:T(8,128)S(1)}, f32[48,768]{1,0:T(8,128)S(1)}, u32[]{:S(2)}, u32[]{:S(2)}) collective-permute-start(f32[48,768]{1,0:T(8,128)S(1)} %get-tuple-element.265), channel_id=1, source_target_pairs={{0,16},{2,18},{4,20},{6,22},{8,24},{10,26},{12,28},{14,30},{16,0},... | collective-permute-start | bytes 442376 | tf_op jit(solution)/shard_map/ppermute | solution.py:437
  (21 other events, 173.7 us)

commit v6 on v5

--- a/solution.py
+++ b/solution.py
@@ -94,17 +94,20 @@
 
 
 def front_kernel(*refs, length, seqs, crops):
-    sources, table, held = refs[:4], refs[4], refs[5:9]
-    first_out, q, k, v, lse = refs[9:14]
-    outs, sems = refs[14:-1], refs[-1]
+    sources, count = refs[:5], 5 + seqs
+    targets, held, kept, sems = refs[5 : 5 + count], refs[5 + count : 10 + count], refs[10 + count : -1], refs[-1]
     copies = copies_of(sources, held, sems)
-    tokens, w_q, w_k, w_v = held
+    tokens, table, w_q, w_k, w_v = held
+    first_out, q, k, v, lse, *outs = kept
+    stores = [pltpu.make_async_copy(a, b, sems.at[5 + i]) for i, (a, b) in enumerate(zip(kept, targets))]
     copies[0].wait()
     unit, _ = unit_rows(tokens[...].astype(HIGH))
+    copies[1].wait()
     local, width = w_q.shape[1], tokens.shape[1]
     first = (unit * row(table, GAIN_ATTN, width) + row(table, SHIFT_ATTN, width)).astype(LOW)
     first_out[...] = first
-    for copy in copies[1:]:
+    stores[0].start()
+    for copy in copies[2:]:
         copy.wait()
     q_all = plain_dot(first, w_q[...]) + row(table, BIAS_Q, local)
     q_all = (q_all.astype(LOW) * 0.125).astype(LOW)
@@ -113,6 +116,8 @@
     q[...] = q_all
     k[...] = k_all
     v[...] = v_all
+    for store in stores[1:4]:
+        store.start()
     low_half, masks = half_masks()
     for s, o in enumerate(outs):
         rows = slice(s * length, (s + 1) * length)
@@ -131,6 +136,10 @@
                 h = 2 * t + half
                 lse[rows, h : h + 1] = top + jnp.log(total)
             o[:, at] = jnp.where(low_half, got[0], got[1])
+        stores[5 + s].start()
+    stores[4].start()
+    for store in stores:
+        store.wait()
 
 
 def relative_rows(here, width, count, bits):
@@ -343,6 +352,13 @@
         outs[0][size:, :] = refs[-pieces - 1][...]
 
 
+def part_kernel(*refs, plan, start, added):
+    out = refs[-1]
+    at = slice(start, start + out.shape[0])
+    for columns, value in products(plan, refs, at):
+        out[:, columns] = value + refs[-2][:, columns] if added else value
+
+
 def near_kernel(*refs, plan, pieces, small):
     outs, got = refs[-2:], refs[-2 - pieces - small :]
     half = outs[0].shape[0]
@@ -410,7 +426,7 @@
         self.last = None
 
     def __call__(
-        self, kernel, name, outs, args, scratch=(), limit=12, smem=0, whole=0, tie=0, alias=None, cost=0
+        self, kernel, name, outs, args, scratch=(), limit=12, smem=0, whole=(), tie=0, alias=None, cost=0, out_whole=False
     ):
         args = list(args)
         if self.last is not None:
@@ -423,7 +439,7 @@
             + [pl.BlockSpec(memory_space=pl.ANY) if i in whole else VMEM for i in range(smem, len(args))]
             if whole
             else [pl.BlockSpec(memory_space=pltpu.SMEM)] * smem + [VMEM] * (len(args) - smem),
-            out_specs=[VMEM] * len(outs),
+            out_specs=[pl.BlockSpec(memory_space=pl.ANY) if out_whole else VMEM] * len(outs),
             scratch_shapes=list(scratch),
             input_output_aliases=alias or {},
             compiler_params=pltpu.CompilerParams(vmem_limit_bytes=limit << 20),
@@ -485,6 +501,22 @@
         outs = self.shapes(self.rows, self.rows + self.extra)
         self.keep, self.sent = self.steps(kernel, "near", outs, held)
         self.got = send(self.sent, self.bits[1], self.count)
+
+    def part(self, start, added):
+        kernel = partial(part_kernel, plan=self.plan, start=start * self.rows // 2, added=len(added))
+        outs = self.shapes(self.rows // 2)
+        return self.steps(kernel, "part", outs, self.arrays + added)[0]
+
+    def far_part(self, sent):
+        return send(self.part(2 + sent, []), self.bits[0], self.count)
+
+    def near_sent(self, got):
+        self.sent = self.part(1, [got])
+        self.got = send(self.sent, self.bits[1], self.count)
+
+    def near_keep(self, got):
+        self.keep = self.part(0, [got])
+        self.rows //= 2
 
     def rest(self):
         while self.at + 1 < len(self.bits):
@@ -587,21 +619,21 @@
     def like(*arrays):
         return [(a.shape, a.dtype) for a in arrays]
 
-    front = steps(
+    loaded = [tokens, table, w_query, w_key, w_value]
+    made = [((rows, width), LOW)] + [((rows, local), LOW)] * 3
+    made += [((rows, 128), HIGH)] + [((length, local), HIGH)] * seqs
+    first, query, key_rows, value_rows, log_total, *mixed = steps(
         partial(front_kernel, length=length, seqs=seqs, crops=crops),
         "front",
-        like(tokens, w_query, w_key, w_value)
-        + [((rows, width), LOW)]
-        + [((rows, local), LOW)] * 3
-        + [((rows, 128), HIGH)]
-        + [((length, local), HIGH)] * seqs,
-        [tokens, w_query, w_key, w_value, table],
-        scratch=[pltpu.SemaphoreType.DMA((4,))],
-        whole=range(4),
+        made,
+        loaded,
+        scratch=[pltpu.VMEM(*v) for v in like(*loaded) + made]
+        + [pltpu.SemaphoreType.DMA((len(loaded) + len(made),))],
+        whole=range(5),
+        out_whole=True,
+        tie=1,
         limit=58,
     )
-    tokens, w_query, w_key, w_value, first, query, key_rows, value_rows, log_total = front[:9]
-    mixed = list(front[9:])
     mixed_other = [swap(o) for o in mixed]
 
     got, _ = lax.optimization_barrier((got, first))
@@ -665,12 +697,13 @@
 
     down = Scatter(steps, count, orders[0], [(cot_a, active)])
     up = Scatter(steps, count, orders[1], [(a2_b, g_pre)])
-    down.far()
-    up.far()
+    parts = [one.far_part(sent) for sent in (1, 0) for one in (down, up)]
+    down.near_sent(parts[0])
+    up.near_sent(parts[1])
     mlp_part = steps(mlp_kernel, "mlp", [((rows, width), HIGH)], [w_down] + active, tie=1)[0]
     mlp_other = swap(mlp_part)
-    down.near()
-    up.near()
+    down.near_keep(parts[2])
+    up.near_keep(parts[3])
     g_hidden, gh_b, g_qk, g_val, carried = [], [], [], [], [bias_sum, cot_sum]
     for s in range(seqs):
         if s == seqs - 1:
@@ -725,13 +758,6 @@
         [table, tokens, g_first] + g_hidden,
         tie=2,
     )
-    grad_tokens = steps(
-        partial(last_kernel, length=length),
-        "last",
-        [((rows, width), HIGH)],
-        [table, base, unit, scale, first_other],
-        tie=1,
-    )[0]
     size = width // count
     (
         done_bias_q,
@@ -756,6 +782,13 @@
     gains_other = swap(gains)
     grad_w_q, grad_w_k = finish([heads], heads.got)
     grad_w_v, w_out_t = finish([others], others.got)
+    grad_tokens = steps(
+        partial(last_kernel, length=length),
+        "last",
+        [((rows, width), HIGH)],
+        [table, base, unit, scale, first_other],
+        tie=1,
+    )[0]
     done_gain_attn, done_shift_attn = steps(
         gain_kernel, "gains", [((size,), HIGH)] * 2, [gains, gains_other]
     )

time: 149 us -> 145 us (0.973)
  waiting for transfers between devices: 69.8 us -> 65.1 us
    ppermute x8, waiting for transfers between devices: 39.6 us -> 36.3 us  [swap(): return lax.ppermute(values, 'mp', [(0, 1), (1, 0)])]
    pallas_call x33 -> x37, Pallas kernels: 45.9 us -> 45.8 us  [__call__(): pl.pallas_call(kernel, name=name, out_shape=[jax.ShapeDtypeStruct(s, d) f...]
  transfers between devices with their start and end apart: 30 -> 30, of which waited for: 15 -> 14; matrix products, arithmetic and copies ran while one was open for 0% -> 0% of each run, Pallas kernels for 26% -> 27%
where the time goes in v6:
time: 145 us
  waiting for transfers between devices  65.1 us (45%)
  Pallas kernels  45.8 us (32%)
  starting transfers between devices  29.6 us (20%)
  local copies, waits for them, and re-layouts  2.98 us (2%)
    pallas_call x37, Pallas kernels, __call__(): pl.pallas_call(kernel, name=name, out_shape=[jax.ShapeDtypeStruct(s, d) f...  45.8 us
    ppermute x8, waiting for transfers between devices, swap(): return lax.ppermute(values, 'mp', [(0, 1), (1, 0)])  36.3 us
    ppermute x22, waiting for transfers between devices, send(): return lax.ppermute(values, 'dp', [(i, i ^ 1 << bit) for i in range(count)])  28.8 us
    ppermute x22, starting transfers between devices, send(): return lax.ppermute(values, 'dp', [(i, i ^ 1 << bit) for i in range(count)])  21.7 us
    ppermute x8, starting transfers between devices, swap(): return lax.ppermute(values, 'mp', [(0, 1), (1, 0)])  7.94 us
    unnamed x30, local copies, waits for them, and re-layouts  2.98 us
  transfers between devices with their start and end apart: 30, of which 14 were waited for; matrix products, arithmetic and copies ran while one was open for 0% of the time, Pallas kernels for 27%

profile of v6, /device:TPU:0, one launch (start us, length us, event | category | flops | bytes accessed | tf_op | source)
XLA Modules:
  0.0 144.5 jit_solution(5687726163883046499)
XLA Ops:
  0.7 1.8 %load.1 = (f32[96,768]{1,0:T(8,128)}, f32[12,768]{1,0:T(8,128)}) custom-call(s32[1]{0:T(128)} %bitcast.here, bf16[384,768]{1,0:T(8,128)(2,1)} %refs_3_.5, s32[2,256]{1,0:T(2,128)} %crops.1, f32[768]{0:T(1024)} %refs_0_.6, f32[768]{0:T(1024)} %refs_1_.2, f32[384]{0:T(512)} %refs_2_.3, f32[384]{0:T(512)} %refs_3_.3, f32[768]{0:T(1024)} %refs_4_.2, ...), custom_call_target="tpu_custom_call" | custom-call | flops 1000 | bytes 1000 | tf_op jit(solution)/shard_map/load/pallas_call | solution.py:434
  2.4 3.0 %collective-permute-start = (f32[96,768]{1,0:T(8,128)}, f32[96,768]{1,0:T(8,128)S(1)}, u32[]{:S(2)}, u32[]{:S(2)}) collective-permute-start(f32[96,768]{1,0:T(8,128)} %get-tuple-element.142), channel_id=1, source_target_pairs={{0,1},{1,0},{2,3},{3,2},{4,5},{5,4},{6,7},{7,6},{8,9},{9,8},{10,11... | collective-permute-start | bytes 884744 | tf_op jit(solution)/shard_map/ppermute | solution.py:457
  5.4 6.1 %front.1 = (bf16[512,768]{1,0:T(8,128)(2,1)}, bf16[512,384]{1,0:T(8,128)(2,1)}, bf16[512,384]{1,0:T(8,128)(2,1)}, bf16[512,384]{1,0:T(8,128)(2,1)}, f32[512,128]...) custom-call(bf16[512,768]{1,0:T(8,128)(2,1)} %tokens.1, ...), custom_call_target="tpu_custom_call" | custom-call | flops 1000 | bytes 1000 | tf_op jit(solution)/shard_map/front/pallas_call | solution.py:434
  12.7 1.8 %collective-permute-start.3 = (f32[96,768]{1,0:T(8,128)S(1)}, f32[96,768]{1,0:T(8,128)S(1)}, u32[]{:S(2)}, u32[]{:S(2)}) collective-permute-start(f32[96,768]{1,0:T(8,128)S(1)} %collective-permute-done.refs_0_), channel_id=1, source_target_pairs={{0,4},{2,6},{4,0},{6,2},{8,12},{10,14},{12,8},{14,10},{16,20},{18,... | collective-permute-start | bytes 884744 | tf_op jit(solution)/shard_map/ppermute | solution.py:453
  17.1 3.7 %turn.1 = (bf16[512,768]{1,0:T(8,128)(2,1)S(1)}, bf16[768,1536]{1,0:T(8,128)(2,1)S(1)}, bf16[384,768]{1,0:T(8,128)(2,1)S(1)}, bf16[768,768]{1,0:T(8,128)(2,1)S(1...) custom-call(s32[1]{0:T(128)} %bitcast.here, ...), custom_call_target="tpu_custom_call" | custom-call | flops 1000 | bytes 1000 | tf_op jit(solution)/shard_map/turn/pallas_call | solution.py:434
  21.4 2.5 %collective-permute-done.1.values = f32[256,384]{1,0:T(8,128)S(1)} collective-permute-done((f32[256,384]{1,0:T(8,128)}, f32[256,384]{1,0:T(8,128)S(1)}, u32[]{:S(2)}, u32[]{:S(2)}) %collective-permute-start.1) | collective-permute-done | bytes 393248 | tf_op jit(solution)/shard_map/ppermute | solution.py:457
  25.9 4.2 %middle.2 = (f32[256,768]{1,0:T(8,128)S(1)}, bf16[768,256]{1,0:T(8,128)(2,1)S(1)}, bf16[256,1536]{1,0:T(8,128)(2,1)S(1)}, bf16[256,1536]{1,0:T(8,128)(2,1)S(1)},...) custom-call(bf16[512,768]{1,0:T(8,128)(2,1)S(1)} %copy-done.1, f32[256,384]{1,0:T(8,128)S(1)} %copy-done.2, ...), custom_call_target="tpu_custom_call" | custom-call | flops 1000 | bytes 1000 | tf_op jit(solution)/shard_map/middle/pallas_call | solution.py:434
  30.9 4.3 %middle.3 = (f32[256,768]{1,0:T(8,128)S(1)}, bf16[768,256]{1,0:T(8,128)(2,1)S(1)}, bf16[256,1536]{1,0:T(8,128)(2,1)S(1)}, bf16[256,1536]{1,0:T(8,128)(2,1)S(1)},...) custom-call(bf16[512,768]{1,0:T(8,128)(2,1)S(1)} %copy-done.1, f32[256,384]{1,0:T(8,128)S(1)} %copy-done.3, ...), custom_call_target="tpu_custom_call" | custom-call | flops 1000 | bytes 1000 | tf_op jit(solution)/shard_map/middle/pallas_call | solution.py:434
  39.2 1.7 %collective-permute-start.11 = (f32[192,1536]{1,0:T(8,128)S(1)}, f32[192,1536]{1,0:T(8,128)S(1)}, u32[]{:S(2)}, u32[]{:S(2)}) collective-permute-start(f32[192,1536]{1,0:T(8,128)S(1)} %part.12.refs_1_), channel_id=1, source_target_pairs={{0,4},{2,6},{4,0},{6,2},{8,12},{10,14},{12,8},{14,10},{16,20},{18,... | collective-permute-start | bytes 3538952 | tf_op jit(solution)/shard_map/ppermute | solution.py:453
  41.7 1.6 %collective-permute-start.12 = (f32[192,1536]{1,0:T(8,128)S(1)}, f32[192,1536]{1,0:T(8,128)S(1)}, u32[]{:S(2)}, u32[]{:S(2)}) collective-permute-start(f32[192,1536]{1,0:T(8,128)S(1)} %part.13.refs_1_), channel_id=1, source_target_pairs={{0,8},{2,10},{4,12},{6,14},{8,0},{10,2},{12,4},{14,6},{16,24},{18,... | collective-permute-start | bytes 3538952 | tf_op jit(solution)/shard_map/ppermute | solution.py:453
  47.8 10.9 %collective-permute-done.10.refs_5_ = f32[256,768]{1,0:T(8,128)S(1)} collective-permute-done((f32[256,768]{1,0:T(8,128)S(1)}, f32[256,768]{1,0:T(8,128)S(1)}, u32[]{:S(2)}, u32[]{:S(2)}) %collective-permute-start.10) | collective-permute-done | bytes 786464 | tf_op jit(solution)/shard_map/ppermute | solution.py:457
  58.8 4.9 %back.2 = (f32[256,768]{1,0:T(8,128)S(1)}, bf16[768,256]{1,0:T(8,128)(2,1)S(1)}, bf16[256,768]{1,0:T(8,128)(2,1)S(1)}, bf16[256,384]{1,0:T(8,128)(2,1)S(1)}, f32...) custom-call(bf16[512,768]{1,0:T(8,128)(2,1)S(1)} %copy-done.1, f32[12,768]{1,0:T(8,128)S(1)} %copy-done.8, ...), custom_call_target="tpu_custom_call" | custom-call | flops 6000001024 | bytes 1000 | tf_op jit(solution)/shard_map/back/pallas_call | solution.py:434
  63.6 3.5 %collective-permute-done.11.refs_2_ = f32[192,1536]{1,0:T(8,128)S(1)} collective-permute-done((f32[192,1536]{1,0:T(8,128)S(1)}, f32[192,1536]{1,0:T(8,128)S(1)}, u32[]{:S(2)}, u32[]{:S(2)}) %collective-permute-start.11) | collective-permute-done | bytes 1179680 | tf_op jit(solution)/shard_map/ppermute | solution.py:453
  67.2 1.9 %collective-permute-done.12.refs_2_ = f32[192,1536]{1,0:T(8,128)S(1)} collective-permute-done((f32[192,1536]{1,0:T(8,128)S(1)}, f32[192,1536]{1,0:T(8,128)S(1)}, u32[]{:S(2)}, u32[]{:S(2)}) %collective-permute-start.12) | collective-permute-done | bytes 1179680 | tf_op jit(solution)/shard_map/ppermute | solution.py:453
  72.3 3.3 %collective-permute-done.13.refs_5_ = f32[256,768]{1,0:T(8,128)S(1)} collective-permute-done((f32[256,768]{1,0:T(8,128)S(1)}, f32[256,768]{1,0:T(8,128)S(1)}, u32[]{:S(2)}, u32[]{:S(2)}) %collective-permute-start.13) | collective-permute-done | bytes 786464 | tf_op jit(solution)/shard_map/ppermute | solution.py:457
  75.6 4.9 %back.3 = (f32[256,768]{1,0:T(8,128)S(1)}, bf16[768,256]{1,0:T(8,128)(2,1)S(1)}, bf16[256,768]{1,0:T(8,128)(2,1)S(1)}, bf16[256,384]{1,0:T(8,128)(2,1)S(1)}, f32...) custom-call(bf16[512,768]{1,0:T(8,128)(2,1)S(1)} %copy-done.1, f32[12,768]{1,0:T(8,128)S(1)} %copy-done.8, ...), custom_call_target="tpu_custom_call" | custom-call | flops 1000 | bytes 1000 | tf_op jit(solution)/shard_map/back/pallas_call | solution.py:434
  88.0 1.6 %collective-permute-start.22 = (f32[192,768]{1,0:T(8,128)S(1)}, f32[192,768]{1,0:T(8,128)S(1)}, u32[]{:S(2)}, u32[]{:S(2)}) collective-permute-start(f32[192,768]{1,0:T(8,128)S(1)} %get-tuple-element.227.refs_1_), channel_id=1, source_target_pairs={{0,8},{2,10},{4,12},{6,14},{8,0},{10,2},{12,4},{14,6},{16,24},{18,... | collective-permute-start | bytes 1769480 | tf_op jit(solution)/shard_map/ppermute | solution.py:453
  89.6 2.6 %collective-permute-start.23 = (f32[96,1536]{1,0:T(8,128)S(1)}, f32[96,1536]{1,0:T(8,128)S(1)}, u32[]{:S(2)}, u32[]{:S(2)}) collective-permute-start(f32[96,1536]{1,0:T(8,128)S(1)} %get-tuple-element.231), channel_id=1, source_target_pairs={{0,16},{2,18},{4,20},{6,22},{8,24},{10,26},{12,28},{14,30},{16,0},... | collective-permute-start | bytes 1769480 | tf_op jit(solution)/shard_map/ppermute | solution.py:453
  92.2 17.1 %collective-permute-done.20.refs_2_ = f32[512,768]{1,0:T(8,128)S(1)} collective-permute-done((f32[512,768]{1,0:T(8,128)S(1)}, f32[512,768]{1,0:T(8,128)S(1)}, u32[]{:S(2)}, u32[]{:S(2)}) %collective-permute-start.20) | collective-permute-done | bytes 1572896 | tf_op jit(solution)/shard_map/ppermute | solution.py:457
  112.1 4.6 %collective-permute-done.22.refs_2_ = f32[192,768]{1,0:T(8,128)S(1)} collective-permute-done((f32[192,768]{1,0:T(8,128)S(1)}, f32[192,768]{1,0:T(8,128)S(1)}, u32[]{:S(2)}, u32[]{:S(2)}) %collective-permute-start.22) | collective-permute-done | bytes 589856 | tf_op jit(solution)/shard_map/ppermute | solution.py:453
  118.5 4.7 %collective-permute-done.24.refs_2_ = f32[112,768]{1,0:T(8,128)S(1)} collective-permute-done((f32[112,768]{1,0:T(8,128)S(1)}, f32[112,768]{1,0:T(8,128)S(1)}, u32[]{:S(2)}, u32[]{:S(2)}) %collective-permute-start.24) | collective-permute-done | bytes 344096 | tf_op jit(solution)/shard_map/ppermute | solution.py:453
  123.3 2.7 %collective-permute-start.26 = (f32[64,768]{1,0:T(8,128)S(1)}, f32[64,768]{1,0:T(8,128)S(1)}, u32[]{:S(2)}, u32[]{:S(2)}) collective-permute-start(f32[64,768]{1,0:T(8,128)S(1)} %get-tuple-element.242.sent), channel_id=1, source_target_pairs={{0,16},{2,18},{4,20},{6,22},{8,24},{10,26},{12,28},{14,30},{16,0},... | collective-permute-start | bytes 589832 | tf_op jit(solution)/shard_map/ppermute | solution.py:453
  127.4 11.3 %collective-permute-done.26.got.refs_1_ = f32[64,768]{1,0:T(8,128)S(1)} collective-permute-done((f32[64,768]{1,0:T(8,128)S(1)}, f32[64,768]{1,0:T(8,128)S(1)}, u32[]{:S(2)}, u32[]{:S(2)}) %collective-permute-start.26) | collective-permute-done | bytes 196640 | tf_op jit(solution)/shard_map/ppermute | solution.py:453
  142.2 1.9 %last.1 = f32[512,768]{1,0:T(8,128)} custom-call(f32[12,768]{1,0:T(8,128)S(1)} %copy-done.8, f32[512,768]{1,0:T(8,128)S(1)} %get-tuple-element.249.base, f32[512,768]{1,0:T(8,128)S(1)} %get-tuple-element.250.unit, f32[512,1]{1,0:T(8,128)S(1)} %get-tuple-element.251.scale, f32[512,768]{1,0:T(8,128)S(1)} %collective-permute-done.28.other), custom_call_target="tpu_custom_call" | custom-call | flops 1000 | bytes 1000 | tf_op jit(solution)/shard_map/last/pallas_call | solution.py:434
  (103 shorter events, 36.9 us)
Async XLA Ops:
  2.4 10.2 %collective-permute-start = (f32[96,768]{1,0:T(8,128)}, f32[96,768]{1,0:T(8,128)S(1)}, u32[]{:S(2)}, u32[]{:S(2)}) collective-permute-start(f32[96,768]{1,0:T(8,128)} %get-tuple-element.142), channel_id=1, source_target_pairs={{0,1},{1,0},{2,3},{3,2},{4,5},{5,4},{6,7},{7,6},{8,9},{9,8},{10,11... | collective-permute-start | bytes 884744 | tf_op jit(solution)/shard_map/ppermute | solution.py:457
  11.6 12.3 %collective-permute-start.1 = (f32[256,384]{1,0:T(8,128)}, f32[256,384]{1,0:T(8,128)S(1)}, u32[]{:S(2)}, u32[]{:S(2)}) collective-permute-start(f32[256,384]{1,0:T(8,128)} %get-tuple-element.153.refs_1_.refs_6_), channel_id=1, source_target_pairs={{0,1},{1,0},{2,3},{3,2},{4,5},{5,4},{6,7},{7,6},{8,9},{9,8},{10,11... | collective-permute-start | bytes 1179656 | tf_op jit(solution)/shard_map/ppermute | solution.py:457
  12.7 8.2 %collective-permute-start.3 = (f32[96,768]{1,0:T(8,128)S(1)}, f32[96,768]{1,0:T(8,128)S(1)}, u32[]{:S(2)}, u32[]{:S(2)}) collective-permute-start(f32[96,768]{1,0:T(8,128)S(1)} %collective-permute-done.refs_0_), channel_id=1, source_target_pairs={{0,4},{2,6},{4,0},{6,2},{8,12},{10,14},{12,8},{14,10},{16,20},{18,... | collective-permute-start | bytes 884744 | tf_op jit(solution)/shard_map/ppermute | solution.py:453
  14.4 16.4 %collective-permute-start.5 = (f32[256,384]{1,0:T(8,128)}, f32[256,384]{1,0:T(8,128)S(1)}, u32[]{:S(2)}, u32[]{:S(2)}) collective-permute-start(f32[256,384]{1,0:T(8,128)} %get-tuple-element.161.refs_1_.refs_7_), channel_id=1, source_target_pairs={{0,1},{1,0},{2,3},{3,2},{4,5},{5,4},{6,7},{7,6},{8,9},{9,8},{10,11... | collective-permute-start | bytes 1179656 | tf_op jit(solution)/shard_map/ppermute | solution.py:457
  36.2 4.8 %collective-permute-start.7 = (f32[192,1536]{1,0:T(8,128)S(1)}, f32[192,1536]{1,0:T(8,128)S(1)}, u32[]{:S(2)}, u32[]{:S(2)}) collective-permute-start(f32[192,1536]{1,0:T(8,128)S(1)} %part.9), channel_id=1, source_target_pairs={{0,2},{2,0},{4,6},{6,4},{8,10},{10,8},{12,14},{14,12},{16,18},{18,... | collective-permute-start | bytes 3538952 | tf_op jit(solution)/shard_map/ppermute | solution.py:453
  37.2 6.1 %collective-permute-start.8 = (f32[192,1536]{1,0:T(8,128)S(1)}, f32[192,1536]{1,0:T(8,128)S(1)}, u32[]{:S(2)}, u32[]{:S(2)}) collective-permute-start(f32[192,1536]{1,0:T(8,128)S(1)} %part.10), channel_id=1, source_target_pairs={{0,2},{2,0},{4,6},{6,4},{8,10},{10,8},{12,14},{14,12},{16,18},{18,... | collective-permute-start | bytes 3538952 | tf_op jit(solution)/shard_map/ppermute | solution.py:453
  37.8 9.0 %collective-permute-start.9 = (f32[192,1536]{1,0:T(8,128)S(1)}, f32[192,1536]{1,0:T(8,128)S(1)}, u32[]{:S(2)}, u32[]{:S(2)}) collective-permute-start(f32[192,1536]{1,0:T(8,128)S(1)} %part.11), channel_id=1, source_target_pairs={{0,2},{2,0},{4,6},{6,4},{8,10},{10,8},{12,14},{14,12},{16,18},{18,... | collective-permute-start | bytes 3538952 | tf_op jit(solution)/shard_map/ppermute | solution.py:453
  38.3 20.4 %collective-permute-start.10 = (f32[256,768]{1,0:T(8,128)S(1)}, f32[256,768]{1,0:T(8,128)S(1)}, u32[]{:S(2)}, u32[]{:S(2)}) collective-permute-start(f32[256,768]{1,0:T(8,128)S(1)} %get-tuple-element.181.refs_4_), channel_id=1, source_target_pairs={{0,1},{1,0},{2,3},{3,2},{4,5},{5,4},{6,7},{7,6},{8,9},{9,8},{10,11... | collective-permute-start | bytes 2359304 | tf_op jit(solution)/shard_map/ppermute | solution.py:457
  39.2 27.9 %collective-permute-start.11 = (f32[192,1536]{1,0:T(8,128)S(1)}, f32[192,1536]{1,0:T(8,128)S(1)}, u32[]{:S(2)}, u32[]{:S(2)}) collective-permute-start(f32[192,1536]{1,0:T(8,128)S(1)} %part.12.refs_1_), channel_id=1, source_target_pairs={{0,4},{2,6},{4,0},{6,2},{8,12},{10,14},{12,8},{14,10},{16,20},{18,... | collective-permute-start | bytes 3538952 | tf_op jit(solution)/shard_map/ppermute | solution.py:453
  41.7 27.5 %collective-permute-start.12 = (f32[192,1536]{1,0:T(8,128)S(1)}, f32[192,1536]{1,0:T(8,128)S(1)}, u32[]{:S(2)}, u32[]{:S(2)}) collective-permute-start(f32[192,1536]{1,0:T(8,128)S(1)} %part.13.refs_1_), channel_id=1, source_target_pairs={{0,8},{2,10},{4,12},{6,14},{8,0},{10,2},{12,4},{14,6},{16,24},{18,... | collective-permute-start | bytes 3538952 | tf_op jit(solution)/shard_map/ppermute | solution.py:453
  43.3 32.3 %collective-permute-start.13 = (f32[256,768]{1,0:T(8,128)S(1)}, f32[256,768]{1,0:T(8,128)S(1)}, u32[]{:S(2)}, u32[]{:S(2)}) collective-permute-start(f32[256,768]{1,0:T(8,128)S(1)} %get-tuple-element.194.refs_4_), channel_id=1, source_target_pairs={{0,1},{1,0},{2,3},{3,2},{4,5},{5,4},{6,7},{7,6},{8,9},{9,8},{10,11... | collective-permute-start | bytes 2359304 | tf_op jit(solution)/shard_map/ppermute | solution.py:457
  46.8 62.5 %collective-permute-start.20 = (f32[512,768]{1,0:T(8,128)S(1)}, f32[512,768]{1,0:T(8,128)S(1)}, u32[]{:S(2)}, u32[]{:S(2)}) collective-permute-start(f32[512,768]{1,0:T(8,128)S(1)} %mlp.1.refs_1_), channel_id=1, source_target_pairs={{0,1},{1,0},{2,3},{3,2},{4,5},{5,4},{6,7},{7,6},{8,9},{9,8},{10,11... | collective-permute-start | bytes 4718600 | tf_op jit(solution)/shard_map/ppermute | solution.py:457
  69.2 14.3 %collective-permute-start.15 = (f32[96,1536]{1,0:T(8,128)S(1)}, f32[96,1536]{1,0:T(8,128)S(1)}, u32[]{:S(2)}, u32[]{:S(2)}) collective-permute-start(f32[96,1536]{1,0:T(8,128)S(1)} %get-tuple-element.213.refs_3_), channel_id=1, source_target_pairs={{0,4},{2,6},{4,0},{6,2},{8,12},{10,14},{12,8},{14,10},{16,20},{18,... | collective-permute-start | bytes 1769480 | tf_op jit(solution)/shard_map/ppermute | solution.py:453
  70.7 14.3 %collective-permute-start.14 = (f32[96,1536]{1,0:T(8,128)S(1)}, f32[96,1536]{1,0:T(8,128)S(1)}, u32[]{:S(2)}, u32[]{:S(2)}) collective-permute-start(f32[96,1536]{1,0:T(8,128)S(1)} %get-tuple-element.212.refs_2_), channel_id=1, source_target_pairs={{0,8},{2,10},{4,12},{6,14},{8,0},{10,2},{12,4},{14,6},{16,24},{18,... | collective-permute-start | bytes 1769480 | tf_op jit(solution)/shard_map/ppermute | solution.py:453
  81.1 4.2 %collective-permute-start.16 = (f32[208,768]{1,0:T(8,128)S(1)}, f32[208,768]{1,0:T(8,128)S(1)}, u32[]{:S(2)}, u32[]{:S(2)}) collective-permute-start(f32[208,768]{1,0:T(8,128)S(1)} %get-tuple-element.203), channel_id=1, source_target_pairs={{0,2},{2,0},{4,6},{6,4},{8,10},{10,8},{12,14},{14,12},{16,18},{18,... | collective-permute-start | bytes 1916936 | tf_op jit(solution)/shard_map/ppermute | solution.py:453
  85.0 57.2 %collective-permute-start.28 = (f32[512,768]{1,0:T(8,128)S(1)}, f32[512,768]{1,0:T(8,128)S(1)}, u32[]{:S(2)}, u32[]{:S(2)}) collective-permute-start(f32[512,768]{1,0:T(8,128)S(1)} %get-tuple-element.239.own), channel_id=1, source_target_pairs={{0,1},{1,0},{2,3},{3,2},{4,5},{5,4},{6,7},{7,6},{8,9},{9,8},{10,11... | collective-permute-start | bytes 4718600 | tf_op jit(solution)/shard_map/ppermute | solution.py:457
  86.1 24.3 %collective-permute-start.21 = (f32[208,768]{1,0:T(8,128)S(1)}, f32[208,768]{1,0:T(8,128)S(1)}, u32[]{:S(2)}, u32[]{:S(2)}) collective-permute-start(f32[208,768]{1,0:T(8,128)S(1)} %get-tuple-element.224.refs_1_), channel_id=1, source_target_pairs={{0,4},{2,6},{4,0},{6,2},{8,12},{10,14},{12,8},{14,10},{16,20},{18,... | collective-permute-start | bytes 1916936 | tf_op jit(solution)/shard_map/ppermute | solution.py:453
  88.0 28.8 %collective-permute-start.22 = (f32[192,768]{1,0:T(8,128)S(1)}, f32[192,768]{1,0:T(8,128)S(1)}, u32[]{:S(2)}, u32[]{:S(2)}) collective-permute-start(f32[192,768]{1,0:T(8,128)S(1)} %get-tuple-element.227.refs_1_), channel_id=1, source_target_pairs={{0,8},{2,10},{4,12},{6,14},{8,0},{10,2},{12,4},{14,6},{16,24},{18,... | collective-permute-start | bytes 1769480 | tf_op jit(solution)/shard_map/ppermute | solution.py:453
  89.6 28.1 %collective-permute-start.23 = (f32[96,1536]{1,0:T(8,128)S(1)}, f32[96,1536]{1,0:T(8,128)S(1)}, u32[]{:S(2)}, u32[]{:S(2)}) collective-permute-start(f32[96,1536]{1,0:T(8,128)S(1)} %get-tuple-element.231), channel_id=1, source_target_pairs={{0,16},{2,18},{4,20},{6,22},{8,24},{10,26},{12,28},{14,30},{16,0},... | collective-permute-start | bytes 1769480 | tf_op jit(solution)/shard_map/ppermute | solution.py:453
  110.5 12.8 %collective-permute-start.24 = (f32[112,768]{1,0:T(8,128)S(1)}, f32[112,768]{1,0:T(8,128)S(1)}, u32[]{:S(2)}, u32[]{:S(2)}) collective-permute-start(f32[112,768]{1,0:T(8,128)S(1)} %get-tuple-element.234.refs_1_), channel_id=1, source_target_pairs={{0,8},{2,10},{4,12},{6,14},{8,0},{10,2},{12,4},{14,6},{16,24},{18,... | collective-permute-start | bytes 1032200 | tf_op jit(solution)/shard_map/ppermute | solution.py:453
  116.8 9.1 %collective-permute-start.25 = (f32[96,768]{1,0:T(8,128)S(1)}, f32[96,768]{1,0:T(8,128)S(1)}, u32[]{:S(2)}, u32[]{:S(2)}) collective-permute-start(f32[96,768]{1,0:T(8,128)S(1)} %get-tuple-element.237.refs_1_), channel_id=1, source_target_pairs={{0,4},{2,6},{4,0},{6,2},{8,12},{10,14},{12,8},{14,10},{16,20},{18,... | collective-permute-start | bytes 884744 | tf_op jit(solution)/shard_map/ppermute | solution.py:453
  123.3 15.5 %collective-permute-start.26 = (f32[64,768]{1,0:T(8,128)S(1)}, f32[64,768]{1,0:T(8,128)S(1)}, u32[]{:S(2)}, u32[]{:S(2)}) collective-permute-start(f32[64,768]{1,0:T(8,128)S(1)} %get-tuple-element.242.sent), channel_id=1, source_target_pairs={{0,16},{2,18},{4,20},{6,22},{8,24},{10,26},{12,28},{14,30},{16,0},... | collective-permute-start | bytes 589832 | tf_op jit(solution)/shard_map/ppermute | solution.py:453
  126.0 14.7 %collective-permute-start.27 = (f32[48,768]{1,0:T(8,128)S(1)}, f32[48,768]{1,0:T(8,128)S(1)}, u32[]{:S(2)}, u32[]{:S(2)}) collective-permute-start(f32[48,768]{1,0:T(8,128)S(1)} %get-tuple-element.247), channel_id=1, source_target_pairs={{0,16},{2,18},{4,20},{6,22},{8,24},{10,26},{12,28},{14,30},{16,0},... | collective-permute-start | bytes 442376 | tf_op jit(solution)/shard_map/ppermute | solution.py:453
  139.3 4.7 %collective-permute-start.29 = (f32[8,128]{1,0:T(8,128)S(1)}, f32[8,128]{1,0:T(8,128)S(1)}, u32[]{:S(2)}, u32[]{:S(2)}) collective-permute-start(f32[8,128]{1,0:T(8,128)S(1)} %get-tuple-element.257.own), channel_id=1, source_target_pairs={{0,1},{1,0},{2,3},{3,2},{4,5},{5,4},{6,7},{7,6},{8,9},{9,8},{10,11... | collective-permute-start | bytes 12296 | tf_op jit(solution)/shard_map/ppermute | solution.py:457
  (21 other events, 138.2 us)

commit v7 on v6

--- a/solution.py
+++ b/solution.py
@@ -664,7 +664,7 @@
     hidden, a2_b, active, g_pre, second, carried = [], [], [], [], [], []
     for s in range(seqs):
         result = steps(
-            partial(middle_kernel, blocks=4, seq=s, length=length),
+            partial(middle_kernel, blocks=2, seq=s, length=length),
             "middle",
             [
                 ((length, width), HIGH),
@@ -738,6 +738,7 @@
     _, mlp_got = join(down, up)
     heads.near()
     others.near()
+    heads.step()
     block_out = steps(
         partial(out_kernel, seqs=seqs, length=length),
         "out",
@@ -746,7 +747,6 @@
         tie=1,
         cost=3 * 10**9,
     )[0]
-    heads.step()
     others.step()
     w_down_t, done_w_up = finish([down, up], mlp_got, 15 * 10**8)
     heads.rest()

time: 145 us -> 144 us (level)
  Pallas kernels: 45.8 us -> 44.3 us
    ppermute x22, waiting for transfers between devices: 28.8 us -> 40.2 us  [send(): return lax.ppermute(values, 'dp', [(i, i ^ 1 << bit) for i in range(count)])]
    ppermute x8, waiting for transfers between devices: 36.3 us -> 25.6 us  [swap(): return lax.ppermute(values, 'mp', [(0, 1), (1, 0)])]
    pallas_call x37, Pallas kernels: 45.8 us -> 44.3 us  [__call__(): pl.pallas_call(kernel, name=name, out_shape=[jax.ShapeDtypeStruct(s, d) f...]
  transfers between devices with their start and end apart: 30 -> 30, of which waited for: 14 -> 16; matrix products, arithmetic and copies ran while one was open for 0% -> 0% of each run, Pallas kernels for 27% -> 26%
where the time goes in v7:
time: 144 us
  waiting for transfers between devices  65.8 us (46%)
  Pallas kernels  44.3 us (31%)
  starting transfers between devices  29.6 us (21%)
  local copies, waits for them, and re-layouts  2.98 us (2%)
    pallas_call x37, Pallas kernels, __call__(): pl.pallas_call(kernel, name=name, out_shape=[jax.ShapeDtypeStruct(s, d) f...  44.3 us
    ppermute x22, waiting for transfers between devices, send(): return lax.ppermute(values, 'dp', [(i, i ^ 1 << bit) for i in range(count)])  40.2 us
    ppermute x8, waiting for transfers between devices, swap(): return lax.ppermute(values, 'mp', [(0, 1), (1, 0)])  25.6 us
    ppermute x22, starting transfers between devices, send(): return lax.ppermute(values, 'dp', [(i, i ^ 1 << bit) for i in range(count)])  21.9 us
    ppermute x8, starting transfers between devices, swap(): return lax.ppermute(values, 'mp', [(0, 1), (1, 0)])  7.79 us
    unnamed x30, local copies, waits for them, and re-layouts  2.98 us
  transfers between devices with their start and end apart: 30, of which 16 were waited for; matrix products, arithmetic and copies ran while one was open for 0% of the time, Pallas kernels for 26%

profile of v7, /device:TPU:0, one launch (start us, length us, event | category | flops | bytes accessed | tf_op | source)
XLA Modules:
  0.0 143.8 jit_solution(6302189551184030283)
XLA Ops:
  0.7 1.8 %load.1 = (f32[96,768]{1,0:T(8,128)}, f32[12,768]{1,0:T(8,128)}) custom-call(s32[1]{0:T(128)} %bitcast.here, bf16[384,768]{1,0:T(8,128)(2,1)} %refs_3_.5, s32[2,256]{1,0:T(2,128)} %crops.1, f32[768]{0:T(1024)} %refs_0_.6, f32[768]{0:T(1024)} %refs_1_.2, f32[384]{0:T(512)} %refs_2_.3, f32[384]{0:T(512)} %refs_3_.3, f32[768]{0:T(1024)} %refs_4_.2, ...), custom_call_target="tpu_custom_call" | custom-call | flops 1000 | bytes 1000 | tf_op jit(solution)/shard_map/load/pallas_call | solution.py:434
  2.4 3.0 %collective-permute-start = (f32[96,768]{1,0:T(8,128)}, f32[96,768]{1,0:T(8,128)S(1)}, u32[]{:S(2)}, u32[]{:S(2)}) collective-permute-start(f32[96,768]{1,0:T(8,128)} %get-tuple-element.142), channel_id=1, source_target_pairs={{0,1},{1,0},{2,3},{3,2},{4,5},{5,4},{6,7},{7,6},{8,9},{9,8},{10,11... | collective-permute-start | bytes 884744 | tf_op jit(solution)/shard_map/ppermute | solution.py:457
  5.4 6.1 %front.1 = (bf16[512,768]{1,0:T(8,128)(2,1)}, bf16[512,384]{1,0:T(8,128)(2,1)}, bf16[512,384]{1,0:T(8,128)(2,1)}, bf16[512,384]{1,0:T(8,128)(2,1)}, f32[512,128]...) custom-call(bf16[512,768]{1,0:T(8,128)(2,1)} %tokens.1, ...), custom_call_target="tpu_custom_call" | custom-call | flops 1000 | bytes 1000 | tf_op jit(solution)/shard_map/front/pallas_call | solution.py:434
  12.7 1.8 %collective-permute-start.3 = (f32[96,768]{1,0:T(8,128)S(1)}, f32[96,768]{1,0:T(8,128)S(1)}, u32[]{:S(2)}, u32[]{:S(2)}) collective-permute-start(f32[96,768]{1,0:T(8,128)S(1)} %collective-permute-done.refs_0_), channel_id=1, source_target_pairs={{0,4},{2,6},{4,0},{6,2},{8,12},{10,14},{12,8},{14,10},{16,20},{18,... | collective-permute-start | bytes 884744 | tf_op jit(solution)/shard_map/ppermute | solution.py:453
  17.1 3.7 %turn.1 = (bf16[512,768]{1,0:T(8,128)(2,1)S(1)}, bf16[768,1536]{1,0:T(8,128)(2,1)S(1)}, bf16[384,768]{1,0:T(8,128)(2,1)S(1)}, bf16[768,768]{1,0:T(8,128)(2,1)S(1...) custom-call(s32[1]{0:T(128)} %bitcast.here, ...), custom_call_target="tpu_custom_call" | custom-call | flops 1000 | bytes 1000 | tf_op jit(solution)/shard_map/turn/pallas_call | solution.py:434
  21.4 2.5 %collective-permute-done.1.values = f32[256,384]{1,0:T(8,128)S(1)} collective-permute-done((f32[256,384]{1,0:T(8,128)}, f32[256,384]{1,0:T(8,128)S(1)}, u32[]{:S(2)}, u32[]{:S(2)}) %collective-permute-start.1) | collective-permute-done | bytes 393248 | tf_op jit(solution)/shard_map/ppermute | solution.py:457
  25.9 3.5 %middle.2 = (f32[256,768]{1,0:T(8,128)S(1)}, bf16[768,256]{1,0:T(8,128)(2,1)S(1)}, bf16[256,1536]{1,0:T(8,128)(2,1)S(1)}, bf16[256,1536]{1,0:T(8,128)(2,1)S(1)},...) custom-call(bf16[512,768]{1,0:T(8,128)(2,1)S(1)} %copy-done.1, f32[256,384]{1,0:T(8,128)S(1)} %copy-done.2, ...), custom_call_target="tpu_custom_call" | custom-call | flops 1000 | bytes 1000 | tf_op jit(solution)/shard_map/middle/pallas_call | solution.py:434
  30.9 3.5 %middle.3 = (f32[256,768]{1,0:T(8,128)S(1)}, bf16[768,256]{1,0:T(8,128)(2,1)S(1)}, bf16[256,1536]{1,0:T(8,128)(2,1)S(1)}, bf16[256,1536]{1,0:T(8,128)(2,1)S(1)},...) custom-call(bf16[512,768]{1,0:T(8,128)(2,1)S(1)} %copy-done.1, f32[256,384]{1,0:T(8,128)S(1)} %copy-done.3, ...), custom_call_target="tpu_custom_call" | custom-call | flops 1000 | bytes 1000 | tf_op jit(solution)/shard_map/middle/pallas_call | solution.py:434
  38.4 1.7 %collective-permute-start.11 = (f32[192,1536]{1,0:T(8,128)S(1)}, f32[192,1536]{1,0:T(8,128)S(1)}, u32[]{:S(2)}, u32[]{:S(2)}) collective-permute-start(f32[192,1536]{1,0:T(8,128)S(1)} %part.12.refs_1_), channel_id=1, source_target_pairs={{0,4},{2,6},{4,0},{6,2},{8,12},{10,14},{12,8},{14,10},{16,20},{18,... | collective-permute-start | bytes 3538952 | tf_op jit(solution)/shard_map/ppermute | solution.py:453
  40.7 1.6 %collective-permute-start.12 = (f32[192,1536]{1,0:T(8,128)S(1)}, f32[192,1536]{1,0:T(8,128)S(1)}, u32[]{:S(2)}, u32[]{:S(2)}) collective-permute-start(f32[192,1536]{1,0:T(8,128)S(1)} %part.13.refs_1_), channel_id=1, source_target_pairs={{0,8},{2,10},{4,12},{6,14},{8,0},{10,2},{12,4},{14,6},{16,24},{18,... | collective-permute-start | bytes 3538952 | tf_op jit(solution)/shard_map/ppermute | solution.py:453
  47.1 10.9 %collective-permute-done.10.refs_5_ = f32[256,768]{1,0:T(8,128)S(1)} collective-permute-done((f32[256,768]{1,0:T(8,128)S(1)}, f32[256,768]{1,0:T(8,128)S(1)}, u32[]{:S(2)}, u32[]{:S(2)}) %collective-permute-start.10) | collective-permute-done | bytes 786464 | tf_op jit(solution)/shard_map/ppermute | solution.py:457
  58.0 4.9 %back.2 = (f32[256,768]{1,0:T(8,128)S(1)}, bf16[768,256]{1,0:T(8,128)(2,1)S(1)}, bf16[256,768]{1,0:T(8,128)(2,1)S(1)}, bf16[256,384]{1,0:T(8,128)(2,1)S(1)}, f32...) custom-call(bf16[512,768]{1,0:T(8,128)(2,1)S(1)} %copy-done.1, f32[12,768]{1,0:T(8,128)S(1)} %copy-done.8, ...), custom_call_target="tpu_custom_call" | custom-call | flops 6000001024 | bytes 1000 | tf_op jit(solution)/shard_map/back/pallas_call | solution.py:434
  62.9 3.5 %collective-permute-done.11.refs_2_ = f32[192,1536]{1,0:T(8,128)S(1)} collective-permute-done((f32[192,1536]{1,0:T(8,128)S(1)}, f32[192,1536]{1,0:T(8,128)S(1)}, u32[]{:S(2)}, u32[]{:S(2)}) %collective-permute-start.11) | collective-permute-done | bytes 1179680 | tf_op jit(solution)/shard_map/ppermute | solution.py:453
  66.5 1.7 %collective-permute-done.12.refs_2_ = f32[192,1536]{1,0:T(8,128)S(1)} collective-permute-done((f32[192,1536]{1,0:T(8,128)S(1)}, f32[192,1536]{1,0:T(8,128)S(1)}, u32[]{:S(2)}, u32[]{:S(2)}) %collective-permute-start.12) | collective-permute-done | bytes 1179680 | tf_op jit(solution)/shard_map/ppermute | solution.py:453
  71.3 3.5 %collective-permute-done.13.refs_5_ = f32[256,768]{1,0:T(8,128)S(1)} collective-permute-done((f32[256,768]{1,0:T(8,128)S(1)}, f32[256,768]{1,0:T(8,128)S(1)}, u32[]{:S(2)}, u32[]{:S(2)}) %collective-permute-start.13) | collective-permute-done | bytes 786464 | tf_op jit(solution)/shard_map/ppermute | solution.py:457
  74.8 4.9 %back.3 = (f32[256,768]{1,0:T(8,128)S(1)}, bf16[768,256]{1,0:T(8,128)(2,1)S(1)}, bf16[256,768]{1,0:T(8,128)(2,1)S(1)}, bf16[256,384]{1,0:T(8,128)(2,1)S(1)}, f32...) custom-call(bf16[512,768]{1,0:T(8,128)(2,1)S(1)} %copy-done.1, f32[12,768]{1,0:T(8,128)S(1)} %copy-done.8, ...), custom_call_target="tpu_custom_call" | custom-call | flops 1000 | bytes 1000 | tf_op jit(solution)/shard_map/back/pallas_call | solution.py:434
  88.6 2.6 %collective-permute-start.23 = (f32[96,1536]{1,0:T(8,128)S(1)}, f32[96,1536]{1,0:T(8,128)S(1)}, u32[]{:S(2)}, u32[]{:S(2)}) collective-permute-start(f32[96,1536]{1,0:T(8,128)S(1)} %get-tuple-element.231), channel_id=1, source_target_pairs={{0,16},{2,18},{4,20},{6,22},{8,24},{10,26},{12,28},{14,30},{16,0},... | collective-permute-start | bytes 1769480 | tf_op jit(solution)/shard_map/ppermute | solution.py:453
  91.2 10.3 %collective-permute-done.20.refs_2_ = f32[208,768]{1,0:T(8,128)S(1)} collective-permute-done((f32[208,768]{1,0:T(8,128)S(1)}, f32[208,768]{1,0:T(8,128)S(1)}, u32[]{:S(2)}, u32[]{:S(2)}) %collective-permute-start.20) | collective-permute-done | bytes 639008 | tf_op jit(solution)/shard_map/ppermute | solution.py:453
  103.2 5.3 %collective-permute-done.21.refs_2_ = f32[512,768]{1,0:T(8,128)S(1)} collective-permute-done((f32[512,768]{1,0:T(8,128)S(1)}, f32[512,768]{1,0:T(8,128)S(1)}, u32[]{:S(2)}, u32[]{:S(2)}) %collective-permute-start.21) | collective-permute-done | bytes 1572896 | tf_op jit(solution)/shard_map/ppermute | solution.py:457
  109.6 6.2 %collective-permute-done.22.refs_2_ = f32[192,768]{1,0:T(8,128)S(1)} collective-permute-done((f32[192,768]{1,0:T(8,128)S(1)}, f32[192,768]{1,0:T(8,128)S(1)}, u32[]{:S(2)}, u32[]{:S(2)}) %collective-permute-start.22) | collective-permute-done | bytes 589856 | tf_op jit(solution)/shard_map/ppermute | solution.py:453
  117.7 4.6 %collective-permute-done.24.refs_2_ = f32[112,768]{1,0:T(8,128)S(1)} collective-permute-done((f32[112,768]{1,0:T(8,128)S(1)}, f32[112,768]{1,0:T(8,128)S(1)}, u32[]{:S(2)}, u32[]{:S(2)}) %collective-permute-start.24) | collective-permute-done | bytes 344096 | tf_op jit(solution)/shard_map/ppermute | solution.py:453
  122.4 2.7 %collective-permute-start.26 = (f32[64,768]{1,0:T(8,128)S(1)}, f32[64,768]{1,0:T(8,128)S(1)}, u32[]{:S(2)}, u32[]{:S(2)}) collective-permute-start(f32[64,768]{1,0:T(8,128)S(1)} %get-tuple-element.242.sent), channel_id=1, source_target_pairs={{0,16},{2,18},{4,20},{6,22},{8,24},{10,26},{12,28},{14,30},{16,0},... | collective-permute-start | bytes 589832 | tf_op jit(solution)/shard_map/ppermute | solution.py:453
  126.5 11.4 %collective-permute-done.26.got.refs_1_ = f32[64,768]{1,0:T(8,128)S(1)} collective-permute-done((f32[64,768]{1,0:T(8,128)S(1)}, f32[64,768]{1,0:T(8,128)S(1)}, u32[]{:S(2)}, u32[]{:S(2)}) %collective-permute-start.26) | collective-permute-done | bytes 196640 | tf_op jit(solution)/shard_map/ppermute | solution.py:453
  141.4 1.9 %last.1 = f32[512,768]{1,0:T(8,128)} custom-call(f32[12,768]{1,0:T(8,128)S(1)} %copy-done.8, f32[512,768]{1,0:T(8,128)S(1)} %get-tuple-element.249.base, f32[512,768]{1,0:T(8,128)S(1)} %get-tuple-element.250.unit, f32[512,1]{1,0:T(8,128)S(1)} %get-tuple-element.251.scale, f32[512,768]{1,0:T(8,128)S(1)} %collective-permute-done.28.other), custom_call_target="tpu_custom_call" | custom-call | flops 1000 | bytes 1000 | tf_op jit(solution)/shard_map/last/pallas_call | solution.py:434
  (103 shorter events, 39.3 us)
Async XLA Ops:
  2.4 10.2 %collective-permute-start = (f32[96,768]{1,0:T(8,128)}, f32[96,768]{1,0:T(8,128)S(1)}, u32[]{:S(2)}, u32[]{:S(2)}) collective-permute-start(f32[96,768]{1,0:T(8,128)} %get-tuple-element.142), channel_id=1, source_target_pairs={{0,1},{1,0},{2,3},{3,2},{4,5},{5,4},{6,7},{7,6},{8,9},{9,8},{10,11... | collective-permute-start | bytes 884744 | tf_op jit(solution)/shard_map/ppermute | solution.py:457
  11.6 12.3 %collective-permute-start.1 = (f32[256,384]{1,0:T(8,128)}, f32[256,384]{1,0:T(8,128)S(1)}, u32[]{:S(2)}, u32[]{:S(2)}) collective-permute-start(f32[256,384]{1,0:T(8,128)} %get-tuple-element.153.refs_1_.refs_6_), channel_id=1, source_target_pairs={{0,1},{1,0},{2,3},{3,2},{4,5},{5,4},{6,7},{7,6},{8,9},{9,8},{10,11... | collective-permute-start | bytes 1179656 | tf_op jit(solution)/shard_map/ppermute | solution.py:457
  12.7 8.2 %collective-permute-start.3 = (f32[96,768]{1,0:T(8,128)S(1)}, f32[96,768]{1,0:T(8,128)S(1)}, u32[]{:S(2)}, u32[]{:S(2)}) collective-permute-start(f32[96,768]{1,0:T(8,128)S(1)} %collective-permute-done.refs_0_), channel_id=1, source_target_pairs={{0,4},{2,6},{4,0},{6,2},{8,12},{10,14},{12,8},{14,10},{16,20},{18,... | collective-permute-start | bytes 884744 | tf_op jit(solution)/shard_map/ppermute | solution.py:453
  14.4 16.4 %collective-permute-start.5 = (f32[256,384]{1,0:T(8,128)}, f32[256,384]{1,0:T(8,128)S(1)}, u32[]{:S(2)}, u32[]{:S(2)}) collective-permute-start(f32[256,384]{1,0:T(8,128)} %get-tuple-element.161.refs_1_.refs_7_), channel_id=1, source_target_pairs={{0,1},{1,0},{2,3},{3,2},{4,5},{5,4},{6,7},{7,6},{8,9},{9,8},{10,11... | collective-permute-start | bytes 1179656 | tf_op jit(solution)/shard_map/ppermute | solution.py:457
  35.4 4.8 %collective-permute-start.7 = (f32[192,1536]{1,0:T(8,128)S(1)}, f32[192,1536]{1,0:T(8,128)S(1)}, u32[]{:S(2)}, u32[]{:S(2)}) collective-permute-start(f32[192,1536]{1,0:T(8,128)S(1)} %part.9), channel_id=1, source_target_pairs={{0,2},{2,0},{4,6},{6,4},{8,10},{10,8},{12,14},{14,12},{16,18},{18,... | collective-permute-start | bytes 3538952 | tf_op jit(solution)/shard_map/ppermute | solution.py:453
  36.5 5.9 %collective-permute-start.8 = (f32[192,1536]{1,0:T(8,128)S(1)}, f32[192,1536]{1,0:T(8,128)S(1)}, u32[]{:S(2)}, u32[]{:S(2)}) collective-permute-start(f32[192,1536]{1,0:T(8,128)S(1)} %part.10), channel_id=1, source_target_pairs={{0,2},{2,0},{4,6},{6,4},{8,10},{10,8},{12,14},{14,12},{16,18},{18,... | collective-permute-start | bytes 3538952 | tf_op jit(solution)/shard_map/ppermute | solution.py:453
  37.0 9.0 %collective-permute-start.9 = (f32[192,1536]{1,0:T(8,128)S(1)}, f32[192,1536]{1,0:T(8,128)S(1)}, u32[]{:S(2)}, u32[]{:S(2)}) collective-permute-start(f32[192,1536]{1,0:T(8,128)S(1)} %part.11), channel_id=1, source_target_pairs={{0,2},{2,0},{4,6},{6,4},{8,10},{10,8},{12,14},{14,12},{16,18},{18,... | collective-permute-start | bytes 3538952 | tf_op jit(solution)/shard_map/ppermute | solution.py:453
  37.6 20.4 %collective-permute-start.10 = (f32[256,768]{1,0:T(8,128)S(1)}, f32[256,768]{1,0:T(8,128)S(1)}, u32[]{:S(2)}, u32[]{:S(2)}) collective-permute-start(f32[256,768]{1,0:T(8,128)S(1)} %get-tuple-element.180.refs_4_), channel_id=1, source_target_pairs={{0,1},{1,0},{2,3},{3,2},{4,5},{5,4},{6,7},{7,6},{8,9},{9,8},{10,11... | collective-permute-start | bytes 2359304 | tf_op jit(solution)/shard_map/ppermute | solution.py:457
  38.4 27.9 %collective-permute-start.11 = (f32[192,1536]{1,0:T(8,128)S(1)}, f32[192,1536]{1,0:T(8,128)S(1)}, u32[]{:S(2)}, u32[]{:S(2)}) collective-permute-start(f32[192,1536]{1,0:T(8,128)S(1)} %part.12.refs_1_), channel_id=1, source_target_pairs={{0,4},{2,6},{4,0},{6,2},{8,12},{10,14},{12,8},{14,10},{16,20},{18,... | collective-permute-start | bytes 3538952 | tf_op jit(solution)/shard_map/ppermute | solution.py:453
  40.7 27.5 %collective-permute-start.12 = (f32[192,1536]{1,0:T(8,128)S(1)}, f32[192,1536]{1,0:T(8,128)S(1)}, u32[]{:S(2)}, u32[]{:S(2)}) collective-permute-start(f32[192,1536]{1,0:T(8,128)S(1)} %part.13.refs_1_), channel_id=1, source_target_pairs={{0,8},{2,10},{4,12},{6,14},{8,0},{10,2},{12,4},{14,6},{16,24},{18,... | collective-permute-start | bytes 3538952 | tf_op jit(solution)/shard_map/ppermute | solution.py:453
  42.3 32.5 %collective-permute-start.13 = (f32[256,768]{1,0:T(8,128)S(1)}, f32[256,768]{1,0:T(8,128)S(1)}, u32[]{:S(2)}, u32[]{:S(2)}) collective-permute-start(f32[256,768]{1,0:T(8,128)S(1)} %get-tuple-element.194.refs_4_), channel_id=1, source_target_pairs={{0,1},{1,0},{2,3},{3,2},{4,5},{5,4},{6,7},{7,6},{8,9},{9,8},{10,11... | collective-permute-start | bytes 2359304 | tf_op jit(solution)/shard_map/ppermute | solution.py:457
  46.0 62.5 %collective-permute-start.21 = (f32[512,768]{1,0:T(8,128)S(1)}, f32[512,768]{1,0:T(8,128)S(1)}, u32[]{:S(2)}, u32[]{:S(2)}) collective-permute-start(f32[512,768]{1,0:T(8,128)S(1)} %mlp.1.refs_1_), channel_id=1, source_target_pairs={{0,1},{1,0},{2,3},{3,2},{4,5},{5,4},{6,7},{7,6},{8,9},{9,8},{10,11... | collective-permute-start | bytes 4718600 | tf_op jit(solution)/shard_map/ppermute | solution.py:457
  68.3 14.3 %collective-permute-start.15 = (f32[96,1536]{1,0:T(8,128)S(1)}, f32[96,1536]{1,0:T(8,128)S(1)}, u32[]{:S(2)}, u32[]{:S(2)}) collective-permute-start(f32[96,1536]{1,0:T(8,128)S(1)} %get-tuple-element.213.refs_3_), channel_id=1, source_target_pairs={{0,4},{2,6},{4,0},{6,2},{8,12},{10,14},{12,8},{14,10},{16,20},{18,... | collective-permute-start | bytes 1769480 | tf_op jit(solution)/shard_map/ppermute | solution.py:453
  69.7 14.3 %collective-permute-start.14 = (f32[96,1536]{1,0:T(8,128)S(1)}, f32[96,1536]{1,0:T(8,128)S(1)}, u32[]{:S(2)}, u32[]{:S(2)}) collective-permute-start(f32[96,1536]{1,0:T(8,128)S(1)} %get-tuple-element.212.refs_2_), channel_id=1, source_target_pairs={{0,8},{2,10},{4,12},{6,14},{8,0},{10,2},{12,4},{14,6},{16,24},{18,... | collective-permute-start | bytes 1769480 | tf_op jit(solution)/shard_map/ppermute | solution.py:453
  80.3 4.0 %collective-permute-start.16 = (f32[208,768]{1,0:T(8,128)S(1)}, f32[208,768]{1,0:T(8,128)S(1)}, u32[]{:S(2)}, u32[]{:S(2)}) collective-permute-start(f32[208,768]{1,0:T(8,128)S(1)} %get-tuple-element.203), channel_id=1, source_target_pairs={{0,2},{2,0},{4,6},{6,4},{8,10},{10,8},{12,14},{14,12},{16,18},{18,... | collective-permute-start | bytes 1916936 | tf_op jit(solution)/shard_map/ppermute | solution.py:453
  84.0 57.4 %collective-permute-start.28 = (f32[512,768]{1,0:T(8,128)S(1)}, f32[512,768]{1,0:T(8,128)S(1)}, u32[]{:S(2)}, u32[]{:S(2)}) collective-permute-start(f32[512,768]{1,0:T(8,128)S(1)} %get-tuple-element.239.own), channel_id=1, source_target_pairs={{0,1},{1,0},{2,3},{3,2},{4,5},{5,4},{6,7},{7,6},{8,9},{9,8},{10,11... | collective-permute-start | bytes 4718600 | tf_op jit(solution)/shard_map/ppermute | solution.py:457
  84.8 16.7 %collective-permute-start.20 = (f32[208,768]{1,0:T(8,128)S(1)}, f32[208,768]{1,0:T(8,128)S(1)}, u32[]{:S(2)}, u32[]{:S(2)}) collective-permute-start(f32[208,768]{1,0:T(8,128)S(1)} %get-tuple-element.222.refs_1_), channel_id=1, source_target_pairs={{0,4},{2,6},{4,0},{6,2},{8,12},{10,14},{12,8},{14,10},{16,20},{18,... | collective-permute-start | bytes 1916936 | tf_op jit(solution)/shard_map/ppermute | solution.py:453
  87.0 28.8 %collective-permute-start.22 = (f32[192,768]{1,0:T(8,128)S(1)}, f32[192,768]{1,0:T(8,128)S(1)}, u32[]{:S(2)}, u32[]{:S(2)}) collective-permute-start(f32[192,768]{1,0:T(8,128)S(1)} %get-tuple-element.227.refs_1_), channel_id=1, source_target_pairs={{0,8},{2,10},{4,12},{6,14},{8,0},{10,2},{12,4},{14,6},{16,24},{18,... | collective-permute-start | bytes 1769480 | tf_op jit(solution)/shard_map/ppermute | solution.py:453
  88.6 28.2 %collective-permute-start.23 = (f32[96,1536]{1,0:T(8,128)S(1)}, f32[96,1536]{1,0:T(8,128)S(1)}, u32[]{:S(2)}, u32[]{:S(2)}) collective-permute-start(f32[96,1536]{1,0:T(8,128)S(1)} %get-tuple-element.231), channel_id=1, source_target_pairs={{0,16},{2,18},{4,20},{6,22},{8,24},{10,26},{12,28},{14,30},{16,0},... | collective-permute-start | bytes 1769480 | tf_op jit(solution)/shard_map/ppermute | solution.py:453
  101.6 20.7 %collective-permute-start.24 = (f32[112,768]{1,0:T(8,128)S(1)}, f32[112,768]{1,0:T(8,128)S(1)}, u32[]{:S(2)}, u32[]{:S(2)}) collective-permute-start(f32[112,768]{1,0:T(8,128)S(1)} %get-tuple-element.234.refs_1_), channel_id=1, source_target_pairs={{0,8},{2,10},{4,12},{6,14},{8,0},{10,2},{12,4},{14,6},{16,24},{18,... | collective-permute-start | bytes 1032200 | tf_op jit(solution)/shard_map/ppermute | solution.py:453
  115.8 9.2 %collective-permute-start.25 = (f32[96,768]{1,0:T(8,128)S(1)}, f32[96,768]{1,0:T(8,128)S(1)}, u32[]{:S(2)}, u32[]{:S(2)}) collective-permute-start(f32[96,768]{1,0:T(8,128)S(1)} %get-tuple-element.237.refs_1_), channel_id=1, source_target_pairs={{0,4},{2,6},{4,0},{6,2},{8,12},{10,14},{12,8},{14,10},{16,20},{18,... | collective-permute-start | bytes 884744 | tf_op jit(solution)/shard_map/ppermute | solution.py:453
  122.4 15.5 %collective-permute-start.26 = (f32[64,768]{1,0:T(8,128)S(1)}, f32[64,768]{1,0:T(8,128)S(1)}, u32[]{:S(2)}, u32[]{:S(2)}) collective-permute-start(f32[64,768]{1,0:T(8,128)S(1)} %get-tuple-element.242.sent), channel_id=1, source_target_pairs={{0,16},{2,18},{4,20},{6,22},{8,24},{10,26},{12,28},{14,30},{16,0},... | collective-permute-start | bytes 589832 | tf_op jit(solution)/shard_map/ppermute | solution.py:453
  125.1 14.7 %collective-permute-start.27 = (f32[48,768]{1,0:T(8,128)S(1)}, f32[48,768]{1,0:T(8,128)S(1)}, u32[]{:S(2)}, u32[]{:S(2)}) collective-permute-start(f32[48,768]{1,0:T(8,128)S(1)} %get-tuple-element.247), channel_id=1, source_target_pairs={{0,16},{2,18},{4,20},{6,22},{8,24},{10,26},{12,28},{14,30},{16,0},... | collective-permute-start | bytes 442376 | tf_op jit(solution)/shard_map/ppermute | solution.py:453
  138.5 4.8 %collective-permute-start.29 = (f32[8,128]{1,0:T(8,128)S(1)}, f32[8,128]{1,0:T(8,128)S(1)}, u32[]{:S(2)}, u32[]{:S(2)}) collective-permute-start(f32[8,128]{1,0:T(8,128)S(1)} %get-tuple-element.257.own), channel_id=1, source_target_pairs={{0,1},{1,0},{2,3},{3,2},{4,5},{5,4},{6,7},{7,6},{8,9},{9,8},{10,11... | collective-permute-start | bytes 12296 | tf_op jit(solution)/shard_map/ppermute | solution.py:457
  (21 other events, 137.5 us)

commit v8 on v7

--- a/solution.py
+++ b/solution.py
@@ -507,8 +507,10 @@
         outs = self.shapes(self.rows // 2)
         return self.steps(kernel, "part", outs, self.arrays + added)[0]
 
-    def far_part(self, sent):
-        return send(self.part(2 + sent, []), self.bits[0], self.count)
+    def far_parts(self):
+        kernel = partial(far_kernel, plan=self.plan, start=self.rows, pieces=2, small=False)
+        kept, sent = self.steps(kernel, "far", self.shapes(*[self.rows // 2] * 2), self.arrays)
+        return [send(o, self.bits[0], self.count) for o in (sent, kept)]
 
     def near_sent(self, got):
         self.sent = self.part(1, [got])
@@ -697,13 +699,13 @@
 
     down = Scatter(steps, count, orders[0], [(cot_a, active)])
     up = Scatter(steps, count, orders[1], [(a2_b, g_pre)])
-    parts = [one.far_part(sent) for sent in (1, 0) for one in (down, up)]
-    down.near_sent(parts[0])
-    up.near_sent(parts[1])
+    (down_sent, down_kept), (up_sent, up_kept) = [one.far_parts() for one in (down, up)]
+    down.near_sent(down_sent)
+    up.near_sent(up_sent)
     mlp_part = steps(mlp_kernel, "mlp", [((rows, width), HIGH)], [w_down] + active, tie=1)[0]
     mlp_other = swap(mlp_part)
-    down.near_keep(parts[2])
-    up.near_keep(parts[3])
+    down.near_keep(down_kept)
+    up.near_keep(up_kept)
     g_hidden, gh_b, g_qk, g_val, carried = [], [], [], [], [bias_sum, cot_sum]
     for s in range(seqs):
         if s == seqs - 1:

time: 144 us -> 144 us (level)
    ppermute x8, waiting for transfers between devices: 25.6 us -> 22.5 us  [swap(): return lax.ppermute(values, 'mp', [(0, 1), (1, 0)])]
    ppermute x22, waiting for transfers between devices: 40.2 us -> 43.3 us  [send(): return lax.ppermute(values, 'dp', [(i, i ^ 1 << bit) for i in range(count)])]
    pallas_call x37 -> x35, Pallas kernels: 44.3 us -> 44 us  [__call__(): pl.pallas_call(kernel, name=name, out_shape=[jax.ShapeDtypeStruct(s, d) f...]
  transfers between devices with their start and end apart: 30 -> 30, of which waited for: 16 -> 17; matrix products, arithmetic and copies ran while one was open for 0% -> 0% of each run, Pallas kernels for 26% -> 26%
where the time goes in v8:
time: 144 us; the launch traced here: 143 us
  waiting for transfers between devices  65.8 us (46%)
  Pallas kernels  44 us (31%)
  starting transfers between devices  29.5 us (20%)
  local copies, waits for them, and re-layouts  2.98 us (2%)
    pallas_call x35, Pallas kernels, __call__(): pl.pallas_call(kernel, name=name, out_shape=[jax.ShapeDtypeStruct(s, d) f...  44 us
    ppermute x22, waiting for transfers between devices, send(): return lax.ppermute(values, 'dp', [(i, i ^ 1 << bit) for i in range(count)])  43.3 us
    ppermute x8, waiting for transfers between devices, swap(): return lax.ppermute(values, 'mp', [(0, 1), (1, 0)])  22.5 us
    ppermute x22, starting transfers between devices, send(): return lax.ppermute(values, 'dp', [(i, i ^ 1 << bit) for i in range(count)])  21.4 us
    ppermute x8, starting transfers between devices, swap(): return lax.ppermute(values, 'mp', [(0, 1), (1, 0)])  8.08 us
    unnamed x30, local copies, waits for them, and re-layouts  2.98 us
  transfers between devices with their start and end apart: 30, of which 17 were waited for; matrix products, arithmetic and copies ran while one was open for 0% of the time, Pallas kernels for 26%

profile of v8, /device:TPU:0, one launch (start us, length us, event | category | flops | bytes accessed | tf_op | source)
XLA Modules:
  0.0 143.3 jit_solution(10981978560300030074)
XLA Ops:
  0.7 1.8 %load.1 = (f32[96,768]{1,0:T(8,128)}, f32[12,768]{1,0:T(8,128)}) custom-call(s32[1]{0:T(128)} %bitcast.here, bf16[384,768]{1,0:T(8,128)(2,1)} %refs_3_.5, s32[2,256]{1,0:T(2,128)} %crops.1, f32[768]{0:T(1024)} %refs_0_.6, f32[768]{0:T(1024)} %refs_1_.2, f32[384]{0:T(512)} %refs_2_.3, f32[384]{0:T(512)} %refs_3_.3, f32[768]{0:T(1024)} %refs_4_.2, ...), custom_call_target="tpu_custom_call" | custom-call | flops 1000 | bytes 1000 | tf_op jit(solution)/shard_map/load/pallas_call | solution.py:434
  2.4 3.0 %collective-permute-start = (f32[96,768]{1,0:T(8,128)}, f32[96,768]{1,0:T(8,128)S(1)}, u32[]{:S(2)}, u32[]{:S(2)}) collective-permute-start(f32[96,768]{1,0:T(8,128)} %get-tuple-element.144), channel_id=1, source_target_pairs={{0,1},{1,0},{2,3},{3,2},{4,5},{5,4},{6,7},{7,6},{8,9},{9,8},{10,11... | collective-permute-start | bytes 884744 | tf_op jit(solution)/shard_map/ppermute | solution.py:457
  5.4 6.1 %front.1 = (bf16[512,768]{1,0:T(8,128)(2,1)}, bf16[512,384]{1,0:T(8,128)(2,1)}, bf16[512,384]{1,0:T(8,128)(2,1)}, bf16[512,384]{1,0:T(8,128)(2,1)}, f32[512,128]...) custom-call(bf16[512,768]{1,0:T(8,128)(2,1)} %tokens.1, ...), custom_call_target="tpu_custom_call" | custom-call | flops 1000 | bytes 1000 | tf_op jit(solution)/shard_map/front/pallas_call | solution.py:434
  12.7 1.8 %collective-permute-start.3 = (f32[96,768]{1,0:T(8,128)S(1)}, f32[96,768]{1,0:T(8,128)S(1)}, u32[]{:S(2)}, u32[]{:S(2)}) collective-permute-start(f32[96,768]{1,0:T(8,128)S(1)} %collective-permute-done.refs_0_), channel_id=1, source_target_pairs={{0,4},{2,6},{4,0},{6,2},{8,12},{10,14},{12,8},{14,10},{16,20},{18,... | collective-permute-start | bytes 884744 | tf_op jit(solution)/shard_map/ppermute | solution.py:453
  17.1 3.7 %turn.1 = (bf16[512,768]{1,0:T(8,128)(2,1)S(1)}, bf16[768,1536]{1,0:T(8,128)(2,1)S(1)}, bf16[384,768]{1,0:T(8,128)(2,1)S(1)}, bf16[768,768]{1,0:T(8,128)(2,1)S(1...) custom-call(s32[1]{0:T(128)} %bitcast.here, ...), custom_call_target="tpu_custom_call" | custom-call | flops 1000 | bytes 1000 | tf_op jit(solution)/shard_map/turn/pallas_call | solution.py:434
  21.4 2.5 %collective-permute-done.1.values = f32[256,384]{1,0:T(8,128)S(1)} collective-permute-done((f32[256,384]{1,0:T(8,128)}, f32[256,384]{1,0:T(8,128)S(1)}, u32[]{:S(2)}, u32[]{:S(2)}) %collective-permute-start.1) | collective-permute-done | bytes 393248 | tf_op jit(solution)/shard_map/ppermute | solution.py:457
  25.9 3.5 %middle.2 = (f32[256,768]{1,0:T(8,128)S(1)}, bf16[768,256]{1,0:T(8,128)(2,1)S(1)}, bf16[256,1536]{1,0:T(8,128)(2,1)S(1)}, bf16[256,1536]{1,0:T(8,128)(2,1)S(1)},...) custom-call(bf16[512,768]{1,0:T(8,128)(2,1)S(1)} %copy-done.1, f32[256,384]{1,0:T(8,128)S(1)} %copy-done.2, ...), custom_call_target="tpu_custom_call" | custom-call | flops 1000 | bytes 1000 | tf_op jit(solution)/shard_map/middle/pallas_call | solution.py:434
  30.9 3.5 %middle.3 = (f32[256,768]{1,0:T(8,128)S(1)}, bf16[768,256]{1,0:T(8,128)(2,1)S(1)}, bf16[256,1536]{1,0:T(8,128)(2,1)S(1)}, bf16[256,1536]{1,0:T(8,128)(2,1)S(1)},...) custom-call(bf16[512,768]{1,0:T(8,128)(2,1)S(1)} %copy-done.1, f32[256,384]{1,0:T(8,128)S(1)} %copy-done.3, ...), custom_call_target="tpu_custom_call" | custom-call | flops 1000 | bytes 1000 | tf_op jit(solution)/shard_map/middle/pallas_call | solution.py:434
  40.6 1.6 %collective-permute-start.12 = (f32[192,1536]{1,0:T(8,128)S(1)}, f32[192,1536]{1,0:T(8,128)S(1)}, u32[]{:S(2)}, u32[]{:S(2)}) collective-permute-start(f32[192,1536]{1,0:T(8,128)S(1)} %part.5.refs_1_), channel_id=1, source_target_pairs={{0,8},{2,10},{4,12},{6,14},{8,0},{10,2},{12,4},{14,6},{16,24},{18,... | collective-permute-start | bytes 3538952 | tf_op jit(solution)/shard_map/ppermute | solution.py:453
  47.1 10.5 %collective-permute-done.10.refs_5_ = f32[256,768]{1,0:T(8,128)S(1)} collective-permute-done((f32[256,768]{1,0:T(8,128)S(1)}, f32[256,768]{1,0:T(8,128)S(1)}, u32[]{:S(2)}, u32[]{:S(2)}) %collective-permute-start.10) | collective-permute-done | bytes 786464 | tf_op jit(solution)/shard_map/ppermute | solution.py:457
  57.6 4.9 %back.2 = (f32[256,768]{1,0:T(8,128)S(1)}, bf16[768,256]{1,0:T(8,128)(2,1)S(1)}, bf16[256,768]{1,0:T(8,128)(2,1)S(1)}, bf16[256,384]{1,0:T(8,128)(2,1)S(1)}, f32...) custom-call(bf16[512,768]{1,0:T(8,128)(2,1)S(1)} %copy-done.1, f32[12,768]{1,0:T(8,128)S(1)} %copy-done.8, ...), custom_call_target="tpu_custom_call" | custom-call | flops 6000001024 | bytes 1000 | tf_op jit(solution)/shard_map/back/pallas_call | solution.py:434
  62.4 4.2 %collective-permute-done.11.refs_2_ = f32[192,1536]{1,0:T(8,128)S(1)} collective-permute-done((f32[192,1536]{1,0:T(8,128)S(1)}, f32[192,1536]{1,0:T(8,128)S(1)}, u32[]{:S(2)}, u32[]{:S(2)}) %collective-permute-start.11) | collective-permute-done | bytes 1179680 | tf_op jit(solution)/shard_map/ppermute | solution.py:453
  71.7 2.7 %collective-permute-done.13.refs_5_ = f32[256,768]{1,0:T(8,128)S(1)} collective-permute-done((f32[256,768]{1,0:T(8,128)S(1)}, f32[256,768]{1,0:T(8,128)S(1)}, u32[]{:S(2)}, u32[]{:S(2)}) %collective-permute-start.13) | collective-permute-done | bytes 786464 | tf_op jit(solution)/shard_map/ppermute | solution.py:457
  74.4 4.9 %back.3 = (f32[256,768]{1,0:T(8,128)S(1)}, bf16[768,256]{1,0:T(8,128)(2,1)S(1)}, bf16[256,768]{1,0:T(8,128)(2,1)S(1)}, bf16[256,384]{1,0:T(8,128)(2,1)S(1)}, f32...) custom-call(bf16[512,768]{1,0:T(8,128)(2,1)S(1)} %copy-done.1, f32[12,768]{1,0:T(8,128)S(1)} %copy-done.8, ...), custom_call_target="tpu_custom_call" | custom-call | flops 1000 | bytes 1000 | tf_op jit(solution)/shard_map/back/pallas_call | solution.py:434
  80.9 1.9 %collective-permute-done.15.refs_5_ = f32[96,1536]{1,0:T(8,128)S(1)} collective-permute-done((f32[96,1536]{1,0:T(8,128)S(1)}, f32[96,1536]{1,0:T(8,128)S(1)}, u32[]{:S(2)}, u32[]{:S(2)}) %collective-permute-start.15) | collective-permute-done | bytes 589856 | tf_op jit(solution)/shard_map/ppermute | solution.py:453
  87.2 1.6 %collective-permute-start.22 = (f32[192,768]{1,0:T(8,128)S(1)}, f32[192,768]{1,0:T(8,128)S(1)}, u32[]{:S(2)}, u32[]{:S(2)}) collective-permute-start(f32[192,768]{1,0:T(8,128)S(1)} %get-tuple-element.231.refs_1_), channel_id=1, source_target_pairs={{0,8},{2,10},{4,12},{6,14},{8,0},{10,2},{12,4},{14,6},{16,24},{18,... | collective-permute-start | bytes 1769480 | tf_op jit(solution)/shard_map/ppermute | solution.py:453
  88.9 2.6 %collective-permute-start.23 = (f32[96,1536]{1,0:T(8,128)S(1)}, f32[96,1536]{1,0:T(8,128)S(1)}, u32[]{:S(2)}, u32[]{:S(2)}) collective-permute-start(f32[96,1536]{1,0:T(8,128)S(1)} %get-tuple-element.235), channel_id=1, source_target_pairs={{0,16},{2,18},{4,20},{6,22},{8,24},{10,26},{12,28},{14,30},{16,0},... | collective-permute-start | bytes 1769480 | tf_op jit(solution)/shard_map/ppermute | solution.py:453
  91.5 10.6 %collective-permute-done.20.refs_2_ = f32[208,768]{1,0:T(8,128)S(1)} collective-permute-done((f32[208,768]{1,0:T(8,128)S(1)}, f32[208,768]{1,0:T(8,128)S(1)}, u32[]{:S(2)}, u32[]{:S(2)}) %collective-permute-start.20) | collective-permute-done | bytes 639008 | tf_op jit(solution)/shard_map/ppermute | solution.py:453
  103.8 4.3 %collective-permute-done.21.refs_2_ = f32[512,768]{1,0:T(8,128)S(1)} collective-permute-done((f32[512,768]{1,0:T(8,128)S(1)}, f32[512,768]{1,0:T(8,128)S(1)}, u32[]{:S(2)}, u32[]{:S(2)}) %collective-permute-start.21) | collective-permute-done | bytes 1572896 | tf_op jit(solution)/shard_map/ppermute | solution.py:457
  109.2 6.8 %collective-permute-done.22.refs_2_ = f32[192,768]{1,0:T(8,128)S(1)} collective-permute-done((f32[192,768]{1,0:T(8,128)S(1)}, f32[192,768]{1,0:T(8,128)S(1)}, u32[]{:S(2)}, u32[]{:S(2)}) %collective-permute-start.22) | collective-permute-done | bytes 589856 | tf_op jit(solution)/shard_map/ppermute | solution.py:453
  118.3 4.4 %collective-permute-done.24.refs_2_ = f32[112,768]{1,0:T(8,128)S(1)} collective-permute-done((f32[112,768]{1,0:T(8,128)S(1)}, f32[112,768]{1,0:T(8,128)S(1)}, u32[]{:S(2)}, u32[]{:S(2)}) %collective-permute-start.24) | collective-permute-done | bytes 344096 | tf_op jit(solution)/shard_map/ppermute | solution.py:453
  122.7 2.7 %collective-permute-start.26 = (f32[64,768]{1,0:T(8,128)S(1)}, f32[64,768]{1,0:T(8,128)S(1)}, u32[]{:S(2)}, u32[]{:S(2)}) collective-permute-start(f32[64,768]{1,0:T(8,128)S(1)} %get-tuple-element.246.sent), channel_id=1, source_target_pairs={{0,16},{2,18},{4,20},{6,22},{8,24},{10,26},{12,28},{14,30},{16,0},... | collective-permute-start | bytes 589832 | tf_op jit(solution)/shard_map/ppermute | solution.py:453
  126.8 11.4 %collective-permute-done.26.got.refs_1_ = f32[64,768]{1,0:T(8,128)S(1)} collective-permute-done((f32[64,768]{1,0:T(8,128)S(1)}, f32[64,768]{1,0:T(8,128)S(1)}, u32[]{:S(2)}, u32[]{:S(2)}) %collective-permute-start.26) | collective-permute-done | bytes 196640 | tf_op jit(solution)/shard_map/ppermute | solution.py:453
  140.9 1.9 %last.1 = f32[512,768]{1,0:T(8,128)} custom-call(f32[12,768]{1,0:T(8,128)S(1)} %copy-done.8, f32[512,768]{1,0:T(8,128)S(1)} %get-tuple-element.253.base, f32[512,768]{1,0:T(8,128)S(1)} %get-tuple-element.254.unit, f32[512,1]{1,0:T(8,128)S(1)} %get-tuple-element.255.scale, f32[512,768]{1,0:T(8,128)S(1)} %collective-permute-done.28.other), custom_call_target="tpu_custom_call" | custom-call | flops 1000 | bytes 1000 | tf_op jit(solution)/shard_map/last/pallas_call | solution.py:434
  (101 shorter events, 39.3 us)
Async XLA Ops:
  2.4 10.2 %collective-permute-start = (f32[96,768]{1,0:T(8,128)}, f32[96,768]{1,0:T(8,128)S(1)}, u32[]{:S(2)}, u32[]{:S(2)}) collective-permute-start(f32[96,768]{1,0:T(8,128)} %get-tuple-element.144), channel_id=1, source_target_pairs={{0,1},{1,0},{2,3},{3,2},{4,5},{5,4},{6,7},{7,6},{8,9},{9,8},{10,11... | collective-permute-start | bytes 884744 | tf_op jit(solution)/shard_map/ppermute | solution.py:457
  11.6 12.3 %collective-permute-start.1 = (f32[256,384]{1,0:T(8,128)}, f32[256,384]{1,0:T(8,128)S(1)}, u32[]{:S(2)}, u32[]{:S(2)}) collective-permute-start(f32[256,384]{1,0:T(8,128)} %get-tuple-element.155.refs_1_.refs_6_), channel_id=1, source_target_pairs={{0,1},{1,0},{2,3},{3,2},{4,5},{5,4},{6,7},{7,6},{8,9},{9,8},{10,11... | collective-permute-start | bytes 1179656 | tf_op jit(solution)/shard_map/ppermute | solution.py:457
  12.7 8.2 %collective-permute-start.3 = (f32[96,768]{1,0:T(8,128)S(1)}, f32[96,768]{1,0:T(8,128)S(1)}, u32[]{:S(2)}, u32[]{:S(2)}) collective-permute-start(f32[96,768]{1,0:T(8,128)S(1)} %collective-permute-done.refs_0_), channel_id=1, source_target_pairs={{0,4},{2,6},{4,0},{6,2},{8,12},{10,14},{12,8},{14,10},{16,20},{18,... | collective-permute-start | bytes 884744 | tf_op jit(solution)/shard_map/ppermute | solution.py:453
  14.4 16.4 %collective-permute-start.5 = (f32[256,384]{1,0:T(8,128)}, f32[256,384]{1,0:T(8,128)S(1)}, u32[]{:S(2)}, u32[]{:S(2)}) collective-permute-start(f32[256,384]{1,0:T(8,128)} %get-tuple-element.163.refs_1_.refs_7_), channel_id=1, source_target_pairs={{0,1},{1,0},{2,3},{3,2},{4,5},{5,4},{6,7},{7,6},{8,9},{9,8},{10,11... | collective-permute-start | bytes 1179656 | tf_op jit(solution)/shard_map/ppermute | solution.py:457
  36.0 4.1 %collective-permute-start.7 = (f32[192,1536]{1,0:T(8,128)S(1)}, f32[192,1536]{1,0:T(8,128)S(1)}, u32[]{:S(2)}, u32[]{:S(2)}) collective-permute-start(f32[192,1536]{1,0:T(8,128)S(1)} %get-tuple-element.178), channel_id=1, source_target_pairs={{0,2},{2,0},{4,6},{6,4},{8,10},{10,8},{12,14},{14,12},{16,18},{18,... | collective-permute-start | bytes 3538952 | tf_op jit(solution)/shard_map/ppermute | solution.py:453
  36.6 5.7 %collective-permute-start.8 = (f32[192,1536]{1,0:T(8,128)S(1)}, f32[192,1536]{1,0:T(8,128)S(1)}, u32[]{:S(2)}, u32[]{:S(2)}) collective-permute-start(f32[192,1536]{1,0:T(8,128)S(1)} %get-tuple-element.169), channel_id=1, source_target_pairs={{0,2},{2,0},{4,6},{6,4},{8,10},{10,8},{12,14},{14,12},{16,18},{18,... | collective-permute-start | bytes 3538952 | tf_op jit(solution)/shard_map/ppermute | solution.py:453
  36.7 8.8 %collective-permute-start.9 = (f32[192,1536]{1,0:T(8,128)S(1)}, f32[192,1536]{1,0:T(8,128)S(1)}, u32[]{:S(2)}, u32[]{:S(2)}) collective-permute-start(f32[192,1536]{1,0:T(8,128)S(1)} %get-tuple-element.174), channel_id=1, source_target_pairs={{0,2},{2,0},{4,6},{6,4},{8,10},{10,8},{12,14},{14,12},{16,18},{18,... | collective-permute-start | bytes 3538952 | tf_op jit(solution)/shard_map/ppermute | solution.py:453
  37.1 20.4 %collective-permute-start.10 = (f32[256,768]{1,0:T(8,128)S(1)}, f32[256,768]{1,0:T(8,128)S(1)}, u32[]{:S(2)}, u32[]{:S(2)}) collective-permute-start(f32[256,768]{1,0:T(8,128)S(1)} %get-tuple-element.184.refs_4_), channel_id=1, source_target_pairs={{0,1},{1,0},{2,3},{3,2},{4,5},{5,4},{6,7},{7,6},{8,9},{9,8},{10,11... | collective-permute-start | bytes 2359304 | tf_op jit(solution)/shard_map/ppermute | solution.py:457
  38.6 28.1 %collective-permute-start.11 = (f32[192,1536]{1,0:T(8,128)S(1)}, f32[192,1536]{1,0:T(8,128)S(1)}, u32[]{:S(2)}, u32[]{:S(2)}) collective-permute-start(f32[192,1536]{1,0:T(8,128)S(1)} %part.4.refs_1_), channel_id=1, source_target_pairs={{0,4},{2,6},{4,0},{6,2},{8,12},{10,14},{12,8},{14,10},{16,20},{18,... | collective-permute-start | bytes 3538952 | tf_op jit(solution)/shard_map/ppermute | solution.py:453
  40.6 27.8 %collective-permute-start.12 = (f32[192,1536]{1,0:T(8,128)S(1)}, f32[192,1536]{1,0:T(8,128)S(1)}, u32[]{:S(2)}, u32[]{:S(2)}) collective-permute-start(f32[192,1536]{1,0:T(8,128)S(1)} %part.5.refs_1_), channel_id=1, source_target_pairs={{0,8},{2,10},{4,12},{6,14},{8,0},{10,2},{12,4},{14,6},{16,24},{18,... | collective-permute-start | bytes 3538952 | tf_op jit(solution)/shard_map/ppermute | solution.py:453
  42.3 32.1 %collective-permute-start.13 = (f32[256,768]{1,0:T(8,128)S(1)}, f32[256,768]{1,0:T(8,128)S(1)}, u32[]{:S(2)}, u32[]{:S(2)}) collective-permute-start(f32[256,768]{1,0:T(8,128)S(1)} %get-tuple-element.198.refs_4_), channel_id=1, source_target_pairs={{0,1},{1,0},{2,3},{3,2},{4,5},{5,4},{6,7},{7,6},{8,9},{9,8},{10,11... | collective-permute-start | bytes 2359304 | tf_op jit(solution)/shard_map/ppermute | solution.py:457
  45.5 62.5 %collective-permute-start.21 = (f32[512,768]{1,0:T(8,128)S(1)}, f32[512,768]{1,0:T(8,128)S(1)}, u32[]{:S(2)}, u32[]{:S(2)}) collective-permute-start(f32[512,768]{1,0:T(8,128)S(1)} %mlp.1.refs_1_), channel_id=1, source_target_pairs={{0,1},{1,0},{2,3},{3,2},{4,5},{5,4},{6,7},{7,6},{8,9},{9,8},{10,11... | collective-permute-start | bytes 4718600 | tf_op jit(solution)/shard_map/ppermute | solution.py:457
  68.6 14.3 %collective-permute-start.15 = (f32[96,1536]{1,0:T(8,128)S(1)}, f32[96,1536]{1,0:T(8,128)S(1)}, u32[]{:S(2)}, u32[]{:S(2)}) collective-permute-start(f32[96,1536]{1,0:T(8,128)S(1)} %get-tuple-element.217.refs_3_), channel_id=1, source_target_pairs={{0,4},{2,6},{4,0},{6,2},{8,12},{10,14},{12,8},{14,10},{16,20},{18,... | collective-permute-start | bytes 1769480 | tf_op jit(solution)/shard_map/ppermute | solution.py:453
  70.1 14.3 %collective-permute-start.14 = (f32[96,1536]{1,0:T(8,128)S(1)}, f32[96,1536]{1,0:T(8,128)S(1)}, u32[]{:S(2)}, u32[]{:S(2)}) collective-permute-start(f32[96,1536]{1,0:T(8,128)S(1)} %get-tuple-element.216.refs_2_), channel_id=1, source_target_pairs={{0,8},{2,10},{4,12},{6,14},{8,0},{10,2},{12,4},{14,6},{16,24},{18,... | collective-permute-start | bytes 1769480 | tf_op jit(solution)/shard_map/ppermute | solution.py:453
  79.8 4.6 %collective-permute-start.17 = (f32[192,768]{1,0:T(8,128)S(1)}, f32[192,768]{1,0:T(8,128)S(1)}, u32[]{:S(2)}, u32[]{:S(2)}) collective-permute-start(f32[192,768]{1,0:T(8,128)S(1)} %get-tuple-element.220), channel_id=1, source_target_pairs={{0,2},{2,0},{4,6},{6,4},{8,10},{10,8},{12,14},{14,12},{16,18},{18,... | collective-permute-start | bytes 1769480 | tf_op jit(solution)/shard_map/ppermute | solution.py:453
  79.9 5.2 %collective-permute-start.16 = (f32[208,768]{1,0:T(8,128)S(1)}, f32[208,768]{1,0:T(8,128)S(1)}, u32[]{:S(2)}, u32[]{:S(2)}) collective-permute-start(f32[208,768]{1,0:T(8,128)S(1)} %get-tuple-element.207), channel_id=1, source_target_pairs={{0,2},{2,0},{4,6},{6,4},{8,10},{10,8},{12,14},{14,12},{16,18},{18,... | collective-permute-start | bytes 1916936 | tf_op jit(solution)/shard_map/ppermute | solution.py:453
  84.3 56.6 %collective-permute-start.28 = (f32[512,768]{1,0:T(8,128)S(1)}, f32[512,768]{1,0:T(8,128)S(1)}, u32[]{:S(2)}, u32[]{:S(2)}) collective-permute-start(f32[512,768]{1,0:T(8,128)S(1)} %get-tuple-element.243.own), channel_id=1, source_target_pairs={{0,1},{1,0},{2,3},{3,2},{4,5},{5,4},{6,7},{7,6},{8,9},{9,8},{10,11... | collective-permute-start | bytes 4718600 | tf_op jit(solution)/shard_map/ppermute | solution.py:457
  85.5 16.6 %collective-permute-start.20 = (f32[208,768]{1,0:T(8,128)S(1)}, f32[208,768]{1,0:T(8,128)S(1)}, u32[]{:S(2)}, u32[]{:S(2)}) collective-permute-start(f32[208,768]{1,0:T(8,128)S(1)} %get-tuple-element.226.refs_1_), channel_id=1, source_target_pairs={{0,4},{2,6},{4,0},{6,2},{8,12},{10,14},{12,8},{14,10},{16,20},{18,... | collective-permute-start | bytes 1916936 | tf_op jit(solution)/shard_map/ppermute | solution.py:453
  87.2 28.8 %collective-permute-start.22 = (f32[192,768]{1,0:T(8,128)S(1)}, f32[192,768]{1,0:T(8,128)S(1)}, u32[]{:S(2)}, u32[]{:S(2)}) collective-permute-start(f32[192,768]{1,0:T(8,128)S(1)} %get-tuple-element.231.refs_1_), channel_id=1, source_target_pairs={{0,8},{2,10},{4,12},{6,14},{8,0},{10,2},{12,4},{14,6},{16,24},{18,... | collective-permute-start | bytes 1769480 | tf_op jit(solution)/shard_map/ppermute | solution.py:453
  88.9 28.5 %collective-permute-start.23 = (f32[96,1536]{1,0:T(8,128)S(1)}, f32[96,1536]{1,0:T(8,128)S(1)}, u32[]{:S(2)}, u32[]{:S(2)}) collective-permute-start(f32[96,1536]{1,0:T(8,128)S(1)} %get-tuple-element.235), channel_id=1, source_target_pairs={{0,16},{2,18},{4,20},{6,22},{8,24},{10,26},{12,28},{14,30},{16,0},... | collective-permute-start | bytes 1769480 | tf_op jit(solution)/shard_map/ppermute | solution.py:453
  102.2 20.5 %collective-permute-start.24 = (f32[112,768]{1,0:T(8,128)S(1)}, f32[112,768]{1,0:T(8,128)S(1)}, u32[]{:S(2)}, u32[]{:S(2)}) collective-permute-start(f32[112,768]{1,0:T(8,128)S(1)} %get-tuple-element.238.refs_1_), channel_id=1, source_target_pairs={{0,8},{2,10},{4,12},{6,14},{8,0},{10,2},{12,4},{14,6},{16,24},{18,... | collective-permute-start | bytes 1032200 | tf_op jit(solution)/shard_map/ppermute | solution.py:453
  116.1 9.3 %collective-permute-start.25 = (f32[96,768]{1,0:T(8,128)S(1)}, f32[96,768]{1,0:T(8,128)S(1)}, u32[]{:S(2)}, u32[]{:S(2)}) collective-permute-start(f32[96,768]{1,0:T(8,128)S(1)} %get-tuple-element.241.refs_1_), channel_id=1, source_target_pairs={{0,4},{2,6},{4,0},{6,2},{8,12},{10,14},{12,8},{14,10},{16,20},{18,... | collective-permute-start | bytes 884744 | tf_op jit(solution)/shard_map/ppermute | solution.py:453
  122.7 15.6 %collective-permute-start.26 = (f32[64,768]{1,0:T(8,128)S(1)}, f32[64,768]{1,0:T(8,128)S(1)}, u32[]{:S(2)}, u32[]{:S(2)}) collective-permute-start(f32[64,768]{1,0:T(8,128)S(1)} %get-tuple-element.246.sent), channel_id=1, source_target_pairs={{0,16},{2,18},{4,20},{6,22},{8,24},{10,26},{12,28},{14,30},{16,0},... | collective-permute-start | bytes 589832 | tf_op jit(solution)/shard_map/ppermute | solution.py:453
  125.4 14.8 %collective-permute-start.27 = (f32[48,768]{1,0:T(8,128)S(1)}, f32[48,768]{1,0:T(8,128)S(1)}, u32[]{:S(2)}, u32[]{:S(2)}) collective-permute-start(f32[48,768]{1,0:T(8,128)S(1)} %get-tuple-element.251), channel_id=1, source_target_pairs={{0,16},{2,18},{4,20},{6,22},{8,24},{10,26},{12,28},{14,30},{16,0},... | collective-permute-start | bytes 442376 | tf_op jit(solution)/shard_map/ppermute | solution.py:453
  (21 other events, 137.4 us)

commit v9 on v8

--- a/solution.py
+++ b/solution.py
@@ -699,9 +699,9 @@
 
     down = Scatter(steps, count, orders[0], [(cot_a, active)])
     up = Scatter(steps, count, orders[1], [(a2_b, g_pre)])
-    (down_sent, down_kept), (up_sent, up_kept) = [one.far_parts() for one in (down, up)]
+    (up_sent, up_kept), (down_sent, down_kept) = [one.far_parts() for one in (up, down)]
+    up.near_sent(up_sent)
     down.near_sent(down_sent)
-    up.near_sent(up_sent)
     mlp_part = steps(mlp_kernel, "mlp", [((rows, width), HIGH)], [w_down] + active, tie=1)[0]
     mlp_other = swap(mlp_part)
     down.near_keep(down_kept)

time: 144 us -> 145 us (level)
    ppermute x22, waiting for transfers between devices: 43.3 us -> 46 us  [send(): return lax.ppermute(values, 'dp', [(i, i ^ 1 << bit) for i in range(count)])]
    ppermute x8, waiting for transfers between devices: 22.5 us -> 20.9 us  [swap(): return lax.ppermute(values, 'mp', [(0, 1), (1, 0)])]
  transfers between devices with their start and end apart: 30 -> 30, of which waited for: 17 -> 16; matrix products, arithmetic and copies ran while one was open for 0% -> 0% of each run, Pallas kernels for 26% -> 26%
where the time goes in v9:
time: 145 us; the launch traced here: 144 us
  waiting for transfers between devices  66.9 us (46%)
  Pallas kernels  44 us (30%)
  starting transfers between devices  29.5 us (20%)
  local copies, waits for them, and re-layouts  2.98 us (2%)
    ppermute x22, waiting for transfers between devices, send(): return lax.ppermute(values, 'dp', [(i, i ^ 1 << bit) for i in range(count)])  46 us
    pallas_call x35, Pallas kernels, __call__(): pl.pallas_call(kernel, name=name, out_shape=[jax.ShapeDtypeStruct(s, d) f...  44 us
    ppermute x8, waiting for transfers between devices, swap(): return lax.ppermute(values, 'mp', [(0, 1), (1, 0)])  20.9 us
    ppermute x22, starting transfers between devices, send(): return lax.ppermute(values, 'dp', [(i, i ^ 1 << bit) for i in range(count)])  20.5 us
    ppermute x8, starting transfers between devices, swap(): return lax.ppermute(values, 'mp', [(0, 1), (1, 0)])  9.04 us
    unnamed x30, local copies, waits for them, and re-layouts  2.98 us
  transfers between devices with their start and end apart: 30, of which 16 were waited for; matrix products, arithmetic and copies ran while one was open for 0% of the time, Pallas kernels for 26%

profile of v9, /device:TPU:0, one launch (start us, length us, event | category | flops | bytes accessed | tf_op | source)
XLA Modules:
  0.0 144.4 jit_solution(7396458983665424314)
XLA Ops:
  0.7 1.8 %load.1 = (f32[96,768]{1,0:T(8,128)}, f32[12,768]{1,0:T(8,128)}) custom-call(s32[1]{0:T(128)} %bitcast.here, bf16[384,768]{1,0:T(8,128)(2,1)} %refs_3_.5, s32[2,256]{1,0:T(2,128)} %crops.1, f32[768]{0:T(1024)} %refs_0_.6, f32[768]{0:T(1024)} %refs_1_.2, f32[384]{0:T(512)} %refs_2_.3, f32[384]{0:T(512)} %refs_3_.3, f32[768]{0:T(1024)} %refs_4_.2, ...), custom_call_target="tpu_custom_call" | custom-call | flops 1000 | bytes 1000 | tf_op jit(solution)/shard_map/load/pallas_call | solution.py:434
  2.4 3.0 %collective-permute-start = (f32[96,768]{1,0:T(8,128)}, f32[96,768]{1,0:T(8,128)S(1)}, u32[]{:S(2)}, u32[]{:S(2)}) collective-permute-start(f32[96,768]{1,0:T(8,128)} %get-tuple-element.144), channel_id=1, source_target_pairs={{0,1},{1,0},{2,3},{3,2},{4,5},{5,4},{6,7},{7,6},{8,9},{9,8},{10,11... | collective-permute-start | bytes 884744 | tf_op jit(solution)/shard_map/ppermute | solution.py:457
  5.4 6.1 %front.1 = (bf16[512,768]{1,0:T(8,128)(2,1)}, bf16[512,384]{1,0:T(8,128)(2,1)}, bf16[512,384]{1,0:T(8,128)(2,1)}, bf16[512,384]{1,0:T(8,128)(2,1)}, f32[512,128]...) custom-call(bf16[512,768]{1,0:T(8,128)(2,1)} %tokens.1, ...), custom_call_target="tpu_custom_call" | custom-call | flops 1000 | bytes 1000 | tf_op jit(solution)/shard_map/front/pallas_call | solution.py:434
  12.7 1.8 %collective-permute-start.3 = (f32[96,768]{1,0:T(8,128)S(1)}, f32[96,768]{1,0:T(8,128)S(1)}, u32[]{:S(2)}, u32[]{:S(2)}) collective-permute-start(f32[96,768]{1,0:T(8,128)S(1)} %collective-permute-done.refs_0_), channel_id=1, source_target_pairs={{0,4},{2,6},{4,0},{6,2},{8,12},{10,14},{12,8},{14,10},{16,20},{18,... | collective-permute-start | bytes 884744 | tf_op jit(solution)/shard_map/ppermute | solution.py:453
  17.1 3.7 %turn.1 = (bf16[512,768]{1,0:T(8,128)(2,1)S(1)}, bf16[768,1536]{1,0:T(8,128)(2,1)S(1)}, bf16[384,768]{1,0:T(8,128)(2,1)S(1)}, bf16[768,768]{1,0:T(8,128)(2,1)S(1...) custom-call(s32[1]{0:T(128)} %bitcast.here, ...), custom_call_target="tpu_custom_call" | custom-call | flops 1000 | bytes 1000 | tf_op jit(solution)/shard_map/turn/pallas_call | solution.py:434
  21.4 2.5 %collective-permute-done.1.values = f32[256,384]{1,0:T(8,128)S(1)} collective-permute-done((f32[256,384]{1,0:T(8,128)}, f32[256,384]{1,0:T(8,128)S(1)}, u32[]{:S(2)}, u32[]{:S(2)}) %collective-permute-start.1) | collective-permute-done | bytes 393248 | tf_op jit(solution)/shard_map/ppermute | solution.py:457
  25.9 3.5 %middle.2 = (f32[256,768]{1,0:T(8,128)S(1)}, bf16[768,256]{1,0:T(8,128)(2,1)S(1)}, bf16[256,1536]{1,0:T(8,128)(2,1)S(1)}, bf16[256,1536]{1,0:T(8,128)(2,1)S(1)},...) custom-call(bf16[512,768]{1,0:T(8,128)(2,1)S(1)} %copy-done.1, f32[256,384]{1,0:T(8,128)S(1)} %copy-done.2, ...), custom_call_target="tpu_custom_call" | custom-call | flops 1000 | bytes 1000 | tf_op jit(solution)/shard_map/middle/pallas_call | solution.py:434
  30.9 3.5 %middle.3 = (f32[256,768]{1,0:T(8,128)S(1)}, bf16[768,256]{1,0:T(8,128)(2,1)S(1)}, bf16[256,1536]{1,0:T(8,128)(2,1)S(1)}, bf16[256,1536]{1,0:T(8,128)(2,1)S(1)},...) custom-call(bf16[512,768]{1,0:T(8,128)(2,1)S(1)} %copy-done.1, f32[256,384]{1,0:T(8,128)S(1)} %copy-done.3, ...), custom_call_target="tpu_custom_call" | custom-call | flops 1000 | bytes 1000 | tf_op jit(solution)/shard_map/middle/pallas_call | solution.py:434
  48.2 9.3 %collective-permute-done.10.refs_5_ = f32[256,768]{1,0:T(8,128)S(1)} collective-permute-done((f32[256,768]{1,0:T(8,128)S(1)}, f32[256,768]{1,0:T(8,128)S(1)}, u32[]{:S(2)}, u32[]{:S(2)}) %collective-permute-start.10) | collective-permute-done | bytes 786464 | tf_op jit(solution)/shard_map/ppermute | solution.py:457
  57.6 4.9 %back.2 = (f32[256,768]{1,0:T(8,128)S(1)}, bf16[768,256]{1,0:T(8,128)(2,1)S(1)}, bf16[256,768]{1,0:T(8,128)(2,1)S(1)}, bf16[256,384]{1,0:T(8,128)(2,1)S(1)}, f32...) custom-call(bf16[512,768]{1,0:T(8,128)(2,1)S(1)} %copy-done.1, f32[12,768]{1,0:T(8,128)S(1)} %copy-done.8, ...), custom_call_target="tpu_custom_call" | custom-call | flops 6000001024 | bytes 1000 | tf_op jit(solution)/shard_map/back/pallas_call | solution.py:434
  62.4 5.9 %collective-permute-done.11.refs_2_ = f32[192,1536]{1,0:T(8,128)S(1)} collective-permute-done((f32[192,1536]{1,0:T(8,128)S(1)}, f32[192,1536]{1,0:T(8,128)S(1)}, u32[]{:S(2)}, u32[]{:S(2)}) %collective-permute-start.11) | collective-permute-done | bytes 1179680 | tf_op jit(solution)/shard_map/ppermute | solution.py:453
  71.9 2.5 %collective-permute-done.13.refs_5_ = f32[256,768]{1,0:T(8,128)S(1)} collective-permute-done((f32[256,768]{1,0:T(8,128)S(1)}, f32[256,768]{1,0:T(8,128)S(1)}, u32[]{:S(2)}, u32[]{:S(2)}) %collective-permute-start.13) | collective-permute-done | bytes 786464 | tf_op jit(solution)/shard_map/ppermute | solution.py:457
  74.4 4.9 %back.3 = (f32[256,768]{1,0:T(8,128)S(1)}, bf16[768,256]{1,0:T(8,128)(2,1)S(1)}, bf16[256,768]{1,0:T(8,128)(2,1)S(1)}, bf16[256,384]{1,0:T(8,128)(2,1)S(1)}, f32...) custom-call(bf16[512,768]{1,0:T(8,128)(2,1)S(1)} %copy-done.1, f32[12,768]{1,0:T(8,128)S(1)} %copy-done.8, ...), custom_call_target="tpu_custom_call" | custom-call | flops 1000 | bytes 1000 | tf_op jit(solution)/shard_map/back/pallas_call | solution.py:434
  80.9 3.1 %collective-permute-done.15.refs_5_ = f32[96,1536]{1,0:T(8,128)S(1)} collective-permute-done((f32[96,1536]{1,0:T(8,128)S(1)}, f32[96,1536]{1,0:T(8,128)S(1)}, u32[]{:S(2)}, u32[]{:S(2)}) %collective-permute-start.15) | collective-permute-done | bytes 589856 | tf_op jit(solution)/shard_map/ppermute | solution.py:453
  87.8 1.6 %collective-permute-start.22 = (f32[192,768]{1,0:T(8,128)S(1)}, f32[192,768]{1,0:T(8,128)S(1)}, u32[]{:S(2)}, u32[]{:S(2)}) collective-permute-start(f32[192,768]{1,0:T(8,128)S(1)} %get-tuple-element.231.refs_1_), channel_id=1, source_target_pairs={{0,8},{2,10},{4,12},{6,14},{8,0},{10,2},{12,4},{14,6},{16,24},{18,... | collective-permute-start | bytes 1769480 | tf_op jit(solution)/shard_map/ppermute | solution.py:453
  89.5 2.6 %collective-permute-start.23 = (f32[96,1536]{1,0:T(8,128)S(1)}, f32[96,1536]{1,0:T(8,128)S(1)}, u32[]{:S(2)}, u32[]{:S(2)}) collective-permute-start(f32[96,1536]{1,0:T(8,128)S(1)} %get-tuple-element.235), channel_id=1, source_target_pairs={{0,16},{2,18},{4,20},{6,22},{8,24},{10,26},{12,28},{14,30},{16,0},... | collective-permute-start | bytes 1769480 | tf_op jit(solution)/shard_map/ppermute | solution.py:453
  92.1 10.1 %collective-permute-done.20.refs_2_ = f32[208,768]{1,0:T(8,128)S(1)} collective-permute-done((f32[208,768]{1,0:T(8,128)S(1)}, f32[208,768]{1,0:T(8,128)S(1)}, u32[]{:S(2)}, u32[]{:S(2)}) %collective-permute-start.20) | collective-permute-done | bytes 639008 | tf_op jit(solution)/shard_map/ppermute | solution.py:453
  102.3 1.6 %collective-permute-start.24 = (f32[112,768]{1,0:T(8,128)S(1)}, f32[112,768]{1,0:T(8,128)S(1)}, u32[]{:S(2)}, u32[]{:S(2)}) collective-permute-start(f32[112,768]{1,0:T(8,128)S(1)} %get-tuple-element.238.refs_1_), channel_id=1, source_target_pairs={{0,8},{2,10},{4,12},{6,14},{8,0},{10,2},{12,4},{14,6},{16,24},{18,... | collective-permute-start | bytes 1032200 | tf_op jit(solution)/shard_map/ppermute | solution.py:453
  103.9 4.1 %collective-permute-done.21.refs_2_ = f32[512,768]{1,0:T(8,128)S(1)} collective-permute-done((f32[512,768]{1,0:T(8,128)S(1)}, f32[512,768]{1,0:T(8,128)S(1)}, u32[]{:S(2)}, u32[]{:S(2)}) %collective-permute-start.21) | collective-permute-done | bytes 1572896 | tf_op jit(solution)/shard_map/ppermute | solution.py:457
  109.2 7.5 %collective-permute-done.22.refs_2_ = f32[192,768]{1,0:T(8,128)S(1)} collective-permute-done((f32[192,768]{1,0:T(8,128)S(1)}, f32[192,768]{1,0:T(8,128)S(1)}, u32[]{:S(2)}, u32[]{:S(2)}) %collective-permute-start.22) | collective-permute-done | bytes 589856 | tf_op jit(solution)/shard_map/ppermute | solution.py:453
  118.4 4.7 %collective-permute-done.24.refs_2_ = f32[112,768]{1,0:T(8,128)S(1)} collective-permute-done((f32[112,768]{1,0:T(8,128)S(1)}, f32[112,768]{1,0:T(8,128)S(1)}, u32[]{:S(2)}, u32[]{:S(2)}) %collective-permute-start.24) | collective-permute-done | bytes 344096 | tf_op jit(solution)/shard_map/ppermute | solution.py:453
  123.2 2.7 %collective-permute-start.26 = (f32[64,768]{1,0:T(8,128)S(1)}, f32[64,768]{1,0:T(8,128)S(1)}, u32[]{:S(2)}, u32[]{:S(2)}) collective-permute-start(f32[64,768]{1,0:T(8,128)S(1)} %get-tuple-element.246.sent), channel_id=1, source_target_pairs={{0,16},{2,18},{4,20},{6,22},{8,24},{10,26},{12,28},{14,30},{16,0},... | collective-permute-start | bytes 589832 | tf_op jit(solution)/shard_map/ppermute | solution.py:453
  127.3 11.3 %collective-permute-done.26.got.refs_1_ = f32[64,768]{1,0:T(8,128)S(1)} collective-permute-done((f32[64,768]{1,0:T(8,128)S(1)}, f32[64,768]{1,0:T(8,128)S(1)}, u32[]{:S(2)}, u32[]{:S(2)}) %collective-permute-start.26) | collective-permute-done | bytes 196640 | tf_op jit(solution)/shard_map/ppermute | solution.py:453
  142.1 1.9 %last.1 = f32[512,768]{1,0:T(8,128)} custom-call(f32[12,768]{1,0:T(8,128)S(1)} %copy-done.8, f32[512,768]{1,0:T(8,128)S(1)} %get-tuple-element.253.base, f32[512,768]{1,0:T(8,128)S(1)} %get-tuple-element.254.unit, f32[512,1]{1,0:T(8,128)S(1)} %get-tuple-element.255.scale, f32[512,768]{1,0:T(8,128)S(1)} %collective-permute-done.28.other), custom_call_target="tpu_custom_call" | custom-call | flops 1000 | bytes 1000 | tf_op jit(solution)/shard_map/last/pallas_call | solution.py:434
  (101 shorter events, 38.7 us)
Async XLA Ops:
  2.4 10.2 %collective-permute-start = (f32[96,768]{1,0:T(8,128)}, f32[96,768]{1,0:T(8,128)S(1)}, u32[]{:S(2)}, u32[]{:S(2)}) collective-permute-start(f32[96,768]{1,0:T(8,128)} %get-tuple-element.144), channel_id=1, source_target_pairs={{0,1},{1,0},{2,3},{3,2},{4,5},{5,4},{6,7},{7,6},{8,9},{9,8},{10,11... | collective-permute-start | bytes 884744 | tf_op jit(solution)/shard_map/ppermute | solution.py:457
  11.6 12.3 %collective-permute-start.1 = (f32[256,384]{1,0:T(8,128)}, f32[256,384]{1,0:T(8,128)S(1)}, u32[]{:S(2)}, u32[]{:S(2)}) collective-permute-start(f32[256,384]{1,0:T(8,128)} %get-tuple-element.155.refs_1_.refs_6_), channel_id=1, source_target_pairs={{0,1},{1,0},{2,3},{3,2},{4,5},{5,4},{6,7},{7,6},{8,9},{9,8},{10,11... | collective-permute-start | bytes 1179656 | tf_op jit(solution)/shard_map/ppermute | solution.py:457
  12.7 8.2 %collective-permute-start.3 = (f32[96,768]{1,0:T(8,128)S(1)}, f32[96,768]{1,0:T(8,128)S(1)}, u32[]{:S(2)}, u32[]{:S(2)}) collective-permute-start(f32[96,768]{1,0:T(8,128)S(1)} %collective-permute-done.refs_0_), channel_id=1, source_target_pairs={{0,4},{2,6},{4,0},{6,2},{8,12},{10,14},{12,8},{14,10},{16,20},{18,... | collective-permute-start | bytes 884744 | tf_op jit(solution)/shard_map/ppermute | solution.py:453
  14.4 16.4 %collective-permute-start.5 = (f32[256,384]{1,0:T(8,128)}, f32[256,384]{1,0:T(8,128)S(1)}, u32[]{:S(2)}, u32[]{:S(2)}) collective-permute-start(f32[256,384]{1,0:T(8,128)} %get-tuple-element.163.refs_1_.refs_7_), channel_id=1, source_target_pairs={{0,1},{1,0},{2,3},{3,2},{4,5},{5,4},{6,7},{7,6},{8,9},{9,8},{10,11... | collective-permute-start | bytes 1179656 | tf_op jit(solution)/shard_map/ppermute | solution.py:457
  36.6 6.8 %collective-permute-start.8 = (f32[192,1536]{1,0:T(8,128)S(1)}, f32[192,1536]{1,0:T(8,128)S(1)}, u32[]{:S(2)}, u32[]{:S(2)}) collective-permute-start(f32[192,1536]{1,0:T(8,128)S(1)} %get-tuple-element.174), channel_id=1, source_target_pairs={{0,2},{2,0},{4,6},{6,4},{8,10},{10,8},{12,14},{14,12},{16,18},{18,... | collective-permute-start | bytes 3538952 | tf_op jit(solution)/shard_map/ppermute | solution.py:453
  36.7 9.5 %collective-permute-start.9 = (f32[192,1536]{1,0:T(8,128)S(1)}, f32[192,1536]{1,0:T(8,128)S(1)}, u32[]{:S(2)}, u32[]{:S(2)}) collective-permute-start(f32[192,1536]{1,0:T(8,128)S(1)} %get-tuple-element.170), channel_id=1, source_target_pairs={{0,2},{2,0},{4,6},{6,4},{8,10},{10,8},{12,14},{14,12},{16,18},{18,... | collective-permute-start | bytes 3538952 | tf_op jit(solution)/shard_map/ppermute | solution.py:453
  37.1 20.4 %collective-permute-start.10 = (f32[256,768]{1,0:T(8,128)S(1)}, f32[256,768]{1,0:T(8,128)S(1)}, u32[]{:S(2)}, u32[]{:S(2)}) collective-permute-start(f32[256,768]{1,0:T(8,128)S(1)} %get-tuple-element.184.refs_4_), channel_id=1, source_target_pairs={{0,1},{1,0},{2,3},{3,2},{4,5},{5,4},{6,7},{7,6},{8,9},{9,8},{10,11... | collective-permute-start | bytes 2359304 | tf_op jit(solution)/shard_map/ppermute | solution.py:457
  40.3 28.1 %collective-permute-start.11 = (f32[192,1536]{1,0:T(8,128)S(1)}, f32[192,1536]{1,0:T(8,128)S(1)}, u32[]{:S(2)}, u32[]{:S(2)}) collective-permute-start(f32[192,1536]{1,0:T(8,128)S(1)} %part.5.refs_1_), channel_id=1, source_target_pairs={{0,4},{2,6},{4,0},{6,2},{8,12},{10,14},{12,8},{14,10},{16,20},{18,... | collective-permute-start | bytes 3538952 | tf_op jit(solution)/shard_map/ppermute | solution.py:453
  41.8 27.7 %collective-permute-start.12 = (f32[192,1536]{1,0:T(8,128)S(1)}, f32[192,1536]{1,0:T(8,128)S(1)}, u32[]{:S(2)}, u32[]{:S(2)}) collective-permute-start(f32[192,1536]{1,0:T(8,128)S(1)} %part.4.refs_1_), channel_id=1, source_target_pairs={{0,8},{2,10},{4,12},{6,14},{8,0},{10,2},{12,4},{14,6},{16,24},{18,... | collective-permute-start | bytes 3538952 | tf_op jit(solution)/shard_map/ppermute | solution.py:453
  43.4 30.9 %collective-permute-start.13 = (f32[256,768]{1,0:T(8,128)S(1)}, f32[256,768]{1,0:T(8,128)S(1)}, u32[]{:S(2)}, u32[]{:S(2)}) collective-permute-start(f32[256,768]{1,0:T(8,128)S(1)} %get-tuple-element.198.refs_4_), channel_id=1, source_target_pairs={{0,1},{1,0},{2,3},{3,2},{4,5},{5,4},{6,7},{7,6},{8,9},{9,8},{10,11... | collective-permute-start | bytes 2359304 | tf_op jit(solution)/shard_map/ppermute | solution.py:457
  46.2 61.9 %collective-permute-start.21 = (f32[512,768]{1,0:T(8,128)S(1)}, f32[512,768]{1,0:T(8,128)S(1)}, u32[]{:S(2)}, u32[]{:S(2)}) collective-permute-start(f32[512,768]{1,0:T(8,128)S(1)} %mlp.1.refs_1_), channel_id=1, source_target_pairs={{0,1},{1,0},{2,3},{3,2},{4,5},{5,4},{6,7},{7,6},{8,9},{9,8},{10,11... | collective-permute-start | bytes 4718600 | tf_op jit(solution)/shard_map/ppermute | solution.py:457
  69.7 14.3 %collective-permute-start.15 = (f32[96,1536]{1,0:T(8,128)S(1)}, f32[96,1536]{1,0:T(8,128)S(1)}, u32[]{:S(2)}, u32[]{:S(2)}) collective-permute-start(f32[96,1536]{1,0:T(8,128)S(1)} %get-tuple-element.217.refs_3_), channel_id=1, source_target_pairs={{0,4},{2,6},{4,0},{6,2},{8,12},{10,14},{12,8},{14,10},{16,20},{18,... | collective-permute-start | bytes 1769480 | tf_op jit(solution)/shard_map/ppermute | solution.py:453
  70.3 14.2 %collective-permute-start.14 = (f32[96,1536]{1,0:T(8,128)S(1)}, f32[96,1536]{1,0:T(8,128)S(1)}, u32[]{:S(2)}, u32[]{:S(2)}) collective-permute-start(f32[96,1536]{1,0:T(8,128)S(1)} %get-tuple-element.216.refs_2_), channel_id=1, source_target_pairs={{0,8},{2,10},{4,12},{6,14},{8,0},{10,2},{12,4},{14,6},{16,24},{18,... | collective-permute-start | bytes 1769480 | tf_op jit(solution)/shard_map/ppermute | solution.py:453
  79.8 4.7 %collective-permute-start.17 = (f32[192,768]{1,0:T(8,128)S(1)}, f32[192,768]{1,0:T(8,128)S(1)}, u32[]{:S(2)}, u32[]{:S(2)}) collective-permute-start(f32[192,768]{1,0:T(8,128)S(1)} %get-tuple-element.220), channel_id=1, source_target_pairs={{0,2},{2,0},{4,6},{6,4},{8,10},{10,8},{12,14},{14,12},{16,18},{18,... | collective-permute-start | bytes 1769480 | tf_op jit(solution)/shard_map/ppermute | solution.py:453
  79.9 5.3 %collective-permute-start.16 = (f32[208,768]{1,0:T(8,128)S(1)}, f32[208,768]{1,0:T(8,128)S(1)}, u32[]{:S(2)}, u32[]{:S(2)}) collective-permute-start(f32[208,768]{1,0:T(8,128)S(1)} %get-tuple-element.207), channel_id=1, source_target_pairs={{0,2},{2,0},{4,6},{6,4},{8,10},{10,8},{12,14},{14,12},{16,18},{18,... | collective-permute-start | bytes 1916936 | tf_op jit(solution)/shard_map/ppermute | solution.py:453
  84.5 57.5 %collective-permute-start.28 = (f32[512,768]{1,0:T(8,128)S(1)}, f32[512,768]{1,0:T(8,128)S(1)}, u32[]{:S(2)}, u32[]{:S(2)}) collective-permute-start(f32[512,768]{1,0:T(8,128)S(1)} %get-tuple-element.243.own), channel_id=1, source_target_pairs={{0,1},{1,0},{2,3},{3,2},{4,5},{5,4},{6,7},{7,6},{8,9},{9,8},{10,11... | collective-permute-start | bytes 4718600 | tf_op jit(solution)/shard_map/ppermute | solution.py:457
  85.7 16.5 %collective-permute-start.20 = (f32[208,768]{1,0:T(8,128)S(1)}, f32[208,768]{1,0:T(8,128)S(1)}, u32[]{:S(2)}, u32[]{:S(2)}) collective-permute-start(f32[208,768]{1,0:T(8,128)S(1)} %get-tuple-element.226.refs_1_), channel_id=1, source_target_pairs={{0,4},{2,6},{4,0},{6,2},{8,12},{10,14},{12,8},{14,10},{16,20},{18,... | collective-permute-start | bytes 1916936 | tf_op jit(solution)/shard_map/ppermute | solution.py:453
  87.8 28.8 %collective-permute-start.22 = (f32[192,768]{1,0:T(8,128)S(1)}, f32[192,768]{1,0:T(8,128)S(1)}, u32[]{:S(2)}, u32[]{:S(2)}) collective-permute-start(f32[192,768]{1,0:T(8,128)S(1)} %get-tuple-element.231.refs_1_), channel_id=1, source_target_pairs={{0,8},{2,10},{4,12},{6,14},{8,0},{10,2},{12,4},{14,6},{16,24},{18,... | collective-permute-start | bytes 1769480 | tf_op jit(solution)/shard_map/ppermute | solution.py:453
  89.5 28.1 %collective-permute-start.23 = (f32[96,1536]{1,0:T(8,128)S(1)}, f32[96,1536]{1,0:T(8,128)S(1)}, u32[]{:S(2)}, u32[]{:S(2)}) collective-permute-start(f32[96,1536]{1,0:T(8,128)S(1)} %get-tuple-element.235), channel_id=1, source_target_pairs={{0,16},{2,18},{4,20},{6,22},{8,24},{10,26},{12,28},{14,30},{16,0},... | collective-permute-start | bytes 1769480 | tf_op jit(solution)/shard_map/ppermute | solution.py:453
  102.3 20.8 %collective-permute-start.24 = (f32[112,768]{1,0:T(8,128)S(1)}, f32[112,768]{1,0:T(8,128)S(1)}, u32[]{:S(2)}, u32[]{:S(2)}) collective-permute-start(f32[112,768]{1,0:T(8,128)S(1)} %get-tuple-element.238.refs_1_), channel_id=1, source_target_pairs={{0,8},{2,10},{4,12},{6,14},{8,0},{10,2},{12,4},{14,6},{16,24},{18,... | collective-permute-start | bytes 1032200 | tf_op jit(solution)/shard_map/ppermute | solution.py:453
  116.7 9.2 %collective-permute-start.25 = (f32[96,768]{1,0:T(8,128)S(1)}, f32[96,768]{1,0:T(8,128)S(1)}, u32[]{:S(2)}, u32[]{:S(2)}) collective-permute-start(f32[96,768]{1,0:T(8,128)S(1)} %get-tuple-element.241.refs_1_), channel_id=1, source_target_pairs={{0,4},{2,6},{4,0},{6,2},{8,12},{10,14},{12,8},{14,10},{16,20},{18,... | collective-permute-start | bytes 884744 | tf_op jit(solution)/shard_map/ppermute | solution.py:453
  123.2 15.5 %collective-permute-start.26 = (f32[64,768]{1,0:T(8,128)S(1)}, f32[64,768]{1,0:T(8,128)S(1)}, u32[]{:S(2)}, u32[]{:S(2)}) collective-permute-start(f32[64,768]{1,0:T(8,128)S(1)} %get-tuple-element.246.sent), channel_id=1, source_target_pairs={{0,16},{2,18},{4,20},{6,22},{8,24},{10,26},{12,28},{14,30},{16,0},... | collective-permute-start | bytes 589832 | tf_op jit(solution)/shard_map/ppermute | solution.py:453
  125.9 15.5 %collective-permute-start.27 = (f32[48,768]{1,0:T(8,128)S(1)}, f32[48,768]{1,0:T(8,128)S(1)}, u32[]{:S(2)}, u32[]{:S(2)}) collective-permute-start(f32[48,768]{1,0:T(8,128)S(1)} %get-tuple-element.251), channel_id=1, source_target_pairs={{0,16},{2,18},{4,20},{6,22},{8,24},{10,26},{12,28},{14,30},{16,0},... | collective-permute-start | bytes 442376 | tf_op jit(solution)/shard_map/ppermute | solution.py:453
  139.2 4.7 %collective-permute-start.29 = (f32[8,128]{1,0:T(8,128)S(1)}, f32[8,128]{1,0:T(8,128)S(1)}, u32[]{:S(2)}, u32[]{:S(2)}) collective-permute-start(f32[8,128]{1,0:T(8,128)S(1)} %get-tuple-element.261.own), channel_id=1, source_target_pairs={{0,1},{1,0},{2,3},{3,2},{4,5},{5,4},{6,7},{7,6},{8,9},{9,8},{10,11... | collective-permute-start | bytes 12296 | tf_op jit(solution)/shard_map/ppermute | solution.py:457
  (21 other events, 132.8 us)
